TPU v7x, 32 devices: a whole 2x2x4 slice. The times are simulated.
32 devices in a mesh: seq: 8 (over z, x), tp: 4 (over y, core).
Axes of the slice: x: 2, y: 2, z: 4, core: 2. Of those that a mesh axis runs over, the one named last changes fastest.
Arguments:
- packed_input: int32 [512, 5120], P('seq', 'tp'), may hold values from -2147483648 to 2147483646
- block_exponent: int32 [40, 4096], P('tp', 'seq'), may hold values from -5 to -1
- gate_input: bfloat16 [4096, 5120], P('seq', 'tp'), may hold values from -80 to 80
- state_write: bfloat16 [4096, 128], P('seq'), may hold values from -6 to 6
- state_read: bfloat16 [4096, 128], P('seq'), may hold values from -6 to 6
- log_decay: float32 [80, 4096], P('tp', 'seq'), may hold values from -1.6 to 0
- skip_weight: float32 [80], P('tp'), may hold values from 0.3 to 3
- norm_gain: float32 [5120], P('tp'), may hold values from 0.5 to 1.5
- out_weight: bfloat16 [5120, 2560], P('tp'), may hold values from -0.078125 to 0.078125
- out_cotangent: bfloat16 [4096, 2560], P('seq', 'tp'), may hold values from -6 to 6
Outputs:
- grad_input: bfloat16 [4096, 5120], P('seq', 'tp')
- grad_gate: bfloat16 [4096, 5120], P('seq', 'tp')
- grad_write: float32 [4096, 128], P('seq')
- grad_read: float32 [4096, 128], P('seq')
- grad_decay: float32 [80, 4096], P('tp', 'seq')
- grad_skip: float32 [80], P('tp')
- grad_gain: float32 [5120], P('tp')
- grad_out_weight: float32 [5120, 2560], P('tp', 'seq')
All inputs are finite; a program needn't handle non-finite values.
Results may differ from a plain program's by a relative error of at most 0.0049.
Values may be sent and summed in bfloat16 or wider, within the bound.
No kernel may reach another device: no remote copies, remote signals or barrier semaphores. Data moves between devices by JAX's collectives and lax.ppermute only.
A program may use at most 128 MiB of HBM per device.

v0:
```python
import jax
import jax.numpy as jnp
from jax import lax
from jax.sharding import PartitionSpec as P

PRECISE = lax.Precision.HIGHEST


def dequantize(packed_words, exponents):
    shifts = 4 * jnp.arange(8, dtype=jnp.int32)
    fields = (
        jnp.bitwise_and(jnp.right_shift(packed_words[:, None, :], shifts[None, :, None]), 15) - 8
    )
    fields = fields.reshape(packed_words.shape[0] * 8, packed_words.shape[1])
    factors = jnp.exp2(exponents.astype(jnp.float32))
    group_width = fields.shape[1] // exponents.shape[0]
    factors = jnp.repeat(factors.T, group_width, axis=1)
    return (fields.astype(jnp.float32) * factors).astype(jnp.bfloat16)


def lower_decays(seg_sum):
    length = seg_sum.shape[1]
    is_lower = (jnp.arange(length)[:, None] >= jnp.arange(length)[None, :])[None]
    spread = seg_sum[:, :, None] - seg_sum[:, None, :]
    return jnp.where(is_lower, jnp.exp(jnp.where(is_lower, spread, 0.0)), 0.0)


def on_device(
    packed_input,
    block_exponent,
    gate_input,
    state_write,
    state_read,
    log_decay,
    skip_weight,
    norm_gain,
    out_weight,
    out_cotangent,
):
    head_count, length = log_decay.shape
    x_values = dequantize(packed_input, block_exponent)
    width = x_values.shape[1]
    head_width = width // head_count
    x_heads = x_values.astype(jnp.float32).reshape(length, head_count, head_width)
    write_rows = state_write.astype(jnp.float32)
    read_rows = state_read.astype(jnp.float32)
    decay_sum = jnp.cumsum(log_decay, axis=1)
    decay_total = decay_sum[:, -1]
    to_end = jnp.exp(decay_total[:, None] - decay_sum)
    local_state = jnp.einsum(
        "lhp,ln->hpn", x_heads * to_end.T[:, :, None], write_rows, precision=PRECISE
    )
    totals = lax.all_gather(decay_total[None], "seq", axis=0, tiled=True)
    running = jnp.cumsum(totals, axis=0)
    position = lax.axis_index("seq")
    running_here = lax.dynamic_index_in_dim(running, position, 0, keepdims=False)
    before_here = running_here - decay_total
    shard_piece = lax.all_gather(local_state[None], "seq", axis=0, tiled=True)
    row_count = shard_piece.shape[0]
    sources = jnp.arange(row_count)
    running_part = running
    is_earlier = (sources < position)[:, None]
    weights = jnp.where(
        is_earlier, jnp.exp(jnp.where(is_earlier, before_here[None] - running_part, 0.0)), 0.0
    )
    state_in = jnp.einsum("kh,khpn->hpn", weights, shard_piece, precision=PRECISE)
    block_len = min(256, length)
    block_count = length // block_len
    saved = []
    core_parts = []
    state_now = state_in
    for block_index in range(block_count):
        first_row = block_index * block_len
        x_part = x_heads[first_row : first_row + block_len]
        write_part = write_rows[first_row : first_row + block_len]
        read_part = read_rows[first_row : first_row + block_len]
        seg_sum = jnp.cumsum(log_decay[:, first_row : first_row + block_len], axis=1)
        decay_matrix = lower_decays(seg_sum)
        cross = jnp.dot(read_part, write_part.T, precision=PRECISE)
        mixing = decay_matrix * cross[None]
        read_start = jnp.einsum("in,hpn->ihp", read_part, state_now, precision=PRECISE)
        core_parts.append(
            jnp.einsum("hij,jhp->ihp", mixing, x_part, precision=PRECISE)
            + jnp.exp(seg_sum).T[:, :, None] * read_start
        )
        saved.append((seg_sum, decay_matrix, cross, mixing, read_start, state_now))
        end_weight = jnp.exp(seg_sum[:, -1:] - seg_sum)
        state_now = jnp.exp(seg_sum[:, -1])[:, None, None] * state_now + jnp.einsum(
            "jhp,jn->hpn", x_part * end_weight.T[:, :, None], write_part, precision=PRECISE
        )
    core = jnp.concatenate(core_parts, axis=0)
    y_full = (core + skip_weight[None, :, None] * x_heads).reshape(length, width)
    gate = gate_input.astype(jnp.float32)
    sigma = jax.nn.sigmoid(gate)
    active = gate * sigma
    mixed = y_full * active
    total_width = width * lax.axis_size("tp")
    squares = lax.psum(jnp.sum(mixed * mixed, axis=1), "tp")
    scale_row = lax.rsqrt(squares / total_width + 1e-05)[:, None]
    normed = (mixed * scale_row * norm_gain).astype(jnp.bfloat16)
    shard_piece = lax.all_gather(out_cotangent, "tp", axis=1, tiled=True)
    project_grad_part = lax.dot_general(
        shard_piece, out_weight, (((1,), (1,)), ((), ())), preferred_element_type=jnp.float32
    )
    product = lax.dot_general(
        normed, shard_piece, (((0,), (0,)), ((), ())), preferred_element_type=jnp.float32
    )
    rounded = lax.optimization_barrier(product.astype(jnp.bfloat16))
    weight_part = rounded.astype(jnp.float32)
    grad_v, weight_part = (project_grad_part, weight_part)
    grad_out_weight = lax.psum_scatter(weight_part, "seq", scatter_dimension=1, tiled=True)
    scaled = grad_v * norm_gain
    gain_part = jnp.sum(grad_v * mixed * scale_row, axis=0)
    inner = lax.psum(jnp.sum(scaled * mixed, axis=1), "tp")[:, None]
    grad_mixed = (
        scale_row * scaled - mixed * (scale_row * scale_row * scale_row) * inner / total_width
    )
    grad_gate = (grad_mixed * y_full * sigma * (1.0 + gate * (1.0 - sigma))).astype(jnp.bfloat16)
    grad_y = (grad_mixed * active).reshape(length, head_count, head_width)
    skip_part = jnp.sum(grad_y * x_heads, axis=(0, 2))
    grad_gain, grad_skip = lax.psum((gain_part, skip_part), "seq")
    from_start = jnp.exp(decay_sum)
    local_cot = jnp.einsum(
        "lhp,ln->hpn", grad_y * from_start.T[:, :, None], read_rows, precision=PRECISE
    )
    shard_piece = lax.all_gather(local_cot[None], "seq", axis=0, tiled=True)
    row_count = shard_piece.shape[0]
    sources = jnp.arange(row_count)
    running_part = running
    is_later = (sources > position)[:, None]
    weights = jnp.where(
        is_later, jnp.exp(jnp.where(is_later, running_part - totals - running_here[None], 0.0)), 0.0
    )
    cot_in = jnp.einsum("kh,khpn->hpn", weights, shard_piece, precision=PRECISE)
    grad_x_parts = []
    grad_b_parts = []
    grad_c_parts = []
    grad_a_parts = []
    carry_cot = cot_in
    last_marker = (jnp.arange(block_len) == block_len - 1).astype(jnp.float32)[None, :]
    for block_index in reversed(range(block_count)):
        first_row = block_index * block_len
        x_part = x_heads[first_row : first_row + block_len]
        write_part = write_rows[first_row : first_row + block_len]
        read_part = read_rows[first_row : first_row + block_len]
        grad_part = grad_y[first_row : first_row + block_len]
        seg_sum, decay_matrix, cross, mixing, read_start, state_start = saved[block_index]
        end_weight = jnp.exp(seg_sum[:, -1:] - seg_sum)
        start_weight = jnp.exp(seg_sum)
        pair_dot = jnp.einsum("ihp,jhp->hij", grad_part, x_part, precision=PRECISE)
        weighted = pair_dot * decay_matrix
        summed = jnp.sum(weighted, axis=0)
        cot_write = jnp.einsum("jn,hpn->jhp", write_part, carry_cot, precision=PRECISE)
        grad_x_parts.append(
            skip_weight[None, :, None] * grad_part
            + jnp.einsum("hij,ihp->jhp", mixing, grad_part, precision=PRECISE)
            + end_weight.T[:, :, None] * cot_write
        )
        grad_b_parts.append(
            jnp.dot(summed.T, read_part, precision=PRECISE)
            + jnp.einsum(
                "jhp,hpn->jn", x_part * end_weight.T[:, :, None], carry_cot, precision=PRECISE
            )
        )
        scaled_grad = grad_part * start_weight.T[:, :, None]
        grad_c_parts.append(
            jnp.dot(summed, write_part, precision=PRECISE)
            + jnp.einsum("ihp,hpn->in", scaled_grad, state_start, precision=PRECISE)
        )
        pair_terms = weighted * cross[None]
        seg_grad = jnp.sum(pair_terms, axis=2) - jnp.sum(pair_terms, axis=1)
        seg_grad = seg_grad + jnp.sum(grad_part * read_start, axis=2).T * start_weight
        leaving = jnp.sum(x_part * cot_write, axis=2).T * end_weight
        seg_grad = seg_grad - leaving
        final_term = jnp.sum(leaving, axis=1) + jnp.exp(seg_sum[:, -1]) * jnp.sum(
            carry_cot * state_start, axis=(1, 2)
        )
        seg_grad = seg_grad + final_term[:, None] * last_marker
        grad_a_parts.append(jnp.flip(jnp.cumsum(jnp.flip(seg_grad, 1), axis=1), 1))
        carry_cot = jnp.exp(seg_sum[:, -1])[:, None, None] * carry_cot + jnp.einsum(
            "ihp,in->hpn", scaled_grad, read_part, precision=PRECISE
        )
    grad_input = (
        jnp.concatenate(grad_x_parts[::-1], axis=0).reshape(length, width).astype(jnp.bfloat16)
    )
    grad_write, grad_read = lax.psum(
        (jnp.concatenate(grad_b_parts[::-1], axis=0), jnp.concatenate(grad_c_parts[::-1], axis=0)),
        "tp",
    )
    grad_decay = jnp.concatenate(grad_a_parts[::-1], axis=1)
    return (
        grad_input,
        grad_gate,
        grad_write,
        grad_read,
        grad_decay,
        grad_skip,
        grad_gain,
        grad_out_weight,
    )


def solution(mesh):
    placed = (
        P("seq", "tp"),
        P("tp", "seq"),
        P("seq", "tp"),
        P("seq", None),
        P("seq", None),
        P("tp", "seq"),
        P("tp"),
        P("tp"),
        P("tp", None),
        P("seq", "tp"),
    )
    return jax.shard_map(
        on_device,
        mesh=mesh,
        in_specs=placed,
        out_specs=(
            P("seq", "tp"),
            P("seq", "tp"),
            P("seq", None),
            P("seq", None),
            P("tp", "seq"),
            P("tp"),
            P("tp"),
            P("tp", "seq"),
        ),
        check_vma=False,
    )
```

profile of v0, /device:TPU:0, one launch (start us, length us, event | category | flops | bytes accessed | tf_op | source)
XLA Modules:
  0.0 554.0 jit_solution(4991969997734249149)
XLA Ops:
  8.9 1.2 reduce-window.36
  10.6 1.1 shift_right_arithmetic.33
  11.8 3.7 shift_right_arithmetic.39
  15.5 4.5 copy.168
  20.8 2.6 fusion.35
  25.2 2.2 copy.162
  27.4 2.3 fusion.26
  29.8 1.7 fusion.175
  31.6 1.1 copy.169
  34.2 1.8 copy.173
  36.0 1.4 reshape.212
  37.4 1.3 copy.164
  38.7 1.9 reduce-window.34
  40.6 1.5 slice_reduce_fusion.4
  44.9 1.3 copy.195
  46.2 1.2 dynamic-slice
  48.7 1.3 dynamic-update-slice
  50.0 24.1 %all-reduce = f32[160]{0:T(256)S(1)} all-reduce(f32[160]{0:T(256)} %dynamic-update-slice), channel_id=2, replica_groups=mesh['seq'=8,'tp'=4] {'seq'}, use_global_device_ids=true, to_apply=%add | all-reduce | flops 160 | bytes 1280
  75.3 1.3 select_bitcast_fusion
  76.7 1.4 copy.187
  78.7 1.1 copy.163
  80.4 1.3 exponential_bitcast_fusion.3
  81.8 1.4 exponential_bitcast_fusion.4
  83.2 0.9 fusion.136
  84.1 0.9 fusion.140
  85.0 27.3 %all-gather.9.cloned.1.call-done = f32[160,64,128]{2,1,0:T(8,128)} async-done(((f32[20,64,128]{2,1,0:T(8,128)}), f32[160,64,128]{2,1,0:T(8,128)}) %all-gather.9.cloned.1.call-update) | async-done | bytes 5242896 | tf_op jit(solution)/shard_map/all_gather | solution.py:58
  112.3 10.1 %fusion.2 = f32[20,1,64,128]{3,1,2,0:T(1,128)S(1)} fusion(f32[8,20,1,1]{0,2,3,1:T(1,128)} %copy.187, f32[8,20,64,128]{3,2,1,0:T(8,128)} %bitcast.245), kind=kOutput, calls=%fused_computation.3 | convolution fusion | flops 15728640 | bytes 5898880 | tf_op jit(solution)/shard_map/kh,khpn->hpn/dot_general | solution.py:66
  123.2 0.8 copy-done.4
  124.9 5.5 fusion.76
  130.4 1.7 copy.175
  132.8 6.9 %fusion.79 = f32[256,20,64]{0,2,1:T(8,128)} fusion(bf16[256,20,64]{0,2,1:T(8,128)(2,1)} %bitcast.252, f32[256,256]{1,0:T(8,128)} %fusion.140, f32[20,256]{1,0:T(8,128)} %bitcast.263, pred[256,256]{1,0:T(8,128)(4,1)} %iota_compare_fusion, f32[256,20,64]{0,2,1:T(8,128)S(1)} %convolution_bitcast_fusion.3, f32[256,20]{0,1:T(8,128)} %get-tuple-element.85), kind=kOutput, calls=%fused_computation.80 | convolution fusion | flops 1012531200 | bytes 3645440 | tf_op jit(solution)/shard_map/hij,jhp->ihp/dot_general | solution.py:83
  139.8 2.8 copy.174
  142.6 4.9 multiply_reduce_fusion.7
  147.4 6.3 %psum.42 = f32[512]{0:T(512)} all-reduce(f32[512]{0:T(512)} %get-tuple-element.70), channel_id=1, replica_groups=mesh['seq'=8,'tp'=4] {'tp'}, use_global_device_ids=true, to_apply=%region_8.9 | all-reduce | flops 512 | bytes 4096 | tf_op jit(solution)/shard_map/psum | solution.py:98
  153.8 1.3 multiply_multiply_fusion
  155.1 10.1 %multiply_reduce_fusion.4 = (f32[1280]{0:T(1024)}, f32[512]{0:T(512)}, f32[512,1280]{1,0:T(8,128)}) fusion(f32[512,1280]{1,0:T(8,128)} %get-tuple-element.71, f32[512]{0:T(512)} %get-tuple-element.92, f32[1280]{0:T(1024)S(1)} %copy-done.54, bf16[512,2560]{1,0:T(8,128)(2,1)} %all-gather.7.cloned.1.call-done, bf16[1280,2560]{1,0:T(8,128)(2,1)} %param.18), kind=kOutput, calls=%fused_computation.36 | convolution fusion | flops 3359373568 | bytes 14432256 | tf_op jit(solution)/shard_map/dot_general | solution.py:102
  165.2 7.3 %psum.43 = f32[512]{0:T(512)} all-reduce(f32[512]{0:T(512)} %get-tuple-element.61), channel_id=1, replica_groups=mesh['seq'=8,'tp'=4] {'tp'}, use_global_device_ids=true, to_apply=%region_10.11 | all-reduce | flops 512 | bytes 4096 | tf_op jit(solution)/shard_map/psum | solution.py:114
  172.5 7.1 %multiply_reduce_fusion.5 = (f32[1280]{0:T(1024)}, f32[512,1280]{1,0:T(8,128)}, bf16[512,1280]{1,0:T(8,128)(2,1)}) fusion(bf16[512,1280]{1,0:T(8,128)(2,1)S(1)} %fusion.26, bf16[512,1280]{1,0:T(8,128)(2,1)} %param.12, f32[512]{0:T(512)} %psum.43, f32[512,1280]{1,0:T(8,128)} %get-tuple-element.71, f32[512]{0:T(512)} %get-tuple-element.91, ...), kind=kLoop, calls=%fused_computation.37 | loop fusion | flops 16382720 | bytes 14439424 | tf_op jit(solution)/shard_map/reduce_sum | solution.py:120
  179.5 3.2 copy.178
  182.8 4.1 fusion.27
  187.9 2.8 copy.180
  192.6 1.7 fusion.174
  194.2 1.7 copy.179
  196.0 1.7 copy.176
  197.7 3.4 fusion.111
  201.1 2.9 fusion.117
  204.1 5.6 %multiply_reduce_fusion = (f32[20,256]{1,0:T(8,128)}, f32[20,256]{1,0:T(8,128)}, f32[256,256]{1,0:T(8,128)S(1)}) fusion(f32[256,256]{1,0:T(8,128)S(1)} %copy-done.32, f32[20,256]{1,0:T(8,128)S(1)} %bitcast.257, pred[256,256]{1,0:T(8,128)(4,1)S(1)} %copy-done.44, f32[256,20,64]{0,2,1:T(8,128)S(1)} %bitcast.225, bf16[256,20,64]{0,2,1:T(8,128)(2,1)S(1)} %bitcast.251), kind=kOutput, calls=%fused_computation.15 | convolution fusion | flops 1017042944 | bytes 2617344 | tf_op jit(solution)/shard_map/ihp,jhp->hij/dot_general | solution.py:150
  210.8 5.6 %multiply_reduce_fusion.2 = (f32[20,256]{1,0:T(8,128)}, f32[20,256]{1,0:T(8,128)}, f32[256,256]{1,0:T(8,128)S(1)}) fusion(f32[256,256]{1,0:T(8,128)S(1)} %copy-done.29, f32[20,256]{1,0:T(8,128)S(1)} %bitcast.264, pred[256,256]{1,0:T(8,128)(4,1)S(1)} %copy-done.44, f32[256,20,64]{0,2,1:T(8,128)S(1)} %bitcast.240, bf16[256,20,64]{0,2,1:T(8,128)(2,1)S(1)} %bitcast.253), kind=kOutput, calls=%fused_computation.17 | convolution fusion | flops 1017042944 | bytes 2617344 | tf_op jit(solution)/shard_map/ihp,jhp->hij/dot_general | solution.py:150
  219.0 51.7 %all-gather.11.cloned.1.call-done = f32[160,64,128]{2,1,0:T(8,128)} async-done(((f32[20,64,128]{2,1,0:T(8,128)}), f32[160,64,128]{2,1,0:T(8,128)}) %all-gather.11.cloned.1.call-update) | async-done | bytes 5242896 | tf_op jit(solution)/shard_map/all_gather | solution.py:126
  270.7 10.1 %fusion = f32[20,1,64,128]{3,1,2,0:T(1,128)S(1)} fusion(f32[8,20,1,1]{0,2,3,1:T(1,128)S(1)} %copy-done.46, f32[8,20,64,128]{3,2,1,0:T(8,128)} %bitcast.246), kind=kOutput, calls=%fused_computation.1 | convolution fusion | flops 15728640 | bytes 5898880 | tf_op jit(solution)/shard_map/kh,khpn->hpn/dot_general | solution.py:134
  281.1 0.8 multiply_reduce_fusion.13
  282.2 1.8 multiply_reduce_fusion.10
  284.0 2.6 fusion.108
  286.7 1.8 multiply_reduce_fusion.8
  289.0 2.2 fusion.114
  292.8 8.9 %convolution_convert_fusion = bf16[1280,2560]{1,0:T(8,128)(2,1)} fusion(bf16[512,2560]{1,0:T(8,128)(2,1)} %all-gather.7.cloned.1.call-done, f32[512,1280]{1,0:T(8,128)} %get-tuple-element.71, f32[1280]{0:T(1024)S(1)} %copy-done.55, f32[512]{0:T(512)S(1)} %copy-done.56), kind=kOutput, calls=%fused_computation | convolution fusion | flops 3360686080 | bytes 11803648 | tf_op jit(solution)/shard_map/dot_general | solution.py:105
  301.8 10.5 %copy.193 = f32[1280,2560]{0,1:T(8,128)} copy(bf16[1280,2560]{1,0:T(8,128)(2,1)} %convolution_convert_fusion) | data formatting | bytes 19660800
  313.2 19.9 %all-reduce.1 = (f32[20]{0:T(128)}, f32[1280]{0:T(1024)}) all-reduce(f32[20]{0:T(128)S(1)} %reduce_sum.199, f32[1280]{0:T(1024)S(1)} %copy-done.57), channel_id=1, replica_groups=mesh['seq'=8,'tp'=4] {'seq'}, use_global_device_ids=true, to_apply=%region_33.34 | all-reduce | flops 1300 | bytes 10400 | tf_op jit(solution)/shard_map/psum | solution.py:121
  333.1 5.9 %fusion.85 = bf16[256,20,64]{0,2,1:T(8,128)(2,1)S(1)} fusion(f32[256,20,64]{0,2,1:T(8,128)S(1)} %bitcast.228, f32[256,256]{1,0:T(8,128)S(1)} %copy-done.33, f32[20,256]{1,0:T(8,128)S(1)} %bitcast.260, pred[256,256]{1,0:T(8,128)(4,1)S(1)} %copy-done.45, f32[256,20,64]{0,2,1:T(8,128)} %get-tuple-element.96, f32[256,20]{0,1:T(8,128)S(1)} %get-tuple-element.84, ...), kind=kOutput, calls=%fused_computation.82 | convolution fusion | flops 1013514240 | bytes 3645520 | tf_op jit(solution)/shard_map/hij,ihp->jhp/dot_general | solution.py:156
  339.1 4.8 fusion.82
  344.0 1.4 copy.185
  348.6 195.3 %reduce-scatter.4.cloned.1.call-done = f32[320,1280]{1,0:T(8,128)} async-done(((f32[2560,1280]{1,0:T(8,128)}), f32[320,1280]{1,0:T(8,128)}) %reduce-scatter.4.cloned.1.call-update) | async-done | bytes 1638416
  543.9 1.7 copy.209
  545.6 1.7 copy.210
  (233 shorter events, 27.8 us)
Async XLA Ops:
  7.2 105.2 %all-gather.9.cloned.1.call-start = ((), (), s32[]{:S(2)}) async-start(), calls=%async_computation.2 | async-start | bytes 5898240 | tf_op jit(solution)/shard_map/all_gather | solution.py:58
  10.6 38.0 %copy-start.58 = (f32[20]{0:T(128)}, f32[20]{0:T(128)S(1)}, u32[]{:S(2)}) copy-start(f32[20]{0:T(128)S(1)} %slice_reduce_fusion.5) | copy-start | bytes 244
  15.5 5.3 copy-start.11
  20.1 4.2 copy-start.39
  23.4 131.6 %all-gather.7.cloned.1.call-start = ((), (), s32[]{:S(2)}) async-start(), calls=%async_computation.1 | async-start | bytes 3276800 | tf_op jit(solution)/shard_map/all_gather | solution.py:101
  24.2 246.5 %all-gather.11.cloned.1.call-start = ((), (), s32[]{:S(2)}) async-start(), calls=%async_computation.3 | async-start | bytes 5898240 | tf_op jit(solution)/shard_map/all_gather | solution.py:126
  25.2 2.2 copy-start.13
  29.7 1.7 copy-start.61
  29.7 2.9 copy-start.42
  32.7 50.5 %copy-start.10 = (bf16[512,128]{1,0:T(8,128)(2,1)S(1)}, bf16[512,128]{1,0:T(8,128)(2,1)}, u32[]{:S(2)}) copy-start(bf16[512,128]{1,0:T(8,128)(2,1)} %param.14) | copy-start | bytes 393220
  36.0 86.5 %copy-start.1 = (f32[256,1280]{0,1:T(8,128)}, f32[256,1280]{0,1:T(8,128)S(1)}, u32[]{:S(2)}) copy-start(f32[256,1280]{0,1:T(8,128)S(1)} %copy.173) | copy-start | bytes 3932164
  112.3 10.1 %copy-start.36 = (f32[256,20]{0,1:T(8,128)S(1)}, f32[256,20]{0,1:T(8,128)}, u32[]{:S(2)}) copy-start(f32[256,20]{0,1:T(8,128)} %get-tuple-element.86) | copy-start | bytes 61444
  122.4 2.4 copy-start.18
  122.4 2.4 copy-start.21
  122.4 2.4 copy-start.31
  122.4 2.4 copy-start.34
  122.4 2.4 copy-start.43
  124.8 5.6 %copy-start.6 = (f32[256,20,64]{0,2,1:T(8,128)}, f32[256,20,64]{0,2,1:T(8,128)S(1)}, u32[]{:S(2)}) copy-start(f32[256,20,64]{0,2,1:T(8,128)S(1)} %convolution_bitcast_fusion.2) | copy-start | bytes 3932164
  132.8 6.9 %copy-start.8 = (f32[256,20,64]{0,2,1:T(8,128)}, f32[256,20,64]{0,2,1:T(8,128)S(1)}, u32[]{:S(2)}) copy-start(f32[256,20,64]{0,2,1:T(8,128)S(1)} %convolution_bitcast_fusion.3) | copy-start | bytes 3932164
  142.5 12.5 %copy-start.54 = (f32[1280]{0:T(1024)S(1)}, f32[1280]{0:T(1024)}, u32[]{:S(2)}) copy-start(f32[1280]{0:T(1024)} %param.17) | copy-start | bytes 15364
  182.8 7.9 %copy-start.52 = (f32[8,20,1,1]{1,0,2,3:T(8,128)S(1)}, f32[8,20,1,1]{1,0,2,3:T(8,128)}, u32[]{:S(2)}) copy-start(f32[8,20,1,1]{1,0,2,3:T(8,128)} %get-tuple-element.87) | copy-start | bytes 1924
  182.8 9.8 %copy-start = (f32[512,1280]{1,0:T(8,128)S(1)}, f32[512,1280]{1,0:T(8,128)}, u32[]{:S(2)}) copy-start(f32[512,1280]{1,0:T(8,128)} %get-tuple-element.69) | copy-start | bytes 7864324
  186.9 161.8 %all-reduce.5.cloned.1.call-start = ((), (), s32[]{:S(2)}) async-start(), calls=%async_computation.5 | async-start | bytes 1048576 | tf_op jit(solution)/shard_map/psum | solution.py:186
  197.7 6.4 %copy-start.19 = (bf16[256,1280]{0,1:T(8,128)(2,1)S(1)}, bf16[256,1280]{0,1:T(8,128)(2,1)}, u32[]{:S(2)}) copy-start(bf16[256,1280]{0,1:T(8,128)(2,1)} %copy.169) | copy-start | bytes 1966084
  197.7 6.4 %copy-start.22 = (f32[3,8,2,128]{3,1,2,0:T(8,128)S(1)}, f32[3,8,2,128]{3,1,2,0:T(8,128)}, u32[]{:S(2)}) copy-start(f32[3,8,2,128]{3,1,2,0:T(8,128)} %copy.199) | copy-start | bytes 73732
  197.7 6.4 %copy-start.32 = (f32[256,256]{1,0:T(8,128)S(1)}, f32[256,256]{1,0:T(8,128)}, u32[]{:S(2)}) copy-start(f32[256,256]{1,0:T(8,128)} %fusion.136) | copy-start | bytes 786436
  197.7 6.4 %copy-start.44 = (pred[256,256]{1,0:T(8,128)(4,1)S(1)}, pred[256,256]{1,0:T(8,128)(4,1)}, u32[]{:S(2)}) copy-start(pred[256,256]{1,0:T(8,128)(4,1)} %iota_compare_fusion) | copy-start | bytes 196612
  204.1 6.6 %copy-start.20 = (bf16[256,1280]{0,1:T(8,128)(2,1)S(1)}, bf16[256,1280]{0,1:T(8,128)(2,1)}, u32[]{:S(2)}) copy-start(bf16[256,1280]{0,1:T(8,128)(2,1)} %copy.163) | copy-start | bytes 1966084
  204.1 6.6 %copy-start.26 = (f32[3,8,2,128]{3,1,2,0:T(8,128)S(1)}, f32[3,8,2,128]{3,1,2,0:T(8,128)}, u32[]{:S(2)}) copy-start(f32[3,8,2,128]{3,1,2,0:T(8,128)} %copy-done.25) | copy-start | bytes 73732
  204.1 6.6 %copy-start.29 = (f32[256,256]{1,0:T(8,128)S(1)}, f32[256,256]{1,0:T(8,128)}, u32[]{:S(2)}) copy-start(f32[256,256]{1,0:T(8,128)} %fusion.140) | copy-start | bytes 786436
  210.8 6.6 %copy-start.7 = (f32[256,20,64]{0,2,1:T(8,128)S(1)}, f32[256,20,64]{0,2,1:T(8,128)}, u32[]{:S(2)}) copy-start(f32[256,20,64]{0,2,1:T(8,128)} %copy-done.6) | copy-start | bytes 3932164
  216.4 1.8 copy-start.16
  216.4 1.8 copy-start.9
  217.4 53.3 %copy-start.46 = (f32[8,20,1,1]{0,2,3,1:T(1,128)S(1)}, f32[8,20,1,1]{0,2,3,1:T(1,128)}, u32[]{:S(2)}) copy-start(f32[8,20,1,1]{0,2,3,1:T(1,128)} %copy.190) | copy-start | bytes 1924
  270.7 10.1 %copy-start.5 = (f32[20,64,128]{2,1,0:T(8,128)S(1)}, f32[20,64,128]{2,1,0:T(8,128)}, u32[]{:S(2)}) copy-start(f32[20,64,128]{2,1,0:T(8,128)} %copy-done.4) | copy-start | bytes 1966084
  270.7 10.4 %copy-start.35 = (f32[256,20]{0,1:T(8,128)S(1)}, f32[256,20]{0,1:T(8,128)}, u32[]{:S(2)}) copy-start(f32[256,20]{0,1:T(8,128)} %exponential_bitcast_fusion.3) | copy-start | bytes 61444
  270.7 10.4 %copy-start.60 = (f32[20]{0:T(128)S(1)}, f32[20]{0:T(128)}, u32[]{:S(2)}) copy-start(f32[20]{0:T(128)} %bitcast_exponential_fusion) | copy-start | bytes 244
  280.8 1.3 copy-start.2
  281.1 2.8 copy-start.37
  282.2 4.5 copy-start.3
  283.9 4.5 copy-start.27
  283.9 4.5 copy-start.53
  283.9 4.7 copy-start.23
  283.9 4.9 copy-start.40
  283.9 4.9 copy-start.41
  284.0 4.9 copy-start.48
  284.0 4.9 copy-start.49
  284.0 4.9 copy-start.50
  284.0 4.9 copy-start.51
  284.0 4.9 copy-start.59
  286.6 4.6 copy-start.15
  286.6 5.0 copy-start.17
  288.4 4.4 copy-start.55
  288.4 4.4 copy-start.56
  292.8 251.2 %reduce-scatter.4.cloned.1.call-start = ((), (), s32[]{:S(2)}) async-start(), calls=%async_computation.4 | async-start | bytes 14745600
  312.3 0.9 copy-start.57
  312.3 20.8 %copy-start.24 = (f32[3,8,2,128]{3,1,2,0:T(8,128)S(1)}, f32[3,8,2,128]{3,1,2,0:T(8,128)}, u32[]{:S(2)}) copy-start(f32[3,8,2,128]{3,1,2,0:T(8,128)} %copy.199) | copy-start | bytes 73732
  312.3 20.8 %copy-start.33 = (f32[256,256]{1,0:T(8,128)S(1)}, f32[256,256]{1,0:T(8,128)}, u32[]{:S(2)}) copy-start(f32[256,256]{1,0:T(8,128)} %fusion.136) | copy-start | bytes 786436
  312.3 20.8 %copy-start.45 = (pred[256,256]{1,0:T(8,128)(4,1)S(1)}, pred[256,256]{1,0:T(8,128)(4,1)}, u32[]{:S(2)}) copy-start(pred[256,256]{1,0:T(8,128)(4,1)} %iota_compare_fusion) | copy-start | bytes 196612
  312.3 20.8 %copy-start.62 = (f32[20]{0:T(128)S(1)}, f32[20]{0:T(128)}, u32[]{:S(2)}) copy-start(f32[20]{0:T(128)} %param.16) | copy-start | bytes 244
  333.1 6.0 %copy-start.12 = (f32[256,20,64]{0,2,1:T(8,128)S(1)}, f32[256,20,64]{0,2,1:T(8,128)}, u32[]{:S(2)}) copy-start(f32[256,20,64]{0,2,1:T(8,128)} %get-tuple-element.100) | copy-start | bytes 3932164
  333.1 6.0 %copy-start.28 = (f32[3,8,2,128]{3,1,2,0:T(8,128)S(1)}, f32[3,8,2,128]{3,1,2,0:T(8,128)}, u32[]{:S(2)}) copy-start(f32[3,8,2,128]{3,1,2,0:T(8,128)} %copy-done.25) | copy-start | bytes 73732
  333.1 6.0 %copy-start.30 = (f32[256,256]{1,0:T(8,128)S(1)}, f32[256,256]{1,0:T(8,128)}, u32[]{:S(2)}) copy-start(f32[256,256]{1,0:T(8,128)} %fusion.140) | copy-start | bytes 786436
  333.1 6.0 %copy-start.38 = (f32[256,20]{0,1:T(8,128)S(1)}, f32[256,20]{0,1:T(8,128)}, u32[]{:S(2)}) copy-start(f32[256,20]{0,1:T(8,128)} %get-tuple-element.86) | copy-start | bytes 61444
  (4 other events, 2.9 us)
Sparse Core Ops, SparseCore 0:
  23.6 88.7 all-gather.8
  113.9 23.7 all-gather.6
  187.0 83.6 all-gather.10
  292.9 31.6 all-reduce.4
  328.7 215.2 reduce-scatter.3
where the time goes:
time: 561 us; the launch traced here: 554 us
  waiting for transfers between devices  275 us (49%)
  matrix products  101 us (18%)
  local copies, waits for them, and re-layouts  70.7 us (13%)
  blocking collectives  57.6 us (10%)
  other arithmetic  33.5 us (6%)
  between operations  15.7 us (3%)
    unnamed x6, waiting for transfers between devices  196 us
    all_gather x1, waiting for transfers between devices, on_device(): shard_piece = lax.all_gather(local_cot[None], 'seq', axis=0, tiled=True)  51.7 us
    all_gather x1, waiting for transfers between devices, on_device(): shard_piece = lax.all_gather(local_state[None], 'seq', axis=0, tiled=True)  27.3 us
    unnamed x1, blocking collectives  24.1 us
    unnamed x145, local copies, waits for them, and re-layouts  23.7 us
    psum x1, blocking collectives, on_device(): grad_gain, grad_skip = lax.psum((gain_part, skip_part), 'seq')  19.9 us
    dot_general x2, matrix products, on_device(): jnp.einsum('hij,jhp->ihp', mixing, x_part, precision=PRECISE)  12.5 us
    dot_general x2, matrix products, on_device(): pair_dot = jnp.einsum('ihp,jhp->hij', grad_part, x_part, precision=PRECISE)  11.2 us
  transfers between devices with their start and end apart: 5, of which 3 were waited for; matrix products, arithmetic and copies ran while one was open for 25% of the time, Pallas kernels for 0%

commit v1 on v0

v1 whole, which is shorter than its diff:
```python
import functools
import jax
import jax.numpy as jnp
from jax import lax
from jax.experimental import pallas as pl
from jax.experimental.pallas import tpu as pltpu
from jax.sharding import PartitionSpec as P

F32 = jnp.float32
BF16 = jnp.bfloat16
LANES = 128
EXTRA = 16
EPSILON = 1e-05
NORMED_PARTS = 2


def mm(a, b):
    return jnp.dot(a, b, preferred_element_type=F32)


def mm_t(a, b):
    return lax.dot_general(a, b, (((1,), (1,)), ((), ())), preferred_element_type=F32)


def split2(v):
    high = v.astype(BF16)
    return high, (v - high.astype(F32)).astype(BF16)


def split3(v):
    high = v.astype(BF16)
    rest = v - high.astype(F32)
    middle = rest.astype(BF16)
    return high, middle, (rest - middle.astype(F32)).astype(BF16)


def iota(shape, axis):
    return lax.broadcasted_iota(jnp.int32, shape, axis)


def spread(values, spread2):
    return mm(jnp.concatenate(split2(values), axis=1), spread2)


def params(limit=48 << 20):
    return pltpu.CompilerParams(vmem_limit_bytes=limit)


def cost(flops, nbytes, special=0):
    return pl.CostEstimate(flops=int(flops), bytes_accessed=int(nbytes), transcendentals=int(special))


def prepare_kernel(
    heads, packed, expo_t, decay, skip, write, read,
    x_out, pay_out, seg_t_out, seg_out, spread_out, skip_out, read_t_out, pad, pad16,
):
    length, width = x_out.shape
    head_width = width // heads
    rows8 = packed.shape[0]
    pad[...] = jnp.zeros_like(pad)
    pad[0:heads, :] = decay[...]
    decay_t = pad[...].T
    lower = (iota((length, length), 0) >= iota((length, length), 1)).astype(BF16)
    seg_t = sum(mm(lower, part) for part in split3(decay_t))
    seg_t_out[...] = seg_t
    seg_out[...] = seg_t.T
    of_head = (iota((LANES, width), 1) // head_width == iota((LANES, width), 0)).astype(BF16)
    spread2 = jnp.concatenate([of_head, of_head], axis=0)
    spread_out[...] = spread2
    pad16[...] = jnp.zeros_like(pad16)
    pad16[0:heads, :] = jnp.broadcast_to(skip[...], (heads, LANES))
    skip_row = pad16[...].T[0:8, :]
    skip_out[...] = sum(mm(part, of_head) for part in split3(skip_row))
    total = seg_t[length - 1 : length, :]
    to_end = spread(jnp.exp(total - seg_t), spread2)
    groups = expo_t.shape[1]
    factor = jnp.left_shift(1, expo_t[...] + 8).astype(F32) * (2.0**-8)
    of_group = (
        iota((groups, width), 1) // (width // groups) == iota((groups, width), 0)
    ).astype(BF16)
    factors = mm(factor.astype(BF16), of_group)
    words = jnp.broadcast_to(packed[...][:, None, :], (rows8, 8, width))
    words = jnp.right_shift(words, 4 * iota((rows8, 8, width), 1))
    fields = (jnp.bitwise_and(words, 15) - 8).astype(F32).reshape(length, width)
    x = fields * factors
    x_out[...] = x.astype(BF16)
    states = mm(write[...].T, (x * to_end).astype(BF16))
    read_t_out[...] = read[...].T
    pay_out[0:LANES, :] = states.astype(BF16)
    total8 = jnp.broadcast_to(total, (8, LANES))
    high, middle, low = (mm(part, of_head) for part in split3(total8))
    row = iota((EXTRA, width), 0)
    tail = jnp.where(row == 0, high[0:1, :], jnp.where(row == 1, middle[0:1, :], low[0:1, :]))
    pay_out[LANES:, :] = jnp.where(row < 3, tail, 0.0).astype(BF16)


def prepare(packed, expo_t, decay, skip, write, read):
    heads, length = decay.shape
    width = packed.shape[1]
    shapes = (
        jax.ShapeDtypeStruct((length, width), BF16),
        jax.ShapeDtypeStruct((LANES + EXTRA, width), BF16),
        jax.ShapeDtypeStruct((length, LANES), F32),
        jax.ShapeDtypeStruct((LANES, length), F32),
        jax.ShapeDtypeStruct((2 * LANES, width), BF16),
        jax.ShapeDtypeStruct((8, width), F32),
        jax.ShapeDtypeStruct((LANES, length), BF16),
    )
    return pl.pallas_call(
        functools.partial(prepare_kernel, heads),
        name="prepare",
        out_shape=shapes,
        scratch_shapes=[pltpu.VMEM((LANES, length), F32), pltpu.VMEM((LANES, LANES), F32)],
        compiler_params=params(),
        cost_estimate=cost(3e9, 8e6),
    )(packed, expo_t, decay, skip, write, read)


def pair_columns(seg_t, seg, step):
    rolled = pltpu.roll(seg_t[...], lax.rem(LANES - 2 * step, LANES), 1)
    for side in (0, 1):
        yield side, rolled[:, side : side + 1], seg[pl.ds(2 * step + side, 1), :]


def inside_kernel(head_width, seg_t, seg, write, read, x, skip, out, cross):
    step = pl.program_id(0)
    length = x.shape[0]
    half = length // 2

    @pl.when(step == 0)
    def _():
        cross[...] = mm_t(read[...], write[...])

    diagonal = iota((half, half), 0) >= iota((half, half), 1)
    parts = []
    for side, column, row in pair_columns(seg_t, seg, step):
        rows = []
        for block in (0, 1):
            low = block * half
            square = slice(low, low + half)
            gap = column[square] - row[:, square]
            decayed = jnp.where(diagonal, jnp.exp(jnp.minimum(gap, 0.0)), 0.0)
            mixing = decayed * cross[square, square]
            if block == 1:
                left = jnp.exp(column[square] - row[:, 0:half]) * cross[square, 0:half]
                mixing = jnp.concatenate([left, mixing], axis=1)
            high, rest = split2(mixing)
            values = x[0 : low + half, :]
            rows.append(mm(high, values) + mm(rest, values))
        parts.append(jnp.concatenate(rows, axis=0))
    first = iota((length, LANES), 1) < head_width
    out[...] = jnp.where(first, parts[0], parts[1]) + skip[0:1, :] * x[...].astype(F32)


def whole(shape):
    return pl.BlockSpec(shape, lambda *_: (0,) * len(shape))


def inside(heads, seg_t, seg, write, read, x, skip):
    length, width = x.shape
    column = pl.BlockSpec((length, LANES), lambda j: (0, j))
    return pl.pallas_call(
        functools.partial(inside_kernel, width // heads),
        name="inside",
        grid=(width // LANES,),
        in_specs=[
            whole((length, LANES)), whole((LANES, length)), whole(write.shape), whole(read.shape),
            column, pl.BlockSpec((8, LANES), lambda j: (0, j)),
        ],
        out_specs=column,
        out_shape=jax.ShapeDtypeStruct((length, width), F32),
        scratch_shapes=[pltpu.VMEM((length, length), F32)],
        compiler_params=params(),
        cost_estimate=cost(20e9, 5e6),
    )(seg_t, seg, write, read, x, skip)


def gathered_total(pays, k):
    tail = pays[k][LANES : LANES + 8, :].astype(F32)
    return tail[0:1, :] + tail[1:2, :] + tail[2:3, :]


def boundary(totals, pays, sources, position, later, count):
    width = totals.shape[1]
    column = jnp.zeros((count, 1), jnp.int32)
    for k in range(count):
        column = jnp.where(iota((count, 1), 0) == k, sources[k], column)
    powers = jnp.zeros((count, width), F32)
    for j in range(count):
        if later:
            between = jnp.logical_and(column > sources[j], sources[j] > position)
        else:
            between = jnp.logical_and(column < sources[j], sources[j] < position)
        powers = powers + jnp.where(between, totals[j : j + 1, :], 0.0)
    wanted = column > position if later else column < position
    weights = jnp.where(wanted, jnp.exp(powers), 0.0)
    result = jnp.zeros((LANES, width), F32)
    for k in range(count):
        result = result + weights[k : k + 1, :] * pays[k][0:LANES, :].astype(F32)
    return result


def enter_kernel(
    count, sources, y_local, gate, grad_v, gain, read, seg_t, spread2, *rest,
):
    pays = rest[:count]
    y_out, scaled_t_out, stats_out, state_out, totals_out, state2 = rest[count:]
    width = y_out.shape[1]

    @pl.when(pl.program_id(0) == 0)
    def _():
        for k in range(count):
            totals_out[k : k + 1, :] = gathered_total(pays, k)
        state = boundary(totals_out[...], pays, sources, sources[count], False, count)
        state_out[...] = state
        state2[0:LANES, :], state2[LANES:, :] = split2(state)

    from_start = spread(jnp.exp(seg_t[...]), spread2[...])
    read_part = read[...]
    carried = mm(jnp.concatenate([read_part, read_part], axis=1), state2[...])
    y = y_local[...] + from_start * carried
    y_out[...] = y
    z = gate[...].astype(F32)
    mixed = y * z / (1.0 + jnp.exp(-z))
    with_gain = mixed * gain[...]
    scaled_t_out[...] = with_gain.T
    squares = jnp.sum(mixed * mixed, axis=1, keepdims=True)
    inner = jnp.sum(grad_v[...] * with_gain, axis=1, keepdims=True)
    lane = iota((squares.shape[0], LANES), 1)
    stats = jnp.where(lane == 0, squares, jnp.where(lane == 1, inner, 0.0))
    stats_out[...] = stats.T[0:8, :]


def enter(sources, y_local, gate, grad_v, gain, read, seg_t, spread2, pays):
    length, width = y_local.shape
    count = len(pays)
    block = LANES
    token = pl.BlockSpec((block, width), lambda i, *_: (i, 0))
    narrow = pl.BlockSpec((block, LANES), lambda i, *_: (i, 0))
    shapes = (
        jax.ShapeDtypeStruct((length, width), F32),
        jax.ShapeDtypeStruct((width, length), F32),
        jax.ShapeDtypeStruct((8, length), F32),
        jax.ShapeDtypeStruct((LANES, width), F32),
        jax.ShapeDtypeStruct((count, width), F32),
    )
    return pl.pallas_call(
        functools.partial(enter_kernel, count),
        name="enter",
        grid_spec=pltpu.PrefetchScalarGridSpec(
            num_scalar_prefetch=1,
            grid=(length // block,),
            in_specs=[
                token, token, token, whole((1, width)), narrow, narrow, whole(spread2.shape),
            ] + [whole(pays[0].shape)] * count,
            out_specs=[
                token,
                pl.BlockSpec((width, block), lambda i, *_: (0, i)),
                pl.BlockSpec((8, block), lambda i, *_: (0, i)),
                whole((LANES, width)),
                whole((count, width)),
            ],
            scratch_shapes=[pltpu.VMEM((2 * LANES, width), BF16)],
        ),
        out_shape=shapes,
        compiler_params=params(),
        cost_estimate=cost(3e9, 15e6),
    )(sources, y_local, gate, grad_v, gain, read, seg_t, spread2, *pays)


def gate_kernel(
    total_width, y_ref, gate, grad_v, gain, stats, x, seg_t, spread2, read_t,
    gate_out, grad_y_out, pay_out, columns, cot, sums,
):
    step = pl.program_id(0)
    row = iota((LANES, LANES), 0)
    squares, inner = stats[0:1, :], stats[1:2, :]
    scale_row = lax.rsqrt(squares * (1.0 / total_width) + EPSILON)
    back_row = scale_row * scale_row * scale_row * inner * (1.0 / total_width)
    columns[...] = jnp.where(row == 0, scale_row, jnp.where(row == 1, back_row, 0.0)).T
    scale, back = columns[:, 0:1], columns[:, 1:2]
    y = y_ref[...]
    z = gate[...].astype(F32)
    sigma = 1.0 / (1.0 + jnp.exp(-z))
    active = z * sigma
    mixed = y * active
    scaled_v = scale * grad_v[...]
    grad_mixed = scaled_v * gain[...] - mixed * back
    gate_out[...] = (grad_mixed * y * sigma * (1.0 + z * (1.0 - sigma))).astype(BF16)
    grad_y = grad_mixed * active
    grad_y_out[...] = grad_y
    gain_part = jnp.sum(scaled_v * mixed, axis=0, keepdims=True)
    skip_part = jnp.sum(grad_y * x[...].astype(F32), axis=0, keepdims=True)
    from_start = spread(jnp.exp(seg_t[...]), spread2[...])
    cot_part = mm(read_t[...], (grad_y * from_start).astype(BF16))
    wide = iota((8, grad_y.shape[1]), 0)
    sum_part = jnp.where(wide == 0, gain_part, jnp.where(wide == 1, skip_part, 0.0))

    @pl.when(step == 0)
    def _():
        cot[...] = cot_part
        sums[...] = sum_part

    @pl.when(step > 0)
    def _():
        cot[...] += cot_part
        sums[...] += sum_part

    @pl.when(step == pl.num_programs(0) - 1)
    def _():
        pay_out[0:LANES, :] = cot[...].astype(BF16)
        high, low = split2(sums[...])
        pay_out[LANES:, :] = jnp.concatenate([high, low], axis=0)


def gate_grads(total_width, y, gate, grad_v, gain, stats, x, seg_t, spread2, read_t):
    length, width = y.shape
    block = LANES
    token = pl.BlockSpec((block, width), lambda i: (i, 0))
    narrow = pl.BlockSpec((block, LANES), lambda i: (i, 0))
    shapes = (
        jax.ShapeDtypeStruct((length, width), BF16),
        jax.ShapeDtypeStruct((length, width), F32),
        jax.ShapeDtypeStruct((LANES + EXTRA, width), BF16),
    )
    return pl.pallas_call(
        functools.partial(gate_kernel, total_width),
        name="gate_grads",
        grid=(length // block,),
        in_specs=[
            token, token, token, whole((1, width)), pl.BlockSpec((8, block), lambda i: (0, i)),
            token, narrow, whole(spread2.shape), pl.BlockSpec((LANES, block), lambda i: (0, i)),
        ],
        out_specs=[token, token, whole((LANES + EXTRA, width))],
        out_shape=shapes,
        scratch_shapes=[
            pltpu.VMEM((LANES, LANES), F32), pltpu.VMEM((LANES, width), F32), pltpu.VMEM((8, width), F32),
        ],
        compiler_params=params(),
        cost_estimate=cost(3e9, 15e6),
    )(y, gate, grad_v, gain, stats, x, seg_t, spread2, read_t)


def inside_back_kernel(
    head_width, seg_t, seg, write, read, x, grad_y, out, grad_write, grad_read, cross, grad_cross,
):
    step = pl.program_id(0)
    length = x.shape[0]
    half = length // 2

    @pl.when(step == 0)
    def _():
        cross[...] = mm_t(write[...], read[...])
        grad_cross[...] = jnp.zeros_like(grad_cross)

    diagonal = iota((half, half), 0) <= iota((half, half), 1)
    first = iota((length, LANES), 1) < head_width
    grads = grad_y[...].astype(BF16)
    values = x[...]
    parts = []
    for side, column, row in pair_columns(seg_t, seg, step):
        mine = first if side == 0 else jnp.logical_not(first)
        own = jnp.where(mine, values, jnp.zeros_like(values))
        rows = []
        for block in (0, 1):
            low = block * half
            square = slice(low, low + half)
            gap = row[:, square] - column[square]
            decayed = jnp.where(diagonal, jnp.exp(jnp.minimum(gap, 0.0)), 0.0)
            mixing = decayed * cross[square, square]
            grad_cross[square, square] += mm_t(own[square], grads[square]) * decayed
            if block == 0:
                decayed = jnp.exp(row[:, half:] - column[square])
                mixing = jnp.concatenate([mixing, decayed * cross[square, half:]], axis=1)
                grad_cross[square, half:] += mm_t(own[square], grads[half:]) * decayed
            rows.append(mm(mixing.astype(BF16), grads[low:]))
        parts.append(jnp.concatenate(rows, axis=0))
    out[...] = jnp.where(first, parts[0], parts[1])

    @pl.when(step == pl.num_programs(0) - 1)
    def _():
        high, low = split2(grad_cross[...])
        grad_write[...] = mm(high, read[...]) + mm(low, read[...])
        turned = grad_cross[...].T
        high, low = split2(turned)
        grad_read[...] = mm(high, write[...]) + mm(low, write[...])


def inside_back(heads, seg_t, seg, write, read, x, grad_y):
    length, width = x.shape
    column = pl.BlockSpec((length, LANES), lambda j: (0, j))
    shapes = (
        jax.ShapeDtypeStruct((length, width), F32),
        jax.ShapeDtypeStruct((length, LANES), F32),
        jax.ShapeDtypeStruct((length, LANES), F32),
    )
    return pl.pallas_call(
        functools.partial(inside_back_kernel, width // heads),
        name="inside_back",
        grid=(width // LANES,),
        in_specs=[
            whole((length, LANES)), whole((LANES, length)), whole(write.shape), whole(read.shape),
            column, column,
        ],
        out_specs=[column, whole((length, LANES)), whole((length, LANES))],
        out_shape=shapes,
        scratch_shapes=[pltpu.VMEM((length, length), F32), pltpu.VMEM((length, length), F32)],
        compiler_params=params(),
        cost_estimate=cost(20e9, 8e6),
    )(seg_t, seg, write, read, x, grad_y)


def leave_kernel(
    count, heads, sources, y_ref, x_ref, grad_y_ref, inner_ref, write, seg_t, last, spread2,
    skip, state, totals, write_part, read_part, *rest,
):
    pays = rest[:count]
    (input_out, maps_out, decay_out, gain_out, skip_out, cot2, state16, from_head, per_head, sums) = rest[count:]
    step = pl.program_id(0)
    steps = pl.num_programs(0)
    block, width = y_ref.shape
    length = per_head.shape[0]

    @pl.when(step == 0)
    def _():
        cot = boundary(totals[...], pays, sources, sources[count], True, count)
        cot2[0:LANES, :], cot2[LANES:, :] = split2(cot)
        state16[...] = state[...].astype(BF16)
        from_head[...] = spread2[0:LANES, :].T
        ended = spread(jnp.exp(last[...]), spread2[...])
        through = jnp.sum(cot * state[...], axis=0, keepdims=True) * ended[0:1, :]
        sums[...] = jnp.where(iota((8, width), 0) == 0, through, 0.0)
        collected = jnp.zeros((8, width), F32)
        for k in range(count):
            tail = pays[k][LANES:, :].astype(F32)
            collected = collected + tail[0:8, :] + tail[8:16, :]
        gain_out[...] = collected
        skip_out[...] = sum(mm(part, from_head[...]) for part in split3(collected))

    seg_part = seg_t[...]
    decays = jnp.exp(seg_part)
    to_end = spread(jnp.exp(last[0:1, :] - seg_part), spread2[...])
    from_start = spread(decays, spread2[...])
    x = x_ref[...].astype(F32)
    grad_y = grad_y_ref[...]
    write_rows = write[...]
    from_later = to_end * mm(jnp.concatenate([write_rows, write_rows], axis=1), cot2[...])
    core_grad = inner_ref[...] + from_later
    skip_row = skip[0:1, :]
    input_out[...] = (skip_row * grad_y + core_grad).astype(BF16)
    leaving = jnp.sum(x * from_later, axis=0, keepdims=True)
    sums[...] += jnp.where(iota((8, width), 0) == 0, leaving, 0.0)
    terms = grad_y * (y_ref[...] - skip_row * x) - x * core_grad
    high, low = split2(terms)
    start = pl.multiple_of(step * block, block)
    per_head[pl.ds(start, block), :] = mm(high, from_head[...]) + mm(low, from_head[...])
    maps_out[:, 0:LANES] = write_part[...] + mm_t((x * to_end).astype(BF16), cot2[0:LANES, :])
    maps_out[:, LANES:] = read_part[...] + mm_t((grad_y * from_start).astype(BF16), state16[...])

    @pl.when(step == steps - 1)
    def _():
        final = sum(mm(part, from_head[...]) for part in split3(sums[...]))
        upper = (iota((length, length), 0) <= iota((length, length), 1)).astype(BF16)
        tail = sum(mm(upper, part) for part in split3(per_head[...]))
        decay_out[...] = (tail + final[0:1, :]).T[0:heads, :]


def leave(
    heads, sources, y, x, grad_y, inner, write, seg_t, spread2, skip, state, totals,
    write_part, read_part, pays,
):
    length, width = y.shape
    count = len(pays)
    block = LANES
    token = pl.BlockSpec((block, width), lambda i, *_: (i, 0))
    narrow = pl.BlockSpec((block, LANES), lambda i, *_: (i, 0))
    shapes = (
        jax.ShapeDtypeStruct((length, width), BF16),
        jax.ShapeDtypeStruct((length, 2 * LANES), F32),
        jax.ShapeDtypeStruct((heads, length), F32),
        jax.ShapeDtypeStruct((8, width), F32),
        jax.ShapeDtypeStruct((8, LANES), F32),
    )
    last = jnp.broadcast_to(seg_t[length - 1 :, :], (8, LANES))
    return pl.pallas_call(
        functools.partial(leave_kernel, count, heads),
        name="leave",
        grid_spec=pltpu.PrefetchScalarGridSpec(
            num_scalar_prefetch=1,
            grid=(length // block,),
            in_specs=[
                token, token, token, token, narrow, narrow, whole((8, LANES)),
                whole(spread2.shape), whole((8, width)), whole((LANES, width)),
                whole((count, width)), narrow, narrow,
            ] + [whole(pays[0].shape)] * count,
            out_specs=[
                token,
                pl.BlockSpec((block, 2 * LANES), lambda i, *_: (i, 0)),
                whole((heads, length)),
                whole((8, width)),
                whole((8, LANES)),
            ],
            scratch_shapes=[
                pltpu.VMEM((2 * LANES, width), BF16),
                pltpu.VMEM((LANES, width), BF16),
                pltpu.VMEM((width, LANES), BF16),
                pltpu.VMEM((length, LANES), F32),
                pltpu.VMEM((8, width), F32),
            ],
        ),
        out_shape=shapes,
        compiler_params=params(),
        cost_estimate=cost(5e9, 20e6),
    )(
        sources, y, x, grad_y, inner, write, seg_t, last, spread2, skip, state, totals,
        write_part, read_part, *pays,
    )


def product_kernel(final, index, mine, theirs, cot_mine, cot_theirs, out):
    first = mm(mine[...], cot_mine[0]).astype(BF16).astype(F32)
    second = mm(theirs[...], cot_theirs[0]).astype(BF16).astype(F32)
    out[...] = (first + second).astype(out.dtype)


def product(final, index, mine, theirs, cot_mine, cot_theirs):
    rows, length = mine.shape
    columns = cot_mine.shape[2]
    block = rows // 2 if (rows // 2) % 16 == 0 else rows
    side = pl.BlockSpec((block, length), lambda i, index: (i, 0))
    piece = pl.BlockSpec((1, length, columns), lambda i, index: (index[0], 0, 0))
    return pl.pallas_call(
        functools.partial(product_kernel, final),
        name="product",
        grid_spec=pltpu.PrefetchScalarGridSpec(
            num_scalar_prefetch=1,
            grid=(rows // block,),
            in_specs=[side, side, piece, piece],
            out_specs=pl.BlockSpec((block, columns), lambda i, index: (i, 0)),
        ),
        out_shape=jax.ShapeDtypeStruct((rows, columns), F32 if final else BF16),
        compiler_params=params(),
        cost_estimate=cost(4.0 * rows * length * columns, 2e6),
    )(index, mine, theirs, cot_mine, cot_theirs)


def ring_gather(value, size):
    half = size // 2
    order = [2 * q for q in range(half)] + [2 * (size - 1 - q) + 1 for q in range(half, size)]
    ahead = [(order[i], order[(i + 1) % size]) for i in range(size)]
    behind = [(b, a) for a, b in ahead]
    held = [(value, 0)]
    forward = backward = value
    for hop in range(1, half + 1):
        forward = lax.ppermute(forward, "seq", ahead)
        held.append((forward, -hop))
        if hop < half:
            backward = lax.ppermute(backward, "seq", behind)
            held.append((backward, hop))
    return [v for v, _ in held], [shift for _, shift in held]


def ring_sources(shifts, size):
    position = lax.axis_index("seq")
    half = size // 2
    place = jnp.where(position % 2 == 0, position // 2, size - 1 - position // 2)
    places = (place + jnp.array(shifts, jnp.int32) + size) % size
    found = jnp.where(places < half, 2 * places, 2 * (size - 1 - places) + 1)
    return jnp.concatenate([found, position[None]]).astype(jnp.int32)


def butterfly_sum(value, size):
    stride = 1
    while stride < size:
        value = value + lax.ppermute(value, "tp", [(i, i ^ stride) for i in range(size)])
        stride *= 2
    return value


def gather_columns(value, size):
    place = lax.axis_index("tp")
    stride = size // 2
    held = value
    while stride >= 1:
        other = lax.ppermute(held, "tp", [(i, i ^ stride) for i in range(size)])
        low = (place // stride) % 2 == 0
        held = jnp.stack([jnp.where(low, held, other), jnp.where(low, other, held)])
        stride //= 2
    levels = held.ndim - 2
    held = held.transpose((levels,) + tuple(range(levels - 1, -1, -1)) + (levels + 1,))
    return held.reshape(value.shape[0], size * value.shape[1])


def on_device(
    packed_input, block_exponent, gate_input, state_write, state_read, log_decay,
    skip_weight, norm_gain, out_weight, out_cotangent,
):
    heads, length = log_decay.shape
    width = packed_input.shape[1]
    seq_size = lax.axis_size("seq")
    tp_size = lax.axis_size("tp")
    total_width = width * tp_size
    model_width = out_weight.shape[1]
    columns = model_width // seq_size
    groups = seq_size // 2
    position = lax.axis_index("seq")
    parity = position % 2
    partner = [(i, i ^ 1) for i in range(seq_size)]

    per_shard = out_cotangent.shape[1] // (2 * columns)
    halves = out_cotangent.reshape(length, per_shard, 2, columns)
    other_half = jnp.where(parity == 0, halves[:, :, 1], halves[:, :, 0])
    shard_theirs = lax.ppermute(other_half, "seq", partner).reshape(length, per_shard * columns)
    cot_full = gather_columns(out_cotangent, tp_size)

    gain = norm_gain[None, :]
    x, pay, seg_t, seg, spread2, skip, read_t = prepare(
        packed_input, block_exponent.T, log_decay, skip_weight[:, None], state_write, state_read
    )
    pays, shifts = ring_gather(pay, seq_size)
    sources = ring_sources(shifts, seq_size)
    y_local = inside(heads, seg_t, seg, state_write, state_read, x, skip)
    grad_v = lax.dot_general(
        cot_full, out_weight, (((1,), (1,)), ((), ())), preferred_element_type=F32
    )
    cot_halves = cot_full.reshape(length, groups, 2, columns)
    cot_mine = jnp.where(parity == 0, cot_halves[:, :, 0], cot_halves[:, :, 1]).transpose(1, 0, 2)
    cot_theirs = (
        gather_columns(shard_theirs, tp_size).reshape(length, groups, columns).transpose(1, 0, 2)
    )

    y, scaled_t, stats, state, totals = enter(
        sources, y_local, gate_input, grad_v, gain, state_read, seg_t, spread2, pays
    )
    stats = butterfly_sum(stats, tp_size)
    scale = lax.rsqrt(stats[0:1, :] / total_width + EPSILON)
    part_rows = width // NORMED_PARTS
    normed, normed_theirs = [], []
    for part in range(NORMED_PARTS):
        rows = scaled_t[part * part_rows : (part + 1) * part_rows]
        normed.append((rows * scale).astype(BF16))
        normed_theirs.append(lax.ppermute(normed[part], "seq", partner))

    grad_gate, grad_y, pay_back = gate_grads(
        total_width, y, gate_input, grad_v, gain, stats, x, seg_t, spread2, read_t
    )
    pays_back, _ = ring_gather(pay_back, seq_size)
    inner, write_part, read_part = inside_back(heads, seg_t, seg, state_write, state_read, x, grad_y)

    group = position // 2
    weight_parts = []
    for part in range(NORMED_PARTS):
        received = []
        for shift in range(groups - 1, -1, -1):
            index = ((group + shift) % groups)[None].astype(jnp.int32)
            piece = product(
                shift == 0, index, normed[part], normed_theirs[part], cot_mine, cot_theirs
            )
            if shift > 0:
                moves = [(i, (i + 2 * shift) % seq_size) for i in range(seq_size)]
                piece = lax.ppermute(piece, "seq", moves)
            received.append(piece)
        weight_parts.append(sum(piece.astype(F32) for piece in received))
    grad_out_weight = jnp.concatenate(weight_parts, axis=0)

    grad_input, maps, grad_decay, gain_rows, skip_rows = leave(
        heads, sources, y, x, grad_y, inner, state_write, seg_t, spread2, skip, state, totals,
        write_part, read_part, pays_back,
    )
    maps = butterfly_sum(maps, tp_size)
    return (
        grad_input,
        grad_gate,
        maps[:, 0:LANES],
        maps[:, LANES:],
        grad_decay,
        skip_rows[1, 0:heads],
        gain_rows[0],
        grad_out_weight,
    )


def solution(mesh):
    placed = (
        P("seq", "tp"), P("tp", "seq"), P("seq", "tp"), P("seq", None), P("seq", None),
        P("tp", "seq"), P("tp"), P("tp"), P("tp", None), P("seq", "tp"),
    )
    return jax.shard_map(
        on_device,
        mesh=mesh,
        in_specs=placed,
        out_specs=(
            P("seq", "tp"), P("seq", "tp"), P("seq", None), P("seq", None), P("tp", "seq"),
            P("tp"), P("tp"), P("tp", "seq"),
        ),
        check_vma=False,
    )
```

time: 561 us -> 228 us (0.41); the launches traced: 554 us -> 227 us
  waiting for transfers between devices: 275 us -> 91.9 us
  matrix products: 101 us -> 5.18 us
  Pallas kernels: 0 us -> 58.2 us
  blocking collectives: 57.6 us -> 0 us
  local copies, waits for them, and re-layouts: 70.7 us -> 22.8 us
  starting transfers between devices: 0.37 us -> 32.3 us
  other arithmetic: 33.5 us -> 15.5 us
  between operations: 15.7 us -> 1.32 us
    unnamed x6 -> x0, waiting for transfers between devices: 196 us -> none
    dot_general x28 -> x1, matrix products: 101 us -> 5.18 us  [on_device(): lax.dot_general(cot_full, out_weight, (((1,), (1,)), ((), ())), preferred...]
    ppermute x0 -> x31, waiting for transfers between devices: none -> 91.9 us  [the longest x6 45.3 us: on_device(): piece = lax.ppermute(piece, 'seq', moves)]
    all_gather x3 -> x0, waiting for transfers between devices: 79 us -> none  [the longest x1 51.7 us: on_device(): shard_piece = lax.all_gather(local_cot[None], 'seq', axis=0, tiled=True)]
    pallas_call x0 -> x14, Pallas kernels: none -> 58.2 us  [the longest x1 11.2 us: inside_back(): pl.pallas_call(functools.partial(inside_back_kernel, width // heads), nam...]
    psum x3 -> x0, blocking collectives: 33.5 us -> none  [the longest x1 19.9 us: on_device(): grad_gain, grad_skip = lax.psum((gain_part, skip_part), 'seq')]
    ppermute x0 -> x31, starting transfers between devices: none -> 32.3 us  [the longest x6 10.5 us: on_device(): piece = lax.ppermute(piece, 'seq', moves)]
    unnamed x1 -> x0, blocking collectives: 24.1 us -> none
  transfers between devices with their start and end apart: 5 -> 31, of which waited for: 3 -> 13; matrix products, arithmetic and copies ran while one was open for 25% -> 14% of each run, Pallas kernels for 0% -> 22%
where the time goes in v1:
time: 228 us; the launch traced here: 227 us
  waiting for transfers between devices  91.9 us (40%)
  Pallas kernels  58.2 us (26%)
  starting transfers between devices  32.3 us (14%)
  local copies, waits for them, and re-layouts  22.8 us (10%)
  other arithmetic  15.5 us (7%)
  matrix products  5.18 us (2%)
    ppermute x6, waiting for transfers between devices, on_device(): piece = lax.ppermute(piece, 'seq', moves)  45.3 us
    unnamed x93, local copies, waits for them, and re-layouts  17.5 us
    ppermute x8, waiting for transfers between devices, ring_gather(): forward = lax.ppermute(forward, 'seq', ahead)  16.6 us
    ppermute x4, waiting for transfers between devices, butterfly_sum(): lax.ppermute(value, 'tp', [(i, i ^ stride) for i in range(size)])  11.3 us
    pallas_call x1, Pallas kernels, inside_back(): pl.pallas_call(functools.partial(inside_back_kernel, width // heads), nam...  11.2 us
    pallas_call x1, Pallas kernels, leave(): pl.pallas_call(functools.partial(leave_kernel, count, heads), name='leave...  10.8 us
    ppermute x6, starting transfers between devices, on_device(): piece = lax.ppermute(piece, 'seq', moves)  10.5 us
    ppermute x2, waiting for transfers between devices, on_device(): normed_theirs.append(lax.ppermute(normed[part], 'seq', partner))  10.2 us
  transfers between devices with their start and end apart: 31, of which 13 were waited for; matrix products, arithmetic and copies ran while one was open for 14% of the time, Pallas kernels for 22%

profile of v1, /device:TPU:0, one launch (start us, length us, event | category | flops | bytes accessed | tf_op | source)
XLA Modules:
  0.0 227.2 jit_solution(274416706853126339)
XLA Ops:
  0.7 2.2 copy.28
  2.9 3.0 %collective-permute-start = (bf16[512,640]{0,1:T(8,128)(2,1)}, bf16[512,640]{0,1:T(8,128)(2,1)}, u32[]{:S(2)}, u32[]{:S(2)}) collective-permute-start(bf16[512,640]{0,1:T(8,128)(2,1)} %copy.28), channel_id=1, source_target_pairs={{0,2},{1,3},{2,0},{3,1},{4,6},{5,7},{6,4},{7,5},{8,10},{9,11},{10,... | collective-permute-start | bytes 1966088 | tf_op jit(solution)/shard_map/ppermute | solution.py:585
  6.6 0.9 copy.25
  7.6 2.6 %prepare.1 = (bf16[512,1280]{1,0:T(8,128)(2,1)S(1)}, bf16[144,1280]{1,0:T(8,128)(2,1)S(1)}, f32[512,128]{1,0:T(8,128)S(1)}, f32[128,512]{1,0:T(8,128)S(1)}, bf16...) custom-call(s32[64,1280]{1,0:T(8,128)S(1)} %copy-done.1, s32[512,10]{1,0:T(8,128)S(1)} %bitcast.60, ...), custom_call_target="tpu_custom_call" | custom-call | flops 3000000000 | bytes 8000000 | tf_op jit(solution)/shard_map/prepare/pallas_call | solution.py:109
  10.2 0.9 copy-done.11
  11.1 1.1 copy-done.17
  12.2 1.6 collective-permute-start.2
  14.2 1.8 fusion
  16.0 1.5 collective-permute-start.21
  17.5 6.1 %collective-permute-done.2.rest_1_ = bf16[144,1280]{1,0:T(8,128)(2,1)S(1)} collective-permute-done((bf16[144,1280]{1,0:T(8,128)(2,1)S(1)}, bf16[144,1280]{1,0:T(8,128)(2,1)S(1)}, u32[]{:S(2)}, u32[]{:S(2)}) %collective-permute-start.2) | collective-permute-done | bytes 368672 | tf_op jit(solution)/shard_map/ppermute | solution.py:555
  23.8 1.4 select_bitcast_fusion.6
  25.2 1.2 pad_maximum_fusion.2
  27.5 9.9 %inside.1.y_local = f32[512,1280]{1,0:T(8,128)S(1)} custom-call(f32[512,128]{1,0:T(8,128)S(1)} %get-tuple-element.31.seg_t, f32[128,512]{1,0:T(8,128)S(1)} %get-tuple-element.32.seg, bf16[512,128]{1,0:T(8,128)(2,1)S(1)} %copy-done.4, bf16[512,128]{1,0:T(8,128)(2,1)S(1)} %copy-done.2, bf16[512,1280]{1,0:T(8,128)(2,1)S(1)} %copy-done.18, ...), custom_call_target="tpu_custom_call" | custom-call | flops 20000000000 | bytes 5000000 | tf_op jit(solution)/shard_map/inside/pallas_call | solution.py:162
  37.3 1.5 copy-done.10
  39.5 1.4 collective-permute-start.5
  41.6 6.7 %collective-permute-done.22 = bf16[512,320]{0,1:T(8,128)(2,1)S(1)} collective-permute-done((bf16[512,320]{0,1:T(8,128)(2,1)}, bf16[512,320]{0,1:T(8,128)(2,1)S(1)}, u32[]{:S(2)}, u32[]{:S(2)}) %collective-permute-start.22) | collective-permute-done | bytes 327712 | tf_op jit(solution)/shard_map/ppermute | solution.py:585
  48.2 1.1 select_bitcast_fusion.8
  49.3 0.9 pad_maximum_fusion.3
  50.2 1.9 collective-permute-start.7
  52.3 1.5 select_bitcast_fusion.2
  54.2 5.2 %fusion.6.grad_v = f32[512,1280]{1,0:T(8,128)} fusion(bf16[512,2560]{0,1:T(8,128)(2,1)S(1)} %bitcast.61, bf16[1280,2560]{1,0:T(8,128)(2,1)S(1)} %bitcast.66), kind=kOutput, calls=%fused_computation.34 | convolution fusion | flops 3355443200 | bytes 11796480 | tf_op jit(solution)/shard_map/dot_general | solution.py:623
  59.3 1.9 collective-permute-done.7.rest_6_
  61.2 1.6 collective-permute-done.8.rest_7_
  62.8 8.0 %enter.1 = (f32[512,1280]{1,0:T(8,128)}, f32[1280,512]{1,0:T(8,128)}, f32[8,512]{1,0:T(8,128)S(1)}, f32[128,1280]{1,0:T(8,128)S(1)}, f32[8,1280]{1,0:T(8,128)S(1)}) custom-call(s32[9]{0:T(128)S(1)} %pad_add_fusion.sources, f32[512,1280]{1,0:T(8,128)} %copy-done.10, bf16[512,1280]{1,0:T(8,128)(2,1)S(1)} %copy-done, f32[512,1280]{1,0:T(8,128)} %fusion.6.grad_v, ...), custom_call_target="tpu_custom_call" | custom-call | flops 3000000000 | bytes 15000000 | tf_op jit(solution)/shard_map/enter/pallas_call | solution.py:247
  70.8 0.8 copy-done.15
  72.4 1.1 collective-permute-done.9
  73.8 1.4 select_bitcast_fusion.4
  75.1 2.1 collective-permute-done.10
  77.2 7.3 %gate_grads.1 = (bf16[512,1280]{1,0:T(8,128)(2,1)}, f32[512,1280]{1,0:T(8,128)}, bf16[144,1280]{1,0:T(8,128)(2,1)}) custom-call(f32[512,1280]{1,0:T(8,128)} %get-tuple-element.37.y_ref, bf16[512,1280]{1,0:T(8,128)(2,1)S(1)} %copy-done, f32[512,1280]{1,0:T(8,128)} %fusion.6.grad_v, f32[1,1280]{1,0:T(1,128)S(1)} %broadcast_in_dim.34.gain, ...), custom_call_target="tpu_custom_call" | custom-call | flops 3000000000 | bytes 15000000 | tf_op jit(solution)/shard_map/gate_grads/pallas_call | solution.py:326
  85.0 0.9 copy.34
  85.8 1.8 collective-permute-start.12
  87.6 6.7 %collective-permute-done.11.rest_1_ = bf16[144,1280]{1,0:T(8,128)(2,1)} collective-permute-done((bf16[144,1280]{1,0:T(8,128)(2,1)}, bf16[144,1280]{1,0:T(8,128)(2,1)}, u32[]{:S(2)}, u32[]{:S(2)}) %collective-permute-start.11) | collective-permute-done | bytes 368672 | tf_op jit(solution)/shard_map/ppermute | solution.py:555
  94.7 2.2 multiply_convert_fusion.1
  96.9 1.8 collective-permute-start.20
  98.7 1.8 fusion.4
  100.5 2.5 %copy.37 = bf16[512,4,1,320]{3,0,1,2:T(8,128)(2,1)} copy(bf16[512,4,1,320]{0,3,2,1:T(8,128)(2,1)} %get-tuple-element.72) | data formatting | bytes 2621440
  103.0 2.5 %copy.36 = bf16[512,4,1,320]{3,0,1,2:T(8,128)(2,1)} copy(bf16[512,4,1,320]{0,3,2,1:T(8,128)(2,1)} %get-tuple-element.73) | data formatting | bytes 2621440
  106.2 1.4 collective-permute-start.15
  107.6 1.6 select_bitcast_fusion.cot_mine
  109.9 10.2 %collective-permute-done.20.theirs = bf16[640,512]{1,0:T(8,128)(2,1)S(1)} collective-permute-done((bf16[640,512]{1,0:T(8,128)(2,1)S(1)}, bf16[640,512]{1,0:T(8,128)(2,1)S(1)}, u32[]{:S(2)}, u32[]{:S(2)}) %collective-permute-start.20) | collective-permute-done | bytes 655392 | tf_op jit(solution)/shard_map/ppermute | solution.py:642
  120.1 1.1 product.8
  121.2 2.6 %collective-permute-start.24 = (bf16[640,320]{1,0:T(8,128)(2,1)S(1)}, bf16[640,320]{1,0:T(8,128)(2,1)}, u32[]{:S(2)}, u32[]{:S(2)}) collective-permute-start(bf16[640,320]{1,0:T(8,128)(2,1)S(1)} %product.8), channel_id=1, source_target_pairs={{0,24},{4,28},{8,0},{12,4},{16,8},{20,12},{24,16},{28,20},{1,25},{... | collective-permute-start | bytes 1228808 | tf_op jit(solution)/shard_map/ppermute | solution.py:661
  123.9 2.5 %collective-permute-start.16 = (bf16[144,1280]{1,0:T(8,128)(2,1)S(1)}, bf16[144,1280]{1,0:T(8,128)(2,1)}, u32[]{:S(2)}, u32[]{:S(2)}) collective-permute-start(bf16[144,1280]{1,0:T(8,128)(2,1)S(1)} %collective-permute-done.14.rest_4_), channel_id=1, source_target_pairs={{8,0},{16,8},{24,16},{28,24},{20,28},{12,20},{4,12},{0,4},{9,1},{1... | collective-permute-start | bytes 1105928 | tf_op jit(solution)/shard_map/ppermute | solution.py:558
  126.3 1.8 collective-permute-done.15.rest_5_
  128.2 11.2 %inside_back.1 = (f32[512,1280]{1,0:T(8,128)S(1)}, f32[512,128]{1,0:T(8,128)S(1)}, f32[512,128]{1,0:T(8,128)S(1)}) custom-call(f32[512,128]{1,0:T(8,128)S(1)} %copy-done.8, f32[128,512]{1,0:T(8,128)S(1)} %copy-done.29, bf16[512,128]{1,0:T(8,128)(2,1)S(1)} %copy-done.5, bf16[512,128]{1,0:T(8,128)(2,1)S(1)} %copy-done.3, bf16[512,1280]{1,0:T(8,128)(2,1)S(1)} %copy-done.20, ...), custom_call_target="tpu_custom_call" | custom-call | flops 20000000000 | bytes 8000000 | tf_op jit(solution)/shard_map/inside_back/pallas_call | solution.py:397
  139.3 1.5 copy-done.21
  140.9 1.0 product.9
  141.9 3.2 %collective-permute-start.25 = (bf16[640,320]{1,0:T(8,128)(2,1)S(1)}, bf16[640,320]{1,0:T(8,128)(2,1)}, u32[]{:S(2)}, u32[]{:S(2)}) collective-permute-start(bf16[640,320]{1,0:T(8,128)(2,1)S(1)} %product.9), channel_id=1, source_target_pairs={{0,16},{4,20},{8,24},{12,28},{16,0},{20,4},{24,8},{28,12},{1,17},{... | collective-permute-start | bytes 1228808 | tf_op jit(solution)/shard_map/ppermute | solution.py:661
  145.2 1.0 product.10
  146.2 2.5 %collective-permute-start.26 = (bf16[640,320]{1,0:T(8,128)(2,1)S(1)}, bf16[640,320]{1,0:T(8,128)(2,1)}, u32[]{:S(2)}, u32[]{:S(2)}) collective-permute-start(bf16[640,320]{1,0:T(8,128)(2,1)S(1)} %product.10), channel_id=1, source_target_pairs={{0,8},{4,12},{8,16},{12,20},{16,24},{20,28},{24,0},{28,4},{1,9},{5... | collective-permute-start | bytes 1228808 | tf_op jit(solution)/shard_map/ppermute | solution.py:661
  148.8 1.0 product.14
  149.8 1.1 product.13
  150.9 1.1 product.12
  152.0 1.1 product.11
  153.1 1.1 product.15
  154.2 1.4 collective-permute-start.28
  156.4 10.8 %leave.1 = (bf16[512,1280]{1,0:T(8,128)(2,1)}, f32[512,256]{1,0:T(8,128)S(1)}, f32[20,512]{1,0:T(8,128)}, f32[8,1280]{1,0:T(8,128)S(1)}, f32[8,128]{1,0:T(8,128)S(1)}) custom-call(s32[9]{0:T(128)S(1)} %pad_add_fusion.sources, f32[512,1280]{1,0:T(8,128)} %get-tuple-element.37.y_ref, bf16[512,1280]{1,0:T(8,128)(2,1)} %copy-done.17, ...), custom_call_target="tpu_custom_call" | custom-call | flops 5000000000 | bytes 20000000 | tf_op jit(solution)/shard_map/leave/pallas_call | solution.py:485
  167.2 27.9 %collective-permute-done.25 = bf16[640,320]{1,0:T(8,128)(2,1)} collective-permute-done((bf16[640,320]{1,0:T(8,128)(2,1)S(1)}, bf16[640,320]{1,0:T(8,128)(2,1)}, u32[]{:S(2)}, u32[]{:S(2)}) %collective-permute-start.25) | collective-permute-done | bytes 409632 | tf_op jit(solution)/shard_map/ppermute | solution.py:661
  195.1 1.6 add_add_fusion.1
  196.6 17.4 %collective-permute-done.29 = bf16[640,320]{1,0:T(8,128)(2,1)S(1)} collective-permute-done((bf16[640,320]{1,0:T(8,128)(2,1)S(1)}, bf16[640,320]{1,0:T(8,128)(2,1)S(1)}, u32[]{:S(2)}, u32[]{:S(2)}) %collective-permute-start.29) | collective-permute-done | bytes 409632 | tf_op jit(solution)/shard_map/ppermute | solution.py:661
  214.4 0.9 collective-permute-start.19
  215.4 1.7 copy.35
  218.2 8.1 %collective-permute-done.19 = f32[512,256]{1,0:T(8,128)S(1)} collective-permute-done((f32[512,256]{1,0:T(8,128)S(1)}, f32[512,256]{1,0:T(8,128)S(1)}, u32[]{:S(2)}, u32[]{:S(2)}) %collective-permute-start.19) | collective-permute-done | bytes 524320 | tf_op jit(solution)/shard_map/ppermute | solution.py:575
  226.4 0.8 fusion.5
  (137 shorter events, 9.8 us)
Async XLA Ops:
  0.6 6.9 %copy-start.2 = (bf16[512,128]{1,0:T(8,128)(2,1)S(1)}, bf16[512,128]{1,0:T(8,128)(2,1)}, u32[]{:S(2)}) copy-start(bf16[512,128]{1,0:T(8,128)(2,1)} %read.7) | copy-start | bytes 393220
  0.6 6.9 %copy-start.4 = (bf16[512,128]{1,0:T(8,128)(2,1)S(1)}, bf16[512,128]{1,0:T(8,128)(2,1)}, u32[]{:S(2)}) copy-start(bf16[512,128]{1,0:T(8,128)(2,1)} %write.7) | copy-start | bytes 393220
  0.7 6.9 %copy-start.6 = (f32[20,512]{1,0:T(8,128)S(1)}, f32[20,512]{1,0:T(8,128)}, u32[]{:S(2)}) copy-start(f32[20,512]{1,0:T(8,128)} %decay.1) | copy-start | bytes 122884
  0.7 6.9 %copy-start.1 = (s32[64,1280]{1,0:T(8,128)S(1)}, s32[64,1280]{1,0:T(8,128)}, u32[]{:S(2)}) copy-start(s32[64,1280]{1,0:T(8,128)} %packed.1) | copy-start | bytes 983044
  2.9 20.9 %collective-permute-start = (bf16[512,640]{0,1:T(8,128)(2,1)}, bf16[512,640]{0,1:T(8,128)(2,1)}, u32[]{:S(2)}, u32[]{:S(2)}) collective-permute-start(bf16[512,640]{0,1:T(8,128)(2,1)} %copy.28), channel_id=1, source_target_pairs={{0,2},{1,3},{2,0},{3,1},{4,6},{5,7},{6,4},{7,5},{8,10},{9,11},{10,... | collective-permute-start | bytes 1966088 | tf_op jit(solution)/shard_map/ppermute | solution.py:585
  12.2 14.5 %copy-start.28 = (f32[128,512]{1,0:T(8,128)}, f32[128,512]{1,0:T(8,128)S(1)}, u32[]{:S(2)}) copy-start(f32[128,512]{1,0:T(8,128)S(1)} %get-tuple-element.32.seg) | copy-start | bytes 786436
  12.2 14.5 %copy-start.30 = (f32[8,1280]{1,0:T(8,128)}, f32[8,1280]{1,0:T(8,128)S(1)}, u32[]{:S(2)}) copy-start(f32[8,1280]{1,0:T(8,128)S(1)} %get-tuple-element.34.skip) | copy-start | bytes 122884
  12.2 65.1 %copy-start.7 = (f32[512,128]{1,0:T(8,128)}, f32[512,128]{1,0:T(8,128)S(1)}, u32[]{:S(2)}) copy-start(f32[512,128]{1,0:T(8,128)S(1)} %get-tuple-element.31.seg_t) | copy-start | bytes 786436
  12.2 11.5 %collective-permute-start.2 = (bf16[144,1280]{1,0:T(8,128)(2,1)S(1)}, bf16[144,1280]{1,0:T(8,128)(2,1)S(1)}, u32[]{:S(2)}, u32[]{:S(2)}) collective-permute-start(bf16[144,1280]{1,0:T(8,128)(2,1)S(1)} %get-tuple-element.36.rest_0_), channel_id=1, source_target_pairs={{0,8},{8,16},{16,24},{24,28},{28,20},{20,12},{12,4},{4,0},{1,9},{9... | collective-permute-start | bytes 1105928 | tf_op jit(solution)/shard_map/ppermute | solution.py:555
  13.7 25.8 %collective-permute-start.3 = (bf16[144,1280]{1,0:T(8,128)(2,1)S(1)}, bf16[144,1280]{1,0:T(8,128)(2,1)S(1)}, u32[]{:S(2)}, u32[]{:S(2)}) collective-permute-start(bf16[144,1280]{1,0:T(8,128)(2,1)S(1)} %get-tuple-element.36.rest_0_), channel_id=1, source_target_pairs={{8,0},{16,8},{24,16},{28,24},{20,28},{12,20},{4,12},{0,4},{9,1},{1... | collective-permute-start | bytes 1105928 | tf_op jit(solution)/shard_map/ppermute | solution.py:558
  16.0 22.8 %collective-permute-start.21 = (bf16[512,1,320]{0,2,1:T(8,128)(2,1)}, bf16[512,1,320]{0,2,1:T(8,128)(2,1)}, u32[]{:S(2)}, u32[]{:S(2)}) collective-permute-start(bf16[512,1,320]{0,2,1:T(8,128)(2,1)} %fusion), channel_id=1, source_target_pairs={{0,4},{4,0},{8,12},{12,8},{16,20},{20,16},{24,28},{28,24},{1,5},{5... | collective-permute-start | bytes 983048 | tf_op jit(solution)/shard_map/ppermute | solution.py:613
  23.6 17.3 %collective-permute-start.4 = (bf16[144,1280]{1,0:T(8,128)(2,1)S(1)}, bf16[144,1280]{1,0:T(8,128)(2,1)S(1)}, u32[]{:S(2)}, u32[]{:S(2)}) collective-permute-start(bf16[144,1280]{1,0:T(8,128)(2,1)S(1)} %collective-permute-done.2.rest_1_), channel_id=1, source_target_pairs={{0,8},{8,16},{16,24},{24,28},{28,20},{20,12},{12,4},{4,0},{1,9},{9... | collective-permute-start | bytes 1105928 | tf_op jit(solution)/shard_map/ppermute | solution.py:555
  26.4 26.0 %collective-permute-start.1 = (bf16[2,512,640]{1,2,0:T(8,128)(2,1)}, bf16[2,512,640]{1,2,0:T(8,128)(2,1)}, u32[]{:S(2)}, u32[]{:S(2)}) collective-permute-start(bf16[2,512,640]{1,2,0:T(8,128)(2,1)} %pad_maximum_fusion.2), channel_id=1, source_target_pairs={{0,1},{1,0},{2,3},{3,2},{4,5},{5,4},{6,7},{7,6},{8,9},{9,8},{10,11... | collective-permute-start | bytes 3932168 | tf_op jit(solution)/shard_map/ppermute | solution.py:585
  27.4 11.4 %copy-start.40 = (f32[1280]{0:T(1024)S(1)}, f32[1280]{0:T(1024)}, u32[]{:S(2)}) copy-start(f32[1280]{0:T(1024)} %param.18) | copy-start | bytes 15364
  27.4 12.0 %copy-start.41 = (s32[8]{0:T(128)S(1)}, s32[8]{0:T(128)}, u32[]{:S(2)}) copy-start(s32[8]{0:T(128)} %constant.130.clone) | copy-start | bytes 100
  38.8 13.5 %copy-start.35 = (bf16[1,512,640]{1,2,0:T(8,128)(2,1)S(1)}, bf16[1,512,640]{1,2,0:T(8,128)(2,1)}, u32[]{:S(2)}) copy-start(bf16[1,512,640]{1,2,0:T(8,128)(2,1)} %copy-done.34) | copy-start | bytes 1966084
  38.8 13.5 %copy-start.37 = (bf16[1,512,640]{1,2,0:T(8,128)(2,1)S(1)}, bf16[1,512,640]{1,2,0:T(8,128)(2,1)}, u32[]{:S(2)}) copy-start(bf16[1,512,640]{1,2,0:T(8,128)(2,1)} %copy-done.36) | copy-start | bytes 1966084
  38.8 9.4 %collective-permute-start.22 = (bf16[512,320]{0,1:T(8,128)(2,1)}, bf16[512,320]{0,1:T(8,128)(2,1)S(1)}, u32[]{:S(2)}, u32[]{:S(2)}) collective-permute-start(bf16[512,320]{0,1:T(8,128)(2,1)} %bitcast.20), channel_id=1, source_target_pairs={{0,2},{1,3},{2,0},{3,1},{4,6},{5,7},{6,4},{7,5},{8,10},{9,11},{10,... | collective-permute-start | bytes 983048 | tf_op jit(solution)/shard_map/ppermute | solution.py:585
  39.5 10.7 %collective-permute-start.5 = (bf16[144,1280]{1,0:T(8,128)(2,1)S(1)}, bf16[144,1280]{1,0:T(8,128)(2,1)S(1)}, u32[]{:S(2)}, u32[]{:S(2)}) collective-permute-start(bf16[144,1280]{1,0:T(8,128)(2,1)S(1)} %collective-permute-done.3.rest_2_), channel_id=1, source_target_pairs={{8,0},{16,8},{24,16},{28,24},{20,28},{12,20},{4,12},{0,4},{9,1},{1... | collective-permute-start | bytes 1105928 | tf_op jit(solution)/shard_map/ppermute | solution.py:558
  40.9 11.2 %collective-permute-start.6 = (bf16[144,1280]{1,0:T(8,128)(2,1)S(1)}, bf16[144,1280]{1,0:T(8,128)(2,1)S(1)}, u32[]{:S(2)}, u32[]{:S(2)}) collective-permute-start(bf16[144,1280]{1,0:T(8,128)(2,1)S(1)} %collective-permute-done.4.rest_3_), channel_id=1, source_target_pairs={{0,8},{8,16},{16,24},{24,28},{28,20},{20,12},{12,4},{4,0},{1,9},{9... | collective-permute-start | bytes 1105928 | tf_op jit(solution)/shard_map/ppermute | solution.py:555
  49.3 4.5 %copy-start.38 = (bf16[1,512,320]{1,2,0:T(8,128)(2,1)}, bf16[1,512,320]{1,2,0:T(8,128)(2,1)S(1)}, u32[]{:S(2)}) copy-start(bf16[1,512,320]{1,2,0:T(8,128)(2,1)S(1)} %get-tuple-element.80) | copy-start | bytes 983044
  49.3 4.5 %copy-start.39 = (bf16[1,512,320]{1,2,0:T(8,128)(2,1)}, bf16[1,512,320]{1,2,0:T(8,128)(2,1)S(1)}, u32[]{:S(2)}) copy-start(bf16[1,512,320]{1,2,0:T(8,128)(2,1)S(1)} %get-tuple-element.81) | copy-start | bytes 983044
  49.3 4.8 %slice-start = ((s8[6553600]{0:T(1024)(128)(4,1)}), s8[4194304]{0:T(1024)(128)(4,1)S(1)}, s32[]{:S(2)}) async-start(s8[6553600]{0:T(1024)(128)(4,1)} %bitcast.65), calls=%async_computation | async-start | bytes 8388608
  50.2 3.9 %slice-start.1 = ((s8[6553600]{0:T(1024)(128)(4,1)}), s8[2359296]{0:T(1024)(128)(4,1)S(1)}, s32[]{:S(2)}) async-start(s8[6553600]{0:T(1024)(128)(4,1)} %bitcast.65), calls=%async_computation.1 | async-start | bytes 4718592
  50.2 23.5 %collective-permute-start.23 = (bf16[2,512,320]{1,2,0:T(8,128)(2,1)}, bf16[2,512,320]{1,2,0:T(8,128)(2,1)}, u32[]{:S(2)}, u32[]{:S(2)}) collective-permute-start(bf16[2,512,320]{1,2,0:T(8,128)(2,1)} %pad_maximum_fusion.3), channel_id=1, source_target_pairs={{0,1},{1,0},{2,3},{3,2},{4,5},{5,4},{6,7},{7,6},{8,9},{9,8},{10,11... | collective-permute-start | bytes 1966088 | tf_op jit(solution)/shard_map/ppermute | solution.py:585
  50.2 11.0 %collective-permute-start.7 = (bf16[144,1280]{1,0:T(8,128)(2,1)S(1)}, bf16[144,1280]{1,0:T(8,128)(2,1)S(1)}, u32[]{:S(2)}, u32[]{:S(2)}) collective-permute-start(bf16[144,1280]{1,0:T(8,128)(2,1)S(1)} %collective-permute-done.5.rest_4_), channel_id=1, source_target_pairs={{8,0},{16,8},{24,16},{28,24},{20,28},{12,20},{4,12},{0,4},{9,1},{1... | collective-permute-start | bytes 1105928 | tf_op jit(solution)/shard_map/ppermute | solution.py:558
  52.2 10.7 %collective-permute-start.8 = (bf16[144,1280]{1,0:T(8,128)(2,1)S(1)}, bf16[144,1280]{1,0:T(8,128)(2,1)S(1)}, u32[]{:S(2)}, u32[]{:S(2)}) collective-permute-start(bf16[144,1280]{1,0:T(8,128)(2,1)S(1)} %collective-permute-done.6.rest_5_), channel_id=1, source_target_pairs={{0,8},{8,16},{16,24},{24,28},{28,20},{20,12},{12,4},{4,0},{1,9},{9... | collective-permute-start | bytes 1105928 | tf_op jit(solution)/shard_map/ppermute | solution.py:555
  54.1 5.2 %copy-start.32 = (bf16[2,2,512,640]{2,3,0,1:T(8,128)(2,1)}, bf16[2,2,512,640]{2,3,0,1:T(8,128)(2,1)S(1)}, u32[]{:S(2)}) copy-start(bf16[2,2,512,640]{2,3,0,1:T(8,128)(2,1)S(1)} %pad_maximum_fusion) | copy-start | bytes 7864324
  54.1 8.7 %copy-start = (bf16[512,1280]{1,0:T(8,128)(2,1)S(1)}, bf16[512,1280]{1,0:T(8,128)(2,1)}, u32[]{:S(2)}) copy-start(bf16[512,1280]{1,0:T(8,128)(2,1)} %gate.3) | copy-start | bytes 3932164
  54.1 8.7 %copy-start.12 = (bf16[256,1280]{1,0:T(8,128)(2,1)S(1)}, bf16[256,1280]{1,0:T(8,128)(2,1)}, u32[]{:S(2)}) copy-start(bf16[256,1280]{1,0:T(8,128)(2,1)} %copy-done.11) | copy-start | bytes 1966084
  72.3 4.9 %copy-start.13 = (bf16[256,1280]{1,0:T(8,128)(2,1)S(1)}, bf16[256,1280]{1,0:T(8,128)(2,1)}, u32[]{:S(2)}) copy-start(bf16[256,1280]{1,0:T(8,128)(2,1)} %copy-done.11) | copy-start | bytes 1966084
  72.3 1.2 collective-permute-start.9
  72.4 4.9 %copy-start.19 = (bf16[512,1280]{1,0:T(8,128)(2,1)S(1)}, bf16[512,1280]{1,0:T(8,128)(2,1)}, u32[]{:S(2)}) copy-start(bf16[512,1280]{1,0:T(8,128)(2,1)} %copy-done.17) | copy-start | bytes 3932164
  73.5 3.7 %collective-permute-start.10 = (f32[8,512]{1,0:T(8,128)S(1)}, f32[8,512]{1,0:T(8,128)S(1)}, u32[]{:S(2)}, u32[]{:S(2)}) collective-permute-start(f32[8,512]{1,0:T(8,128)S(1)} %add.106), channel_id=1, source_target_pairs={{0,2},{1,3},{2,0},{3,1},{4,6},{5,7},{6,4},{7,5},{8,10},{9,11},{10,... | collective-permute-start | bytes 49160 | tf_op jit(solution)/shard_map/ppermute | solution.py:575
  84.5 9.9 %collective-permute-start.11 = (bf16[144,1280]{1,0:T(8,128)(2,1)}, bf16[144,1280]{1,0:T(8,128)(2,1)}, u32[]{:S(2)}, u32[]{:S(2)}) collective-permute-start(bf16[144,1280]{1,0:T(8,128)(2,1)} %get-tuple-element.46.rest_0_), channel_id=1, source_target_pairs={{0,8},{8,16},{16,24},{24,28},{28,20},{20,12},{12,4},{4,0},{1,9},{9... | collective-permute-start | bytes 1105928 | tf_op jit(solution)/shard_map/ppermute | solution.py:555
  85.8 19.7 %collective-permute-start.12 = (bf16[144,1280]{1,0:T(8,128)(2,1)}, bf16[144,1280]{1,0:T(8,128)(2,1)}, u32[]{:S(2)}, u32[]{:S(2)}) collective-permute-start(bf16[144,1280]{1,0:T(8,128)(2,1)} %get-tuple-element.46.rest_0_), channel_id=1, source_target_pairs={{8,0},{16,8},{24,16},{28,24},{20,28},{12,20},{4,12},{0,4},{9,1},{1... | collective-permute-start | bytes 1105928 | tf_op jit(solution)/shard_map/ppermute | solution.py:558
  94.4 11.8 %collective-permute-start.13 = (bf16[144,1280]{1,0:T(8,128)(2,1)}, bf16[144,1280]{1,0:T(8,128)(2,1)}, u32[]{:S(2)}, u32[]{:S(2)}) collective-permute-start(bf16[144,1280]{1,0:T(8,128)(2,1)} %collective-permute-done.11.rest_1_), channel_id=1, source_target_pairs={{0,8},{8,16},{16,24},{24,28},{28,20},{20,12},{12,4},{4,0},{1,9},{9... | collective-permute-start | bytes 1105928 | tf_op jit(solution)/shard_map/ppermute | solution.py:555
  94.7 4.0 %copy-start.33 = (bf16[2,2,512,640]{2,3,0,1:T(8,128)(2,1)S(1)}, bf16[2,2,512,640]{2,3,0,1:T(8,128)(2,1)}, u32[]{:S(2)}) copy-start(bf16[2,2,512,640]{2,3,0,1:T(8,128)(2,1)} %copy-done.32) | copy-start | bytes 7864324
  96.9 23.2 %collective-permute-start.20 = (bf16[640,512]{1,0:T(8,128)(2,1)S(1)}, bf16[640,512]{1,0:T(8,128)(2,1)S(1)}, u32[]{:S(2)}, u32[]{:S(2)}) collective-permute-start(bf16[640,512]{1,0:T(8,128)(2,1)S(1)} %get-tuple-element.70.mine), channel_id=1, source_target_pairs={{0,4},{4,0},{8,12},{12,8},{16,20},{20,16},{24,28},{28,24},{1,5},{5... | collective-permute-start | bytes 1966088 | tf_op jit(solution)/shard_map/ppermute | solution.py:642
  105.5 18.3 %collective-permute-start.14 = (bf16[144,1280]{1,0:T(8,128)(2,1)}, bf16[144,1280]{1,0:T(8,128)(2,1)S(1)}, u32[]{:S(2)}, u32[]{:S(2)}) collective-permute-start(bf16[144,1280]{1,0:T(8,128)(2,1)} %collective-permute-done.12.rest_2_), channel_id=1, source_target_pairs={{8,0},{16,8},{24,16},{28,24},{20,28},{12,20},{4,12},{0,4},{9,1},{1... | collective-permute-start | bytes 1105928 | tf_op jit(solution)/shard_map/ppermute | solution.py:558
  106.2 21.9 %collective-permute-start.15 = (bf16[144,1280]{1,0:T(8,128)(2,1)}, bf16[144,1280]{1,0:T(8,128)(2,1)}, u32[]{:S(2)}, u32[]{:S(2)}) collective-permute-start(bf16[144,1280]{1,0:T(8,128)(2,1)} %collective-permute-done.13.rest_3_), channel_id=1, source_target_pairs={{0,8},{8,16},{16,24},{24,28},{28,20},{20,12},{12,4},{4,0},{1,9},{9... | collective-permute-start | bytes 1105928 | tf_op jit(solution)/shard_map/ppermute | solution.py:555
  109.2 37.1 %collective-permute-start.27 = (bf16[640,512]{1,0:T(8,128)(2,1)S(1)}, bf16[640,512]{1,0:T(8,128)(2,1)S(1)}, u32[]{:S(2)}, u32[]{:S(2)}) collective-permute-start(bf16[640,512]{1,0:T(8,128)(2,1)S(1)} %get-tuple-element.71.mine), channel_id=1, source_target_pairs={{0,4},{4,0},{8,12},{12,8},{16,20},{20,16},{24,28},{28,24},{1,5},{5... | collective-permute-start | bytes 1966088 | tf_op jit(solution)/shard_map/ppermute | solution.py:642
  120.1 8.0 %copy-start.3 = (bf16[512,128]{1,0:T(8,128)(2,1)S(1)}, bf16[512,128]{1,0:T(8,128)(2,1)}, u32[]{:S(2)}) copy-start(bf16[512,128]{1,0:T(8,128)(2,1)} %read.7) | copy-start | bytes 393220
  120.1 8.0 %copy-start.5 = (bf16[512,128]{1,0:T(8,128)(2,1)S(1)}, bf16[512,128]{1,0:T(8,128)(2,1)}, u32[]{:S(2)}) copy-start(bf16[512,128]{1,0:T(8,128)(2,1)} %write.7) | copy-start | bytes 393220
  120.1 8.0 %copy-start.8 = (f32[512,128]{1,0:T(8,128)S(1)}, f32[512,128]{1,0:T(8,128)}, u32[]{:S(2)}) copy-start(f32[512,128]{1,0:T(8,128)} %copy-done.7) | copy-start | bytes 786436
  120.1 8.0 %copy-start.20 = (bf16[512,1280]{1,0:T(8,128)(2,1)S(1)}, bf16[512,1280]{1,0:T(8,128)(2,1)}, u32[]{:S(2)}) copy-start(bf16[512,1280]{1,0:T(8,128)(2,1)} %copy-done.17) | copy-start | bytes 3932164
  120.1 8.0 %copy-start.29 = (f32[128,512]{1,0:T(8,128)S(1)}, f32[128,512]{1,0:T(8,128)}, u32[]{:S(2)}) copy-start(f32[128,512]{1,0:T(8,128)} %copy-done.28) | copy-start | bytes 786436
  121.2 33.0 %collective-permute-start.24 = (bf16[640,320]{1,0:T(8,128)(2,1)S(1)}, bf16[640,320]{1,0:T(8,128)(2,1)}, u32[]{:S(2)}, u32[]{:S(2)}) collective-permute-start(bf16[640,320]{1,0:T(8,128)(2,1)S(1)} %product.8), channel_id=1, source_target_pairs={{0,24},{4,28},{8,0},{12,4},{16,8},{20,12},{24,16},{28,20},{1,25},{... | collective-permute-start | bytes 1228808 | tf_op jit(solution)/shard_map/ppermute | solution.py:661
  123.9 31.8 %collective-permute-start.16 = (bf16[144,1280]{1,0:T(8,128)(2,1)S(1)}, bf16[144,1280]{1,0:T(8,128)(2,1)}, u32[]{:S(2)}, u32[]{:S(2)}) collective-permute-start(bf16[144,1280]{1,0:T(8,128)(2,1)S(1)} %collective-permute-done.14.rest_4_), channel_id=1, source_target_pairs={{8,0},{16,8},{24,16},{28,24},{20,28},{12,20},{4,12},{0,4},{9,1},{1... | collective-permute-start | bytes 1105928 | tf_op jit(solution)/shard_map/ppermute | solution.py:558
  128.1 27.7 %collective-permute-start.17 = (bf16[144,1280]{1,0:T(8,128)(2,1)}, bf16[144,1280]{1,0:T(8,128)(2,1)}, u32[]{:S(2)}, u32[]{:S(2)}) collective-permute-start(bf16[144,1280]{1,0:T(8,128)(2,1)} %collective-permute-done.15.rest_5_), channel_id=1, source_target_pairs={{0,8},{8,16},{16,24},{24,28},{28,20},{20,12},{12,4},{4,0},{1,9},{9... | collective-permute-start | bytes 1105928 | tf_op jit(solution)/shard_map/ppermute | solution.py:555
  141.9 53.1 %collective-permute-start.25 = (bf16[640,320]{1,0:T(8,128)(2,1)S(1)}, bf16[640,320]{1,0:T(8,128)(2,1)}, u32[]{:S(2)}, u32[]{:S(2)}) collective-permute-start(bf16[640,320]{1,0:T(8,128)(2,1)S(1)} %product.9), channel_id=1, source_target_pairs={{0,16},{4,20},{8,24},{12,28},{16,0},{20,4},{24,8},{28,12},{1,17},{... | collective-permute-start | bytes 1228808 | tf_op jit(solution)/shard_map/ppermute | solution.py:661
  146.2 48.9 %collective-permute-start.26 = (bf16[640,320]{1,0:T(8,128)(2,1)S(1)}, bf16[640,320]{1,0:T(8,128)(2,1)}, u32[]{:S(2)}, u32[]{:S(2)}) collective-permute-start(bf16[640,320]{1,0:T(8,128)(2,1)S(1)} %product.10), channel_id=1, source_target_pairs={{0,8},{4,12},{8,16},{12,20},{16,24},{20,28},{24,0},{28,4},{1,9},{5... | collective-permute-start | bytes 1228808 | tf_op jit(solution)/shard_map/ppermute | solution.py:661
  153.0 3.3 %copy-start.9 = (f32[512,128]{1,0:T(8,128)S(1)}, f32[512,128]{1,0:T(8,128)}, u32[]{:S(2)}) copy-start(f32[512,128]{1,0:T(8,128)} %copy-done.7) | copy-start | bytes 786436
  153.1 3.3 %copy-start.14 = (bf16[256,1280]{1,0:T(8,128)(2,1)S(1)}, bf16[256,1280]{1,0:T(8,128)(2,1)}, u32[]{:S(2)}) copy-start(bf16[256,1280]{1,0:T(8,128)(2,1)} %copy-done.11) | copy-start | bytes 1966084
  153.1 3.3 %copy-start.16 = (f32[128,1280]{1,0:T(8,128)S(1)}, f32[128,1280]{1,0:T(8,128)}, u32[]{:S(2)}) copy-start(f32[128,1280]{1,0:T(8,128)} %copy-done.15) | copy-start | bytes 1966084
  153.1 3.3 %copy-start.23 = (f32[8,1280]{1,0:T(8,128)S(1)}, f32[8,1280]{1,0:T(8,128)}, u32[]{:S(2)}) copy-start(f32[8,1280]{1,0:T(8,128)} %copy-done.22) | copy-start | bytes 122884
  153.1 3.3 %copy-start.25 = (f32[512,128]{1,0:T(8,128)S(1)}, f32[512,128]{1,0:T(8,128)}, u32[]{:S(2)}) copy-start(f32[512,128]{1,0:T(8,128)} %copy-done.24) | copy-start | bytes 786436
  153.1 3.3 %copy-start.27 = (f32[512,128]{1,0:T(8,128)S(1)}, f32[512,128]{1,0:T(8,128)}, u32[]{:S(2)}) copy-start(f32[512,128]{1,0:T(8,128)} %copy-done.26) | copy-start | bytes 786436
  153.1 3.3 %copy-start.31 = (f32[8,1280]{1,0:T(8,128)S(1)}, f32[8,1280]{1,0:T(8,128)}, u32[]{:S(2)}) copy-start(f32[8,1280]{1,0:T(8,128)} %copy-done.30) | copy-start | bytes 122884
  154.2 42.4 %collective-permute-start.28 = (bf16[640,320]{1,0:T(8,128)(2,1)S(1)}, bf16[640,320]{1,0:T(8,128)(2,1)S(1)}, u32[]{:S(2)}, u32[]{:S(2)}) collective-permute-start(bf16[640,320]{1,0:T(8,128)(2,1)S(1)} %product.12), channel_id=1, source_target_pairs={{0,24},{4,28},{8,0},{12,4},{16,8},{20,12},{24,16},{28,20},{1,25},{... | collective-permute-start | bytes 1228808 | tf_op jit(solution)/shard_map/ppermute | solution.py:661
  155.6 58.4 %collective-permute-start.29 = (bf16[640,320]{1,0:T(8,128)(2,1)S(1)}, bf16[640,320]{1,0:T(8,128)(2,1)S(1)}, u32[]{:S(2)}, u32[]{:S(2)}) collective-permute-start(bf16[640,320]{1,0:T(8,128)(2,1)S(1)} %product.13), channel_id=1, source_target_pairs={{0,16},{4,20},{8,24},{12,28},{16,0},{20,4},{24,8},{28,12},{1,17},{... | collective-permute-start | bytes 1228808 | tf_op jit(solution)/shard_map/ppermute | solution.py:661
  155.8 58.2 %collective-permute-start.30 = (bf16[640,320]{1,0:T(8,128)(2,1)S(1)}, bf16[640,320]{1,0:T(8,128)(2,1)S(1)}, u32[]{:S(2)}, u32[]{:S(2)}) collective-permute-start(bf16[640,320]{1,0:T(8,128)(2,1)S(1)} %product.14), channel_id=1, source_target_pairs={{0,8},{4,12},{8,16},{12,20},{16,24},{20,28},{24,0},{28,4},{1,9},{5... | collective-permute-start | bytes 1228808 | tf_op jit(solution)/shard_map/ppermute | solution.py:661
  195.1 19.2 %collective-permute-start.18 = (f32[512,256]{1,0:T(8,128)S(1)}, f32[512,256]{1,0:T(8,128)S(1)}, u32[]{:S(2)}, u32[]{:S(2)}) collective-permute-start(f32[512,256]{1,0:T(8,128)S(1)} %get-tuple-element.49), channel_id=1, source_target_pairs={{0,1},{1,0},{2,3},{3,2},{4,5},{5,4},{6,7},{7,6},{8,9},{9,8},{10,11... | collective-permute-start | bytes 1572872 | tf_op jit(solution)/shard_map/ppermute | solution.py:575
  214.4 12.0 %collective-permute-start.19 = (f32[512,256]{1,0:T(8,128)S(1)}, f32[512,256]{1,0:T(8,128)S(1)}, u32[]{:S(2)}, u32[]{:S(2)}) collective-permute-start(f32[512,256]{1,0:T(8,128)S(1)} %add.108), channel_id=1, source_target_pairs={{0,2},{1,3},{2,0},{3,1},{4,6},{5,7},{6,4},{7,5},{8,10},{9,11},{10,... | collective-permute-start | bytes 1572872 | tf_op jit(solution)/shard_map/ppermute | solution.py:575
  (11 other events, 13.6 us)

commit v2 on v1

v2 whole, which is shorter than its diff:
```python
import functools
import jax
import jax.numpy as jnp
from jax import lax
from jax.experimental import pallas as pl
from jax.experimental.pallas import tpu as pltpu
from jax.sharding import PartitionSpec as P

F32 = jnp.float32
BF16 = jnp.bfloat16
LANES = 128
EXTRA = 16
EPSILON = 1e-05
NORMED_PARTS = 2
HALF = LANES // 2


def mm(a, b):
    return jnp.dot(a, b, preferred_element_type=F32)


def mm_t(a, b):
    return lax.dot_general(a, b, (((1,), (1,)), ((), ())), preferred_element_type=F32)


def split2(v):
    high = v.astype(BF16)
    return high, (v - high.astype(F32)).astype(BF16)


def split3(v):
    high = v.astype(BF16)
    rest = v - high.astype(F32)
    middle = rest.astype(BF16)
    return high, middle, (rest - middle.astype(F32)).astype(BF16)


def iota(shape, axis):
    return lax.broadcasted_iota(jnp.int32, shape, axis)


def spread(values, spread2):
    return mm(jnp.concatenate(split2(values), axis=1), spread2)


def params(limit=24 << 20):
    return pltpu.CompilerParams(vmem_limit_bytes=limit)


def cost(flops, nbytes, special=0):
    return pl.CostEstimate(flops=int(flops), bytes_accessed=int(nbytes), transcendentals=int(special))


def skipping(kernel, first, extra):
    return lambda *refs: kernel(*refs[:first], *refs[first + extra :])


WAIT = pl.BlockSpec(memory_space=pl.ANY)


def prepare_kernel(
    heads, packed, expo, decay, skip, write, read,
    x_out, near_out, far_out, seg_t_out, seg_out, spread_out, skip_out, read_t_out, pad, pad8,
):
    length, width = x_out.shape
    head_width = width // heads
    rows8 = packed.shape[0]
    groups = expo.shape[0]
    pad[...] = jnp.zeros_like(pad)
    pad[0:heads, :] = decay[...]
    decay_t = pad[...].T
    lower = (iota((length, length), 0) >= iota((length, length), 1)).astype(BF16)
    seg_t = sum(mm(lower, part) for part in split3(decay_t))
    seg_t_out[...] = seg_t
    seg_out[...] = seg_t.T
    of_head = (iota((LANES, width), 1) // head_width == iota((LANES, width), 0)).astype(BF16)
    spread2 = jnp.concatenate([of_head, of_head], axis=0)
    spread_out[...] = spread2
    pad8[...] = jnp.zeros_like(pad8)
    pad8[0:1, 0:heads] = skip[...]
    skip_out[...] = sum(mm(part, of_head) for part in split3(pad8[...]))
    total = seg_t[length - 1 : length, :]
    to_end = spread(jnp.exp(total - seg_t), spread2)
    pad[...] = jnp.zeros_like(pad)
    pad[0:groups, :] = jnp.left_shift(1, expo[...] + 8).astype(F32) * (2.0**-8)
    of_group = (
        iota((LANES, width), 1) // (width // groups) == iota((LANES, width), 0)
    ).astype(BF16)
    factors = mm(pad[...].T.astype(BF16), of_group)
    words = jnp.broadcast_to(packed[...][:, None, :], (rows8, 8, width))
    words = jnp.right_shift(words, 4 * iota((rows8, 8, width), 1))
    fields = (jnp.bitwise_and(words, 15) - 8).astype(F32).reshape(length, width)
    x = fields * factors
    x_out[...] = x.astype(BF16)
    states = mm(write[...].T, (x * to_end).astype(BF16)).astype(BF16)
    read_t_out[...] = read[...].T
    near_out[0:HALF, :] = states[0:HALF, :]
    far_out[...] = states[HALF:, :]
    total8 = jnp.broadcast_to(total, (8, LANES))
    high, middle, low = (mm(part, of_head) for part in split3(total8))
    row = iota((EXTRA, width), 0)
    tail = jnp.where(row == 0, high[0:1, :], jnp.where(row == 1, middle[0:1, :], low[0:1, :]))
    near_out[HALF:, :] = jnp.where(row < 3, tail, 0.0).astype(BF16)


def prepare(packed, expo, decay, skip, write, read):
    heads, length = decay.shape
    width = packed.shape[1]
    shapes = (
        jax.ShapeDtypeStruct((length, width), BF16),
        jax.ShapeDtypeStruct((HALF + EXTRA, width), BF16),
        jax.ShapeDtypeStruct((HALF, width), BF16),
        jax.ShapeDtypeStruct((length, LANES), F32),
        jax.ShapeDtypeStruct((LANES, length), F32),
        jax.ShapeDtypeStruct((2 * LANES, width), BF16),
        jax.ShapeDtypeStruct((8, width), F32),
        jax.ShapeDtypeStruct((LANES, length), BF16),
    )
    return pl.pallas_call(
        functools.partial(prepare_kernel, heads),
        name="prepare",
        out_shape=shapes,
        scratch_shapes=[pltpu.VMEM((LANES, length), F32), pltpu.VMEM((8, LANES), F32)],
        compiler_params=params(),
        cost_estimate=cost(3e9, 8e6),
    )(packed, expo, decay, skip, write, read)


def pick_kernel(per_half, columns, parity, shard, out):
    odd_wanted = parity[0] == 0
    for sub in range(per_half):
        even_part = shard[:, 2 * sub * columns : (2 * sub + 1) * columns]
        odd_part = shard[:, (2 * sub + 1) * columns : (2 * sub + 2) * columns]
        out[:, sub * columns : (sub + 1) * columns] = jnp.where(odd_wanted, odd_part, even_part)


def pick(parity, shard, columns):
    length, shard_width = shard.shape
    out = (length, shard_width // 2)
    return pl.pallas_call(
        functools.partial(pick_kernel, shard_width // (2 * columns), columns),
        name="pick",
        grid_spec=pltpu.PrefetchScalarGridSpec(
            num_scalar_prefetch=1, grid=(1,), in_specs=[whole(shard.shape)], out_specs=whole(out)
        ),
        out_shape=jax.ShapeDtypeStruct(out, BF16),
        compiler_params=params(),
        cost_estimate=cost(1e8, 2e6),
    )(parity, shard)


def cotangent_kernel(shards, per_half, owners, weight, *rest):
    mine = rest[:shards]
    theirs = rest[shards : 2 * shards]
    grad_v, cot_mine, cot_theirs, full = rest[2 * shards :]
    shard_width = mine[0].shape[1]
    columns = cot_mine.shape[1]

    @pl.when(pl.program_id(0) == 0)
    def _():
        odd = owners[shards] == 1
        for m in range(shards):
            for q in range(shards):
                @pl.when(owners[m] == q)
                def _():
                    full[:, q * shard_width : (q + 1) * shard_width] = mine[m][...]
            for sub in range(per_half):
                even_part = mine[m][:, 2 * sub * columns : (2 * sub + 1) * columns]
                odd_part = mine[m][:, (2 * sub + 1) * columns : (2 * sub + 2) * columns]
                spot = owners[m] * per_half + sub
                cot_mine[spot] = jnp.where(odd, odd_part, even_part).T
                cot_theirs[spot] = theirs[m][:, sub * columns : (sub + 1) * columns].T

    grad_v[...] = mm_t(full[...], weight[...])


def cotangent(owners, weight, mine, theirs, columns, waits):
    shards = len(mine)
    length, shard_width = mine[0].shape
    width, model_width = weight.shape
    per_half = shard_width // (2 * columns)
    groups = shards * per_half
    block = 2 * LANES if width % (2 * LANES) == 0 else LANES
    stacked = (groups, columns, length)
    return pl.pallas_call(
        skipping(
            functools.partial(cotangent_kernel, shards, per_half), 2 + 2 * shards, len(waits)
        ),
        name="cotangent",
        grid_spec=pltpu.PrefetchScalarGridSpec(
            num_scalar_prefetch=1,
            grid=(width // block,),
            in_specs=[pl.BlockSpec((block, model_width), lambda i, *_: (i, 0))]
            + [whole(mine[0].shape)] * shards
            + [whole(theirs[0].shape)] * shards
            + [WAIT] * len(waits),
            out_specs=[
                pl.BlockSpec((length, block), lambda i, *_: (0, i)), whole(stacked), whole(stacked),
            ],
            scratch_shapes=[pltpu.VMEM((length, model_width), BF16)],
        ),
        out_shape=(
            jax.ShapeDtypeStruct((length, width), F32),
            jax.ShapeDtypeStruct(stacked, BF16),
            jax.ShapeDtypeStruct(stacked, BF16),
        ),
        compiler_params=params(),
        cost_estimate=cost(2.0 * length * width * model_width, 20e6),
    )(owners, weight, *mine, *theirs, *waits)


def pair_columns(seg_t, seg, step):
    rolled = pltpu.roll(seg_t[...], lax.rem(LANES - 2 * step, LANES), 1)
    for side in (0, 1):
        yield side, rolled[:, side : side + 1], seg[pl.ds(2 * step + side, 1), :]


def inside_kernel(head_width, start, seg_t, seg, write, read, x, skip, *rest):
    out, cross = rest[-2:]
    step = pl.program_id(0) + start
    length = x.shape[0]
    half = length // 2

    @pl.when(pl.program_id(0) == 0)
    def _():
        cross[...] = mm_t(read[...], write[...])

    diagonal = iota((half, half), 0) >= iota((half, half), 1)
    parts = []
    for side, column, row in pair_columns(seg_t, seg, step):
        rows = []
        for block in (0, 1):
            low = block * half
            square = slice(low, low + half)
            gap = column[square] - row[:, square]
            decayed = jnp.where(diagonal, jnp.exp(jnp.minimum(gap, 0.0)), 0.0)
            mixing = decayed * cross[square, square]
            if block == 1:
                left = jnp.exp(column[square] - row[:, 0:half]) * cross[square, 0:half]
                mixing = jnp.concatenate([left, mixing], axis=1)
            high, rest = split2(mixing)
            values = x[0 : low + half, :]
            rows.append(mm(high, values) + mm(rest, values))
        parts.append(jnp.concatenate(rows, axis=0))
    first = iota((length, LANES), 1) < head_width
    out[...] = jnp.where(first, parts[0], parts[1]) + skip[0:1, :] * x[...].astype(F32)


def whole(shape):
    return pl.BlockSpec(shape, lambda *_: (0,) * len(shape))


def inside(heads, start, stop, seg_t, seg, write, read, x, skip, held=None, waits=()):
    length, width = x.shape
    column = pl.BlockSpec((length, LANES), lambda j: (0, j + start))
    share = (stop - start) / (width // LANES)
    operands = (seg_t, seg, write, read, x, skip)
    specs = [
        whole((length, LANES)), whole((LANES, length)), whole(write.shape), whole(read.shape),
        column, pl.BlockSpec((8, LANES), lambda j: (0, j + start)),
    ]
    aliases = {}
    if held is not None:
        aliases = {len(operands): 0}
        operands = operands + (held,)
        specs = specs + [WAIT]
    operands = operands + tuple(waits)
    specs = specs + [WAIT] * len(waits)
    return pl.pallas_call(
        functools.partial(inside_kernel, width // heads, start),
        name="inside",
        grid=(stop - start,),
        in_specs=specs,
        out_specs=column,
        out_shape=jax.ShapeDtypeStruct((length, width), F32),
        scratch_shapes=[pltpu.VMEM((length, length), F32)],
        input_output_aliases=aliases,
        compiler_params=params(),
        cost_estimate=cost(20e9 * share, 5e6 * share),
    )(*operands)


def gathered_total(pays, k):
    tail = pays[k][HALF : HALF + 8, :].astype(F32)
    return tail[0:1, :] + tail[1:2, :] + tail[2:3, :]


def boundary(totals, near, far, sources, position, count):
    width = totals.shape[1]
    column = jnp.zeros((count, 1), jnp.int32)
    for k in range(count):
        column = jnp.where(iota((count, 1), 0) == k, sources[k], column)
    powers = jnp.zeros((count, width), F32)
    for j in range(count):
        between = jnp.logical_and(column < sources[j], sources[j] < position)
        powers = powers + jnp.where(between, totals[j : j + 1, :], 0.0)
    weights = jnp.where(column < position, jnp.exp(powers), 0.0)
    upper = jnp.zeros((HALF, width), F32)
    lower = jnp.zeros((HALF, width), F32)
    for k in range(count):
        upper = upper + weights[k : k + 1, :] * near[k][0:HALF, :].astype(F32)
        lower = lower + weights[k : k + 1, :] * far[k][...].astype(F32)
    return upper, lower


def enter_kernel(
    count, sources, y_local, gate, grad_v, gain, read, seg_t, spread2, *rest,
):
    near, far = rest[:count], rest[count : 2 * count]
    y_out, scaled_t_out, stats_out, state_out, totals_out, state2 = rest[2 * count :]

    @pl.when(pl.program_id(0) == 0)
    def _():
        for k in range(count):
            totals_out[k : k + 1, :] = gathered_total(near, k)
        upper, lower = boundary(totals_out[...], near, far, sources, sources[count], count)
        state_out[0:HALF, :] = upper
        state_out[HALF:, :] = lower
        state2[0:LANES, :], state2[LANES:, :] = split2(state_out[...])

    from_start = spread(jnp.exp(seg_t[...]), spread2[...])
    read_part = read[...]
    carried = mm(jnp.concatenate([read_part, read_part], axis=1), state2[...])
    y = y_local[...] + from_start * carried
    y_out[...] = y
    z = gate[...].astype(F32)
    mixed = y * z / (1.0 + jnp.exp(-z))
    with_gain = mixed * gain[...]
    scaled_t_out[...] = with_gain.T
    squares = jnp.sum(mixed * mixed, axis=1, keepdims=True)
    inner = jnp.sum(grad_v[...] * with_gain, axis=1, keepdims=True)
    lane = iota((squares.shape[0], LANES), 1)
    stats = jnp.where(lane == 0, squares, jnp.where(lane == 1, inner, 0.0))
    stats_out[...] = stats.T[0:8, :]


def enter(sources, y_local, gate, grad_v, gain, read, seg_t, spread2, near, far):
    length, width = y_local.shape
    count = len(near)
    block = LANES
    token = pl.BlockSpec((block, width), lambda i, *_: (i, 0))
    narrow = pl.BlockSpec((block, LANES), lambda i, *_: (i, 0))
    shapes = (
        jax.ShapeDtypeStruct((length, width), F32),
        jax.ShapeDtypeStruct((width, length), F32),
        jax.ShapeDtypeStruct((8, length), F32),
        jax.ShapeDtypeStruct((LANES, width), F32),
        jax.ShapeDtypeStruct((count, width), F32),
    )
    return pl.pallas_call(
        functools.partial(enter_kernel, count),
        name="enter",
        grid_spec=pltpu.PrefetchScalarGridSpec(
            num_scalar_prefetch=1,
            grid=(length // block,),
            in_specs=[
                token, token, token, whole((1, width)), narrow, narrow, whole(spread2.shape),
            ] + [whole(near[0].shape)] * count + [whole(far[0].shape)] * count,
            out_specs=[
                token,
                pl.BlockSpec((width, block), lambda i, *_: (0, i)),
                pl.BlockSpec((8, block), lambda i, *_: (0, i)),
                whole((LANES, width)),
                whole((count, width)),
            ],
            scratch_shapes=[pltpu.VMEM((2 * LANES, width), BF16)],
        ),
        out_shape=shapes,
        compiler_params=params(),
        cost_estimate=cost(3e9, 15e6),
    )(sources, y_local, gate, grad_v, gain, read, seg_t, spread2, *near, *far)


def gate_kernel(
    total_width, sources, y_ref, gate, grad_v, gain, stats, x, seg_t, spread2, read_t,
    gate_out, grad_y_out, send_out, keep_out, sums, columns, cot,
):
    step = pl.program_id(0)
    row = iota((LANES, LANES), 0)
    squares, inner = stats[0:1, :], stats[1:2, :]
    scale_row = lax.rsqrt(squares * (1.0 / total_width) + EPSILON)
    back_row = scale_row * scale_row * scale_row * inner * (1.0 / total_width)
    columns[...] = jnp.where(row == 0, scale_row, jnp.where(row == 1, back_row, 0.0)).T
    scale, back = columns[:, 0:1], columns[:, 1:2]
    y = y_ref[...]
    z = gate[...].astype(F32)
    sigma = 1.0 / (1.0 + jnp.exp(-z))
    active = z * sigma
    mixed = y * active
    scaled_v = scale * grad_v[...]
    grad_mixed = scaled_v * gain[...] - mixed * back
    gate_out[...] = (grad_mixed * y * sigma * (1.0 + z * (1.0 - sigma))).astype(BF16)
    grad_y = grad_mixed * active
    grad_y_out[...] = grad_y
    gain_part = jnp.sum(scaled_v * mixed, axis=0, keepdims=True)
    skip_part = jnp.sum(grad_y * x[...].astype(F32), axis=0, keepdims=True)
    from_start = spread(jnp.exp(seg_t[...]), spread2[...])
    cot_part = mm(read_t[...], (grad_y * from_start).astype(BF16))
    wide = iota((8, grad_y.shape[1]), 0)
    sum_part = jnp.where(wide == 0, gain_part, jnp.where(wide == 1, skip_part, 0.0))

    @pl.when(step == 0)
    def _():
        cot[...] = cot_part
        sums[...] = sum_part

    @pl.when(step > 0)
    def _():
        cot[...] += cot_part
        sums[...] += sum_part

    @pl.when(step == pl.num_programs(0) - 1)
    def _():
        parity = lax.rem(sources[sources.shape[0] - 1], 2)
        keep_out[...] = cot[pl.ds(pl.multiple_of(parity * HALF, HALF), HALF), :]
        send_out[...] = cot[pl.ds(pl.multiple_of((1 - parity) * HALF, HALF), HALF), :].astype(BF16)


def gate_grads(total_width, sources, y, gate, grad_v, gain, stats, x, seg_t, spread2, read_t):
    length, width = y.shape
    block = LANES
    token = pl.BlockSpec((block, width), lambda i, *_: (i, 0))
    narrow = pl.BlockSpec((block, LANES), lambda i, *_: (i, 0))
    shapes = (
        jax.ShapeDtypeStruct((length, width), BF16),
        jax.ShapeDtypeStruct((length, width), F32),
        jax.ShapeDtypeStruct((HALF, width), BF16),
        jax.ShapeDtypeStruct((HALF, width), F32),
        jax.ShapeDtypeStruct((8, width), F32),
    )
    return pl.pallas_call(
        functools.partial(gate_kernel, total_width),
        name="gate_grads",
        grid_spec=pltpu.PrefetchScalarGridSpec(
            num_scalar_prefetch=1,
            grid=(length // block,),
            in_specs=[
                token, token, token, whole((1, width)), pl.BlockSpec((8, block), lambda i, *_: (0, i)),
                token, narrow, whole(spread2.shape), pl.BlockSpec((LANES, block), lambda i, *_: (0, i)),
            ],
            out_specs=[
                token, token, whole((HALF, width)), whole((HALF, width)), whole((8, width)),
            ],
            scratch_shapes=[pltpu.VMEM((LANES, LANES), F32), pltpu.VMEM((LANES, width), F32)],
        ),
        out_shape=shapes,
        compiler_params=params(),
        cost_estimate=cost(3e9, 15e6),
    )(sources, y, gate, grad_v, gain, stats, x, seg_t, spread2, read_t)


def inside_back_kernel(
    head_width, start, last, seg_t, seg, write, read, x, grad_y, *rest,
):
    step = pl.program_id(0) + start
    if last:
        before, out, grad_write, grad_read, cross, grad_cross = rest[-6:]
    else:
        out, sum_out, cross, grad_cross = rest[-4:]
    length = x.shape[0]
    half = length // 2

    @pl.when(pl.program_id(0) == 0)
    def _():
        cross[...] = mm_t(write[...], read[...])
        grad_cross[...] = before[...] if last else jnp.zeros_like(grad_cross)

    diagonal = iota((half, half), 0) <= iota((half, half), 1)
    first = iota((length, LANES), 1) < head_width
    grads = grad_y[...].astype(BF16)
    values = x[...]
    parts = []
    for side, column, row in pair_columns(seg_t, seg, step):
        mine = first if side == 0 else jnp.logical_not(first)
        own = jnp.where(mine, values, jnp.zeros_like(values))
        rows = []
        for block in (0, 1):
            low = block * half
            square = slice(low, low + half)
            gap = row[:, square] - column[square]
            decayed = jnp.where(diagonal, jnp.exp(jnp.minimum(gap, 0.0)), 0.0)
            mixing = decayed * cross[square, square]
            grad_cross[square, square] += mm_t(own[square], grads[square]) * decayed
            if block == 0:
                decayed = jnp.exp(row[:, half:] - column[square])
                mixing = jnp.concatenate([mixing, decayed * cross[square, half:]], axis=1)
                grad_cross[square, half:] += mm_t(own[square], grads[half:]) * decayed
            rows.append(mm(mixing.astype(BF16), grads[low:]))
        parts.append(jnp.concatenate(rows, axis=0))
    out[...] = jnp.where(first, parts[0], parts[1])

    @pl.when(pl.program_id(0) == pl.num_programs(0) - 1)
    def _():
        if last:
            high, low = split2(grad_cross[...])
            grad_write[...] = mm(high, read[...]) + mm(low, read[...])
            turned = grad_cross[...].T
            high, low = split2(turned)
            grad_read[...] = mm(high, write[...]) + mm(low, write[...])
        else:
            sum_out[...] = grad_cross[...]


def inside_back(heads, start, stop, seg_t, seg, write, read, x, grad_y, held=None, before=None):
    length, width = x.shape
    last = held is not None
    column = pl.BlockSpec((length, LANES), lambda j: (0, j + start))
    square = (length, length)
    small = (length, LANES)
    operands = (seg_t, seg, write, read, x, grad_y)
    specs = [
        whole((length, LANES)), whole((LANES, length)), whole(write.shape), whole(read.shape),
        column, column,
    ]
    share = (stop - start) / (width // LANES)
    outs = (jax.ShapeDtypeStruct((length, width), F32),)
    aliases = {}
    if last:
        operands = operands + (held, before)
        specs = specs + [WAIT, whole(square)]
        aliases = {6: 0}
        outs = outs + (jax.ShapeDtypeStruct(small, F32), jax.ShapeDtypeStruct(small, F32))
        out_specs = [column, whole(small), whole(small)]
    else:
        outs = outs + (jax.ShapeDtypeStruct(square, F32),)
        out_specs = [column, whole(square)]
    return pl.pallas_call(
        functools.partial(inside_back_kernel, width // heads, start, last),
        name="inside_back",
        grid=(stop - start,),
        in_specs=specs,
        out_specs=out_specs,
        out_shape=outs,
        scratch_shapes=[pltpu.VMEM(square, F32), pltpu.VMEM(square, F32)],
        input_output_aliases=aliases,
        compiler_params=params(),
        cost_estimate=cost(20e9 * share, 8e6 * share),
    )(*operands)


def total_of(totals, sources, count, wanted):
    found = jnp.zeros_like(totals[0:1, :])
    for k in range(count):
        found = found + jnp.where(sources[k] == wanted, totals[k : k + 1, :], 0.0)
    return found


def pair_kernel(count, sources, totals, keep, received, out):
    position = sources[count]
    odd = lax.rem(position, 2) == 1
    weight = jnp.exp(total_of(totals, sources, count, position - lax.rem(position, 2)))
    own, other = keep[...], received[...].astype(F32)
    out[...] = jnp.where(odd, other + weight * own, own + weight * other).astype(BF16)


def join_kernel(count, sources, totals, keep, received, *rest):
    shifts = count // 2 - 1
    later, (own_out, send_out) = rest[:shifts], rest[shifts:]
    position = sources[count]
    even_place = position - lax.rem(position, 2)
    odd = lax.rem(position, 2) == 1
    state = jnp.zeros_like(keep)
    power = jnp.zeros_like(totals[0:1, :])
    for shift in range(1, shifts + 1):
        state = state + jnp.exp(power) * later[shift - 1][...].astype(F32)
        if shift < shifts:
            power = power + total_of(totals, sources, count, even_place + 2 * shift)
            power = power + total_of(totals, sources, count, even_place + 2 * shift + 1)
    weight = jnp.exp(total_of(totals, sources, count, even_place + 1))
    of_odd = jnp.where(odd, keep[...], received[...].astype(F32))
    for_even = of_odd + weight * state
    own_out[...] = jnp.where(odd, state, for_even)
    send_out[...] = jnp.where(odd, for_even, state).astype(BF16)


def small_call(kernel, count, outs, sources, *arrays, waits=()):
    return pl.pallas_call(
        skipping(functools.partial(kernel, count), 1 + len(arrays), len(waits)),
        grid_spec=pltpu.PrefetchScalarGridSpec(
            num_scalar_prefetch=1,
            grid=(1,),
            in_specs=[whole(a.shape) for a in arrays] + [WAIT] * len(waits),
            out_specs=[whole(o.shape) for o in outs],
        ),
        out_shape=outs,
        compiler_params=params(),
        cost_estimate=cost(1e9, 2e6),
    )(sources, *arrays, *waits)


def pair_state(totals, sources, send, keep, size):
    partner = [(i, i ^ 1) for i in range(size)]
    received = lax.ppermute(send, "seq", partner)
    narrow = jax.ShapeDtypeStruct(send.shape, BF16)
    (pair,) = small_call(pair_kernel, size, (narrow,), sources, totals, keep, received)
    later = []
    for shift in range(1, size // 2):
        moves = [(i, i - 2 * shift) for i in range(2 * shift, size)]
        later.append(lax.ppermute(pair, "seq", moves))
    return received, later


def join_states(totals, sources, keep, received, later, size, waits):
    narrow = jax.ShapeDtypeStruct(keep.shape, BF16)
    wide = jax.ShapeDtypeStruct(keep.shape, F32)
    own, other = small_call(
        join_kernel, size, (wide, narrow), sources, totals, keep, received, *later,
        waits=waits,
    )
    return own, lax.ppermute(other, "seq", [(i, i ^ 1) for i in range(size)])


def leave_kernel(
    count, heads, sources, y_ref, x_ref, grad_y_ref, inner_ref, write, seg_t, last, spread2,
    skip, state, write_part, read_part, own, other,
    input_out, maps_out, decay_out, cot2, state16, from_head, per_head, sums, cot,
):
    step = pl.program_id(0)
    steps = pl.num_programs(0)
    block, width = y_ref.shape
    length = per_head.shape[0]

    @pl.when(step == 0)
    def _():
        parity = lax.rem(sources[count], 2)
        cot[pl.ds(pl.multiple_of(parity * HALF, HALF), HALF), :] = own[...]
        cot[pl.ds(pl.multiple_of((1 - parity) * HALF, HALF), HALF), :] = other[...].astype(F32)
        cot2[0:LANES, :], cot2[LANES:, :] = split2(cot[...])
        state16[...] = state[...].astype(BF16)
        from_head[...] = spread2[0:LANES, :].T
        ended = spread(jnp.exp(last[...]), spread2[...])
        through = jnp.sum(cot[...] * state[...], axis=0, keepdims=True) * ended[0:1, :]
        sums[...] = jnp.where(iota((8, width), 0) == 0, through, 0.0)

    seg_part = seg_t[...]
    decays = jnp.exp(seg_part)
    to_end = spread(jnp.exp(last[0:1, :] - seg_part), spread2[...])
    from_start = spread(decays, spread2[...])
    x = x_ref[...].astype(F32)
    grad_y = grad_y_ref[...]
    write_rows = write[...]
    from_later = to_end * mm(jnp.concatenate([write_rows, write_rows], axis=1), cot2[...])
    core_grad = inner_ref[...] + from_later
    skip_row = skip[0:1, :]
    input_out[...] = (skip_row * grad_y + core_grad).astype(BF16)
    leaving = jnp.sum(x * from_later, axis=0, keepdims=True)
    sums[...] += jnp.where(iota((8, width), 0) == 0, leaving, 0.0)
    terms = grad_y * (y_ref[...] - skip_row * x) - x * core_grad
    high, low = split2(terms)
    start = pl.multiple_of(step * block, block)
    per_head[pl.ds(start, block), :] = mm(high, from_head[...]) + mm(low, from_head[...])
    maps_out[0] = write_part[...] + mm_t((x * to_end).astype(BF16), cot2[0:LANES, :])
    maps_out[1] = read_part[...] + mm_t((grad_y * from_start).astype(BF16), state16[...])

    @pl.when(step == steps - 1)
    def _():
        final = sum(mm(part, from_head[...]) for part in split3(sums[...]))
        upper = (iota((length, length), 0) <= iota((length, length), 1)).astype(BF16)
        tail = sum(mm(upper, part) for part in split3(per_head[...]))
        decay_out[...] = (tail + final[0:1, :]).T[0:heads, :]


def leave(
    heads, sources, y, x, grad_y, inner, write, seg_t, spread2, skip, state,
    write_part, read_part, own, other, waits,
):
    length, width = y.shape
    count = sources.shape[0] - 1
    block = LANES
    token = pl.BlockSpec((block, width), lambda i, *_: (i, 0))
    narrow = pl.BlockSpec((block, LANES), lambda i, *_: (i, 0))
    shapes = (
        jax.ShapeDtypeStruct((length, width), BF16),
        jax.ShapeDtypeStruct((2, length, LANES), F32),
        jax.ShapeDtypeStruct((heads, length), F32),
    )
    last = jnp.broadcast_to(seg_t[length - 1 :, :], (8, LANES))
    return pl.pallas_call(
        skipping(functools.partial(leave_kernel, count, heads), 15, len(waits)),
        name="leave",
        grid_spec=pltpu.PrefetchScalarGridSpec(
            num_scalar_prefetch=1,
            grid=(length // block,),
            in_specs=[
                token, token, token, token, narrow, narrow, whole((8, LANES)),
                whole(spread2.shape), whole((8, width)), whole((LANES, width)),
                narrow, narrow, whole(own.shape), whole(other.shape),
            ] + [WAIT] * len(waits),
            out_specs=[
                token,
                pl.BlockSpec((2, block, LANES), lambda i, *_: (0, i, 0)),
                whole((heads, length)),
            ],
            scratch_shapes=[
                pltpu.VMEM((2 * LANES, width), BF16),
                pltpu.VMEM((LANES, width), BF16),
                pltpu.VMEM((width, LANES), BF16),
                pltpu.VMEM((length, LANES), F32),
                pltpu.VMEM((8, width), F32),
                pltpu.VMEM((LANES, width), F32),
            ],
        ),
        out_shape=shapes,
        compiler_params=params(),
        cost_estimate=cost(5e9, 20e6),
    )(
        sources, y, x, grad_y, inner, write, seg_t, last, spread2, skip, state,
        write_part, read_part, own, other, *waits,
    )


def product_kernel(masks, group, mine, theirs, cot_mine, cot_theirs, *outs):
    first_rows, second_rows = mine[...], theirs[...]
    for mask, out in zip(masks, outs):
        spot = jnp.bitwise_xor(group[0], mask)
        first = mm_t(cot_mine[spot], first_rows).astype(BF16).astype(F32)
        second = mm_t(cot_theirs[spot], second_rows).astype(BF16).astype(F32)
        out[...] = (first + second).astype(out.dtype)


def products(group, mine, theirs, cot_mine, cot_theirs):
    rows, length = mine.shape
    groups, columns, _ = cot_mine.shape
    masks = list(range(groups - 1, -1, -1))
    block = LANES if rows % LANES == 0 else rows
    side = pl.BlockSpec((block, length), lambda i, *_: (i, 0))
    return pl.pallas_call(
        functools.partial(product_kernel, masks),
        name="product",
        grid_spec=pltpu.PrefetchScalarGridSpec(
            num_scalar_prefetch=1,
            grid=(rows // block,),
            in_specs=[side, side, whole(cot_mine.shape), whole(cot_theirs.shape)],
            out_specs=[pl.BlockSpec((columns, block), lambda i, *_: (0, i))] * groups,
        ),
        out_shape=[
            jax.ShapeDtypeStruct((columns, rows), BF16 if mask else F32) for mask in masks
        ],
        compiler_params=params(),
        cost_estimate=cost(4.0 * rows * length * columns * groups, 5e6),
    )(group, mine, theirs, cot_mine, cot_theirs)


def finish_kernel(count, own, *rest):
    total = own[...]
    for k in range(count):
        total = total + rest[k][...].astype(F32)
    rest[-1][...] = total


def finish(part, parts, own, received, held):
    columns, rows = own.shape
    if rows % LANES:
        total = own + sum(piece.astype(F32) for piece in received)
        return total if held is None else jnp.concatenate([held, total], axis=1)
    small = pl.BlockSpec((columns, rows), lambda i: (0, 0))
    operands = [own, *received]
    specs = [small] * len(operands)
    aliases = {}
    if held is not None:
        aliases = {len(operands): 0}
        operands.append(held)
        specs = specs + [WAIT]
    return pl.pallas_call(
        functools.partial(finish_kernel, len(received)),
        name="finish",
        grid=(1,),
        in_specs=specs,
        out_specs=pl.BlockSpec((columns, rows), lambda i: (0, part)),
        out_shape=jax.ShapeDtypeStruct((columns, parts * rows), F32),
        input_output_aliases=aliases,
        compiler_params=params(),
        cost_estimate=cost(1e9, 4e6),
    )(*operands)


def ring_gather(near, far, size):
    half = size // 2
    order = [2 * q for q in range(half)] + [2 * (size - 1 - q) + 1 for q in range(half, size)]
    ahead = [(order[i], order[(i + 1) % size]) for i in range(size)]
    behind = [(b, a) for a, b in ahead]
    shifts, all_near, all_far = [0], [near], [far]
    up = down = [near, far]
    for hop in range(1, half + 1):
        last = hop == half
        up = [lax.ppermute(v, "seq", ahead) for v in (up[:1] if last else up)]
        down = [lax.ppermute(v, "seq", behind) for v in (down[1:] if last else down)]
        shifts.append(-hop)
        all_near.append(up[0])
        if last:
            all_far.append(down[0])
        else:
            all_far.append(up[1])
            shifts.append(hop)
            all_near.append(down[0])
            all_far.append(down[1])
    return all_near, all_far, shifts


def ring_sources(shifts, size):
    position = lax.axis_index("seq")
    half = size // 2
    place = jnp.where(position % 2 == 0, position // 2, size - 1 - position // 2)
    places = (place + jnp.array(shifts, jnp.int32) + size) % size
    found = jnp.where(places < half, 2 * places, 2 * (size - 1 - places) + 1)
    return jnp.concatenate([found, position[None]]).astype(jnp.int32)


def butterfly_sum(value, axis, size):
    stride = 1
    while stride < size:
        value = value + lax.ppermute(value, axis, [(i, i ^ stride) for i in range(size)])
        stride *= 2
    return value


def all_shards(value, size):
    held = [value]
    masks = [0]
    stride = size // 2
    while stride >= 1:
        moves = [(i, i ^ stride) for i in range(size)]
        held = held + [lax.ppermute(v, "tp", moves) for v in held]
        masks = masks + [m ^ stride for m in masks]
        stride //= 2
    return held, masks


def send_products(pieces, size):
    groups = size // 2
    by_mask = dict(zip(range(groups - 1, -1, -1), pieces))

    def move(value, moves):
        pairs = [(2 * a + p, 2 * b + p) for a, b in moves for p in (0, 1)]
        return lax.ppermute(value, "seq", pairs)

    if groups != 4:
        return [
            move(by_mask[mask], [(g, g ^ mask) for g in range(groups)])
            for mask in range(1, groups)
        ], []
    far = move(by_mask[3], [(0, 1), (3, 2)])
    near = [move(by_mask[3], [(1, 2), (2, 1)]), move(by_mask[1], [(g, g ^ 1) for g in range(4)])]
    merged = (by_mask[2].astype(F32) + far.astype(F32)).astype(BF16)
    return near + [move(merged, [(g, g ^ 2) for g in range(4)])], [merged]


def on_device(
    packed_input, block_exponent, gate_input, state_write, state_read, log_decay,
    skip_weight, norm_gain, out_weight, out_cotangent,
):
    heads, _ = log_decay.shape
    width = packed_input.shape[1]
    seq_size = lax.axis_size("seq")
    tp_size = lax.axis_size("tp")
    total_width = width * tp_size
    columns = out_weight.shape[1] // seq_size
    parity = lax.axis_index("seq") % 2
    partner = [(i, i ^ 1) for i in range(seq_size)]
    gain = norm_gain[None, :]

    x, near, far, seg_t, seg, spread2, skip, read_t = prepare(
        packed_input, block_exponent, log_decay, skip_weight[None, :], state_write, state_read
    )
    near, far, shifts = ring_gather(near, far, seq_size)
    sources = ring_sources(shifts, seq_size)

    other_half = pick(parity[None].astype(jnp.int32), out_cotangent, columns)
    theirs = lax.ppermute(other_half, "seq", partner)
    all_mine, masks = all_shards(out_cotangent, tp_size)
    all_theirs, _ = all_shards(theirs, tp_size)
    owners = jnp.bitwise_xor(lax.axis_index("tp"), jnp.array(masks, jnp.int32))
    owners = jnp.concatenate([owners, parity[None]]).astype(jnp.int32)

    pairs = width // LANES
    calls = min(4, pairs)
    y_local = None
    hops = seq_size // 2
    for call in range(calls):
        start, stop = call * pairs // calls, (call + 1) * pairs // calls
        waits = (*near[1:3], *far[1:3]) if call == 2 and hops > 2 else ()
        y_local = inside(
            heads, start, stop, seg_t, seg, state_write, state_read, x, skip, y_local, waits
        )
    waits = (y_local, *near[3:5], *far[3:5]) if hops > 2 else (y_local,)
    grad_v, cot_mine, cot_theirs = cotangent(
        owners, out_weight, all_mine, all_theirs, columns, waits
    )

    y, scaled_t, stats, state, totals = enter(
        sources, y_local, gate_input, grad_v, gain, state_read, seg_t, spread2, near, far
    )
    stats = butterfly_sum(stats, "tp", tp_size)
    scale = lax.rsqrt(stats[0:1, :] / total_width + EPSILON)
    part_rows = width // NORMED_PARTS
    normed, normed_theirs = [], []
    for part in range(NORMED_PARTS):
        rows = scaled_t[part * part_rows : (part + 1) * part_rows]
        normed.append((rows * scale).astype(BF16))
        normed_theirs.append(lax.ppermute(normed[part], "seq", partner))

    grad_gate, grad_y, send, keep, sums = gate_grads(
        total_width, sources, y, gate_input, grad_v, gain, stats, x, seg_t, spread2, read_t
    )
    received, later = pair_state(totals, sources, send, keep, seq_size)
    middle = pairs // 2
    operands = (seg_t, seg, state_write, state_read, x, grad_y)
    inner, grad_cross = inside_back(heads, 0, middle, *operands)
    inner, write_part, read_part = inside_back(heads, middle, pairs, *operands, inner, grad_cross)
    group = (lax.axis_index("seq") // 2)[None].astype(jnp.int32)
    arrived, own_part, merges = [], [], []
    for part in range(NORMED_PARTS):
        *pieces, last = products(group, normed[part], normed_theirs[part], cot_mine, cot_theirs)
        got, merged = send_products(pieces, seq_size)
        arrived.append(got)
        own_part.append(last)
        merges.append(merged)
    own, other = join_states(
        totals, sources, keep, received, later, seq_size, (write_part, *merges[0])
    )
    grad_input, maps, grad_decay = leave(
        heads, sources, y, x, grad_y, inner, state_write, seg_t, spread2, skip, state,
        write_part, read_part, own, other, tuple(merges[-1]),
    )
    grad_out_weight = None
    for part in range(NORMED_PARTS):
        grad_out_weight = finish(part, NORMED_PARTS, own_part[part], arrived[part], grad_out_weight)
    maps = butterfly_sum(maps, "tp", tp_size)
    sums = butterfly_sum(sums, "seq", seq_size)
    grad_skip = jnp.sum(sums[1].reshape(heads, width // heads), axis=1)
    return (
        grad_input, grad_gate, maps[0], maps[1], grad_decay, grad_skip, sums[0], grad_out_weight.T,
    )


def solution(mesh):
    placed = (
        P("seq", "tp"), P("tp", "seq"), P("seq", "tp"), P("seq", None), P("seq", None),
        P("tp", "seq"), P("tp"), P("tp"), P("tp", None), P("seq", "tp"),
    )
    return jax.shard_map(
        on_device,
        mesh=mesh,
        in_specs=placed,
        out_specs=(
            P("seq", "tp"), P("seq", "tp"), P("seq", None), P("seq", None), P("tp", "seq"),
            P("tp"), P("tp"), P("tp", "seq"),
        ),
        check_vma=False,
    )
```

time: 228 us -> 226 us (level)
  starting transfers between devices: 32.3 us -> 50.7 us
  waiting for transfers between devices: 91.9 us -> 77.6 us
  other arithmetic: 15.5 us -> 3.53 us
  Pallas kernels: 58.2 us -> 66.4 us
  matrix products: 5.18 us -> 0 us
  local copies, waits for them, and re-layouts: 22.8 us -> 26 us
    ppermute x29 -> x41, starting transfers between devices: 29.7 us -> 48.5 us  [the longest x7 12.3 us: ring_gather(): up = [lax.ppermute(v, 'seq', ahead) for v in (up[:1] if last else up)]]
    pallas_call x11 -> x15, Pallas kernels: 40.3 us -> 51.4 us  [the longest x4 10.9 us: inside(): pl.pallas_call(functools.partial(inside_kernel, width // heads, start), n...]
    another operation x7 -> x0, other arithmetic: 7.6 us -> none  [gather_columns(): held = jnp.stack([jnp.where(low, held, other), jnp.where(low, other, held)])]
    ppermute x29 -> x41, waiting for transfers between devices: 81.7 us -> 74.4 us  [the longest x7 24.2 us: butterfly_sum(): lax.ppermute(value, axis, [(i, i ^ stride) for i in range(size)])]
    ppermute x2, waiting for transfers between devices: 10.2 us -> 3.2 us  [on_device(): normed_theirs.append(lax.ppermute(normed[part], 'seq', partner))]
    unnamed x93 -> x84, local copies, waits for them, and re-layouts: 17.5 us -> 24.5 us
    dot_general x1 -> x0, matrix products: 5.18 us -> none  [on_device(): lax.dot_general(cot_full, out_weight, (((1,), (1,)), ((), ())), preferred...]
    slice x3 -> x1, local copies, waits for them, and re-layouts: 3.2 us -> 0.62 us  [on_device(): sums[0]]
  transfers between devices with their start and end apart: 31 -> 43, of which waited for: 13 -> 17; matrix products, arithmetic and copies ran while one was open for 14% -> 1% of each run, Pallas kernels for 22% -> 22%
where the time goes in v2:
time: 226 us; the launch traced here: 225 us
  waiting for transfers between devices  77.6 us (34%)
  Pallas kernels  66.4 us (29%)
  starting transfers between devices  50.7 us (22%)
  local copies, waits for them, and re-layouts  26 us (12%)
  other arithmetic  3.53 us (2%)
    unnamed x84, local copies, waits for them, and re-layouts  24.5 us
    ppermute x7, waiting for transfers between devices, butterfly_sum(): lax.ppermute(value, axis, [(i, i ^ stride) for i in range(size)])  24.2 us
    ppermute x8, waiting for transfers between devices, move(): return lax.ppermute(value, 'seq', pairs)  18.2 us
    ppermute x3, waiting for transfers between devices, pair_state(): later.append(lax.ppermute(pair, 'seq', moves))  14.5 us
    ppermute x7, starting transfers between devices, ring_gather(): up = [lax.ppermute(v, 'seq', ahead) for v in (up[:1] if last else up)]  12.3 us
    ppermute x8, starting transfers between devices, move(): return lax.ppermute(value, 'seq', pairs)  12.1 us
    pallas_call x4, Pallas kernels, inside(): pl.pallas_call(functools.partial(inside_kernel, width // heads, start), n...  10.9 us
    pallas_call x2, Pallas kernels, inside_back(): pl.pallas_call(functools.partial(inside_back_kernel, width // heads, star...  10.5 us
  transfers between devices with their start and end apart: 43, of which 17 were waited for; matrix products, arithmetic and copies ran while one was open for 1% of the time, Pallas kernels for 22%

profile of v2, /device:TPU:0, one launch (start us, length us, event | category | flops | bytes accessed | tf_op | source)
XLA Modules:
  0.0 225.4 jit_solution(8539482638887849633)
XLA Ops:
  0.6 1.0 copy-done.7
  5.6 3.2 %prepare.1 = (bf16[512,1280]{1,0:T(8,128)(2,1)S(1)}, bf16[80,1280]{1,0:T(8,128)(2,1)S(1)}, bf16[64,1280]{1,0:T(8,128)(2,1)}, f32[512,128]{1,0:T(8,128)S(1)}, f32...) custom-call(s32[64,1280]{1,0:T(8,128)S(1)} %copy-done.7, ...), custom_call_target="tpu_custom_call" | custom-call | flops 3000000000 | bytes 8000000 | tf_op jit(solution)/shard_map/prepare/pallas_call | solution.py:119
  10.4 1.1 copy-done.27
  12.8 3.1 %collective-permute-start = (bf16[80,1280]{1,0:T(8,128)(2,1)S(1)}, bf16[80,1280]{1,0:T(8,128)(2,1)}, u32[]{:S(2)}, u32[]{:S(2)}) collective-permute-start(bf16[80,1280]{1,0:T(8,128)(2,1)S(1)} %get-tuple-element.51.rest_0_), channel_id=1, source_target_pairs={{0,8},{8,16},{16,24},{24,28},{28,20},{20,12},{12,4},{4,0},{1,9},{9... | collective-permute-start | bytes 614408 | tf_op jit(solution)/shard_map/ppermute | solution.py:786
  15.9 2.0 collective-permute-start.2
  17.9 2.0 collective-permute-start.4
  22.6 1.3 copy-done.28
  23.9 0.9 copy-done.34
  24.9 2.2 inside.4.rest_0_
  27.2 3.2 %inside.5.rest_0_ = f32[512,1280]{1,0:T(8,128)S(1)} custom-call(f32[512,128]{1,0:T(8,128)S(1)} %copy-done.20, f32[128,512]{1,0:T(8,128)S(1)} %copy-done.34, bf16[512,128]{1,0:T(8,128)(2,1)S(1)} %copy-done.13, bf16[512,128]{1,0:T(8,128)(2,1)S(1)} %copy-done.9, bf16[512,1280]{1,0:T(8,128)(2,1)S(1)} %copy-done.28, ...), custom_call_target="tpu_custom_call", output_to_operand_aliasing={{}: (6, {})} | custom-call | flops 6000000000 | bytes 1500000 | tf_op jit(solution)/shard_map/inside/pallas_call | solution.py:269
  31.5 1.6 collective-permute-start.7
  33.1 1.6 collective-permute-start.13
  35.2 1.6 collective-permute-start.11
  36.9 6.9 %collective-permute-done.7.refs_6_ = bf16[512,320]{1,0:T(8,128)(2,1)S(1)} collective-permute-done((bf16[512,320]{1,0:T(8,128)(2,1)}, bf16[512,320]{1,0:T(8,128)(2,1)S(1)}, u32[]{:S(2)}, u32[]{:S(2)}) %collective-permute-start.7) | collective-permute-done | bytes 327712 | tf_op jit(solution)/shard_map/ppermute | solution.py:869
  43.8 3.2 %collective-permute-done.13.refs_13_.rest_11_ = bf16[64,1280]{1,0:T(8,128)(2,1)S(1)} collective-permute-done((bf16[64,1280]{1,0:T(8,128)(2,1)}, bf16[64,1280]{1,0:T(8,128)(2,1)S(1)}, u32[]{:S(2)}, u32[]{:S(2)}) %collective-permute-start.13) | collective-permute-done | bytes 163872 | tf_op jit(solution)/shard_map/ppermute | solution.py:786
  47.3 1.8 collective-permute-done.11.refs_11_.rest_3_
  51.0 0.9 copy-done.21
  51.9 1.3 copy-done.29
  54.2 2.3 %inside.6.rest_0_ = f32[512,1280]{1,0:T(8,128)S(1)} custom-call(f32[512,128]{1,0:T(8,128)S(1)} %copy-done.21, f32[128,512]{1,0:T(8,128)S(1)} %copy-done.35, bf16[512,128]{1,0:T(8,128)(2,1)S(1)} %copy-done.14, bf16[512,128]{1,0:T(8,128)(2,1)S(1)} %copy-done.10, bf16[512,1280]{1,0:T(8,128)(2,1)S(1)} %copy-done.29, ...), custom_call_target="tpu_custom_call", output_to_operand_aliasing={{}: (6, {})} | custom-call | flops 4000000000 | bytes 1000000 | tf_op jit(solution)/shard_map/inside/pallas_call | solution.py:269
  57.1 2.0 collective-permute-start.15
  59.1 3.2 %inside.7.refs_10_.y_local = f32[512,1280]{1,0:T(8,128)S(1)} custom-call(f32[512,128]{1,0:T(8,128)S(1)} %copy-done.22, f32[128,512]{1,0:T(8,128)S(1)} %copy-done.36, bf16[512,128]{1,0:T(8,128)(2,1)S(1)} %copy-done.15, bf16[512,128]{1,0:T(8,128)(2,1)S(1)} %copy-done.11, bf16[512,1280]{1,0:T(8,128)(2,1)S(1)} %copy-done.30, ...), custom_call_target="tpu_custom_call", output_to_operand_aliasing={{}: (6, {})} | custom-call | flops 6000000000 | bytes 1500000 | tf_op jit(solution)/shard_map/inside/pallas_call | solution.py:269
  62.4 1.7 collective-permute-done.15.rest_5_
  64.1 2.0 collective-permute-start.18
  66.9 2.0 collective-permute-start.20
  69.0 8.5 %cotangent.1 = (f32[512,1280]{1,0:T(8,128)S(1)}, bf16[4,320,512]{2,1,0:T(8,128)(2,1)S(1)}, bf16[4,320,512]{2,1,0:T(8,128)(2,1)S(1)}) custom-call(s32[5]{0:T(128)S(1)} %pad_add_fusion.1.refs_0_, bf16[1280,2560]{1,0:T(8,128)(2,1)S(1)} %bitcast.13, bf16[512,640]{1,0:T(8,128)(2,1)S(1)} %copy-done, bf16[512,640]{1,0:T(8,128)(2,1)} %collective-permute-done.4.refs_3_, ...), custom_call_target="tpu_custom_call" | custom-call | flops 3355443200 | bytes 20000000 | tf_op jit(solution)/shard_map/cotangent/pallas_call | solution.py:185
  77.6 6.2 %enter.1 = (f32[512,1280]{1,0:T(8,128)S(1)}, f32[1280,512]{1,0:T(8,128)S(1)}, f32[8,512]{1,0:T(8,128)S(1)}, f32[128,1280]{1,0:T(8,128)S(1)}, f32[8,1280]{1,0:T(8,128)S(1)}) custom-call(s32[9]{0:T(128)S(1)} %pad_add_fusion.sources.refs_0_, f32[512,1280]{1,0:T(8,128)S(1)} %inside.7.refs_10_.y_local, bf16[512,1280]{1,0:T(8,128)(2,1)S(1)} %copy-done.2, ...), custom_call_target="tpu_custom_call" | custom-call | flops 3000000000 | bytes 15000000 | tf_op jit(solution)/shard_map/enter/pallas_call | solution.py:350
  83.9 1.2 collective-permute-done.21
  85.0 1.5 collective-permute-start.22
  86.5 2.3 %collective-permute-done.22 = f32[8,512]{1,0:T(8,128)S(1)} collective-permute-done((f32[8,512]{1,0:T(8,128)S(1)}, f32[8,512]{1,0:T(8,128)S(1)}, u32[]{:S(2)}, u32[]{:S(2)}) %collective-permute-start.22) | collective-permute-done | bytes 16416 | tf_op jit(solution)/shard_map/ppermute | solution.py:812
  89.2 2.0 collective-permute-start.27
  91.3 5.6 %gate_grads.1 = (bf16[512,1280]{1,0:T(8,128)(2,1)}, f32[512,1280]{1,0:T(8,128)S(1)}, bf16[64,1280]{1,0:T(8,128)(2,1)S(1)}, f32[64,1280]{1,0:T(8,128)S(1)}, f32[8,1280]{1,0:T(8,128)S(1)}) custom-call(s32[9]{0:T(128)S(1)} %pad_add_fusion.sources.refs_0_, f32[512,1280]{1,0:T(8,128)S(1)} %get-tuple-element.55.y_ref.refs_1_, bf16[512,1280]{1,0:T(8,128)(2,1)S(1)} %copy-done.2, ...), custom_call_target="tpu_custom_call" | custom-call | flops 3000000000 | bytes 15000000 | tf_op jit(solution)/shard_map/gate_grads/pallas_call | solution.py:431
  96.9 2.0 collective-permute-start.23
  98.9 4.9 %inside_back.2 = (f32[512,1280]{1,0:T(8,128)S(1)}, f32[512,512]{1,0:T(8,128)S(1)}) custom-call(f32[512,128]{1,0:T(8,128)S(1)} %copy-done.22, f32[128,512]{1,0:T(8,128)S(1)} %copy-done.36, bf16[512,128]{1,0:T(8,128)(2,1)S(1)} %copy-done.15, bf16[512,128]{1,0:T(8,128)(2,1)S(1)} %copy-done.11, bf16[512,1280]{1,0:T(8,128)(2,1)S(1)} %copy-done.30, ...), custom_call_target="tpu_custom_call" | custom-call | flops 10000000000 | bytes 4000000 | tf_op jit(solution)/shard_map/inside_back/pallas_call | solution.py:527
  103.8 3.0 %collective-permute-done.27.theirs = bf16[640,512]{1,0:T(8,128)(2,1)S(1)} collective-permute-done((bf16[640,512]{1,0:T(8,128)(2,1)S(1)}, bf16[640,512]{1,0:T(8,128)(2,1)S(1)}, u32[]{:S(2)}, u32[]{:S(2)}) %collective-permute-start.27) | collective-permute-done | bytes 655392 | tf_op jit(solution)/shard_map/ppermute | solution.py:900
  106.8 4.5 %product.2 = (bf16[320,640]{1,0:T(8,128)(2,1)S(1)}, bf16[320,640]{1,0:T(8,128)(2,1)S(1)}, bf16[320,640]{1,0:T(8,128)(2,1)S(1)}, f32[320,640]{1,0:T(8,128)S(1)}) custom-call(s32[1]{0:T(128)} %bitcast.4.group, bf16[640,512]{1,0:T(8,128)(2,1)S(1)} %get-tuple-element.89.mine, bf16[640,512]{1,0:T(8,128)(2,1)S(1)} %collective-permute-done.27.theirs, ...), custom_call_target="tpu_custom_call" | custom-call | flops 1677721600 | bytes 5000000 | tf_op jit(solution)/shard_map/product/pallas_call | solution.py:727
  111.4 3.7 %collective-permute-start.28 = (bf16[320,640]{1,0:T(8,128)(2,1)S(1)}, bf16[320,640]{1,0:T(8,128)(2,1)S(1)}, u32[]{:S(2)}, u32[]{:S(2)}) collective-permute-start(bf16[320,640]{1,0:T(8,128)(2,1)S(1)} %get-tuple-element.72), channel_id=1, source_target_pairs={{0,8},{4,12},{24,16},{28,20},{1,9},{5,13},{25,17},{29,21},{2,10},{... | collective-permute-start | bytes 1228808 | tf_op jit(solution)/shard_map/ppermute | solution.py:835
  115.1 5.6 %inside_back.3 = (f32[512,1280]{1,0:T(8,128)S(1)}, f32[512,128]{1,0:T(8,128)S(1)}, f32[512,128]{1,0:T(8,128)S(1)}) custom-call(f32[512,128]{1,0:T(8,128)S(1)} %copy-done.22, f32[128,512]{1,0:T(8,128)S(1)} %copy-done.36, bf16[512,128]{1,0:T(8,128)(2,1)S(1)} %copy-done.15, bf16[512,128]{1,0:T(8,128)(2,1)S(1)} %copy-done.11, ...), custom_call_target="tpu_custom_call", output_to_operand_aliasing={{0}: (6, {})} | custom-call | flops 10000000000 | bytes 4000000 | tf_op jit(solution)/shard_map/inside_back/pallas_call | solution.py:527
  120.9 4.9 %product.3 = (bf16[320,640]{1,0:T(8,128)(2,1)}, bf16[320,640]{1,0:T(8,128)(2,1)S(1)}, bf16[320,640]{1,0:T(8,128)(2,1)S(1)}, f32[320,640]{1,0:T(8,128)S(1)}) custom-call(s32[1]{0:T(128)} %bitcast.4.group, bf16[640,512]{1,0:T(8,128)(2,1)S(1)} %get-tuple-element.88.mine, bf16[640,512]{1,0:T(8,128)(2,1)S(1)} %collective-permute-done.30.theirs, ...), custom_call_target="tpu_custom_call" | custom-call | flops 1677721600 | bytes 5000000 | tf_op jit(solution)/shard_map/product/pallas_call | solution.py:727
  125.8 3.6 %collective-permute-start.31 = (bf16[320,640]{1,0:T(8,128)(2,1)}, bf16[320,640]{1,0:T(8,128)(2,1)S(1)}, u32[]{:S(2)}, u32[]{:S(2)}) collective-permute-start(bf16[320,640]{1,0:T(8,128)(2,1)} %get-tuple-element.76), channel_id=1, source_target_pairs={{0,8},{4,12},{24,16},{28,20},{1,9},{5,13},{25,17},{29,21},{2,10},{... | collective-permute-start | bytes 1228808 | tf_op jit(solution)/shard_map/ppermute | solution.py:835
  130.1 1.3 collective-permute-start.24
  131.4 1.3 collective-permute-start.25
  132.7 1.5 collective-permute-start.26
  134.3 3.0 %collective-permute-done.24.refs_4_ = bf16[64,1280]{1,0:T(8,128)(2,1)S(1)} collective-permute-done((bf16[64,1280]{1,0:T(8,128)(2,1)S(1)}, bf16[64,1280]{1,0:T(8,128)(2,1)S(1)}, u32[]{:S(2)}, u32[]{:S(2)}) %collective-permute-start.24) | collective-permute-done | bytes 163872 | tf_op jit(solution)/shard_map/ppermute | solution.py:599
  137.4 3.9 %collective-permute-done.25.refs_5_ = bf16[64,1280]{1,0:T(8,128)(2,1)S(1)} collective-permute-done((bf16[64,1280]{1,0:T(8,128)(2,1)S(1)}, bf16[64,1280]{1,0:T(8,128)(2,1)S(1)}, u32[]{:S(2)}, u32[]{:S(2)}) %collective-permute-start.25) | collective-permute-done | bytes 163872 | tf_op jit(solution)/shard_map/ppermute | solution.py:599
  141.3 7.6 %collective-permute-done.26.refs_6_ = bf16[64,1280]{1,0:T(8,128)(2,1)S(1)} collective-permute-done((bf16[64,1280]{1,0:T(8,128)(2,1)S(1)}, bf16[64,1280]{1,0:T(8,128)(2,1)S(1)}, u32[]{:S(2)}, u32[]{:S(2)}) %collective-permute-start.26) | collective-permute-done | bytes 163872 | tf_op jit(solution)/shard_map/ppermute | solution.py:599
  149.6 1.5 collective-permute-start.29
  151.2 3.7 %collective-permute-done.29.refs_14_ = bf16[64,1280]{1,0:T(8,128)(2,1)S(1)} collective-permute-done((bf16[64,1280]{1,0:T(8,128)(2,1)S(1)}, bf16[64,1280]{1,0:T(8,128)(2,1)S(1)}, u32[]{:S(2)}, u32[]{:S(2)}) %collective-permute-start.29) | collective-permute-done | bytes 163872 | tf_op jit(solution)/shard_map/ppermute | solution.py:610
  155.0 7.1 %leave.1 = (bf16[512,1280]{1,0:T(8,128)(2,1)}, f32[2,512,128]{2,1,0:T(8,128)S(1)}, f32[20,512]{1,0:T(8,128)}) custom-call(s32[9]{0:T(128)S(1)} %pad_add_fusion.sources.refs_0_, f32[512,1280]{1,0:T(8,128)S(1)} %get-tuple-element.55.y_ref.refs_1_, bf16[512,1280]{1,0:T(8,128)(2,1)S(1)} %copy-done.30, f32[512,1280]{1,0:T(8,128)S(1)} %get-tuple-element.58.grad_y.refs_3_, ...), custom_call_target="tpu_custom_call" | custom-call | flops 5000000000 | bytes 20000000 | tf_op jit(solution)/shard_map/leave/pallas_call | solution.py:678
  162.9 1.5 collective-permute-start.34
  164.4 1.5 collective-permute-start.42
  165.9 1.0 collective-permute-done.34
  166.9 1.9 collective-permute-start.35
  168.9 13.3 %collective-permute-done.35 = f32[8,1280]{1,0:T(8,128)S(1)} collective-permute-done((f32[8,1280]{1,0:T(8,128)S(1)}, f32[8,1280]{1,0:T(8,128)S(1)}, u32[]{:S(2)}, u32[]{:S(2)}) %collective-permute-start.35) | collective-permute-done | bytes 40992 | tf_op jit(solution)/shard_map/ppermute | solution.py:812
  182.2 3.4 %collective-permute-start.36 = (f32[8,1280]{1,0:T(8,128)S(1)}, f32[8,1280]{1,0:T(8,128)S(1)}, u32[]{:S(2)}, u32[]{:S(2)}) collective-permute-start(f32[8,1280]{1,0:T(8,128)S(1)} %add.72), channel_id=1, source_target_pairs={{0,16},{4,20},{8,24},{12,28},{16,0},{20,4},{24,8},{28,12},{1,17},{... | collective-permute-start | bytes 122888 | tf_op jit(solution)/shard_map/ppermute | solution.py:812
  187.0 6.4 %collective-permute-done.36 = f32[8,1280]{1,0:T(8,128)S(1)} collective-permute-done((f32[8,1280]{1,0:T(8,128)S(1)}, f32[8,1280]{1,0:T(8,128)S(1)}, u32[]{:S(2)}, u32[]{:S(2)}) %collective-permute-start.36) | collective-permute-done | bytes 40992 | tf_op jit(solution)/shard_map/ppermute | solution.py:812
  194.9 1.3 collective-permute-start.38
  198.8 1.0 copy-done.4
  199.8 1.0 copy-done.6
  200.8 1.1 copy-done.24
  201.9 2.1 finish.2.rest_3_
  204.0 3.8 %collective-permute-done.38.rest_1_ = bf16[320,640]{1,0:T(8,128)(2,1)S(1)} collective-permute-done((bf16[320,640]{1,0:T(8,128)(2,1)S(1)}, bf16[320,640]{1,0:T(8,128)(2,1)S(1)}, u32[]{:S(2)}, u32[]{:S(2)}) %collective-permute-start.38) | collective-permute-done | bytes 409632 | tf_op jit(solution)/shard_map/ppermute | solution.py:835
  207.8 14.5 %collective-permute-done.39.rest_2_ = bf16[320,640]{1,0:T(8,128)(2,1)S(1)} collective-permute-done((bf16[320,640]{1,0:T(8,128)(2,1)S(1)}, bf16[320,640]{1,0:T(8,128)(2,1)S(1)}, u32[]{:S(2)}, u32[]{:S(2)}) %collective-permute-start.39) | collective-permute-done | bytes 409632 | tf_op jit(solution)/shard_map/ppermute | solution.py:835
  222.2 1.1 finish.3
  223.3 1.3 add.70
  (147 shorter events, 25.3 us)
Async XLA Ops:
  5.6 12.3 %copy-start = (bf16[512,640]{1,0:T(8,128)(2,1)S(1)}, bf16[512,640]{1,0:T(8,128)(2,1)}, u32[]{:S(2)}) copy-start(bf16[512,640]{1,0:T(8,128)(2,1)} %refs_2_.1) | copy-start | bytes 1966084
  10.4 1.1 copy-start.27
  12.8 21.9 %collective-permute-start = (bf16[80,1280]{1,0:T(8,128)(2,1)S(1)}, bf16[80,1280]{1,0:T(8,128)(2,1)}, u32[]{:S(2)}, u32[]{:S(2)}) collective-permute-start(bf16[80,1280]{1,0:T(8,128)(2,1)S(1)} %get-tuple-element.51.rest_0_), channel_id=1, source_target_pairs={{0,8},{8,16},{16,24},{24,28},{28,20},{20,12},{12,4},{4,0},{1,9},{9... | collective-permute-start | bytes 614408 | tf_op jit(solution)/shard_map/ppermute | solution.py:786
  15.9 19.3 %collective-permute-start.1 = (bf16[80,1280]{1,0:T(8,128)(2,1)S(1)}, bf16[80,1280]{1,0:T(8,128)(2,1)}, u32[]{:S(2)}, u32[]{:S(2)}) collective-permute-start(bf16[80,1280]{1,0:T(8,128)(2,1)S(1)} %get-tuple-element.51.rest_0_), channel_id=1, source_target_pairs={{8,0},{16,8},{24,16},{28,24},{20,28},{12,20},{4,12},{0,4},{9,1},{1... | collective-permute-start | bytes 614408 | tf_op jit(solution)/shard_map/ppermute | solution.py:787
  15.9 15.6 %collective-permute-start.2 = (bf16[64,1280]{1,0:T(8,128)(2,1)}, bf16[64,1280]{1,0:T(8,128)(2,1)}, u32[]{:S(2)}, u32[]{:S(2)}) collective-permute-start(bf16[64,1280]{1,0:T(8,128)(2,1)} %get-tuple-element.52.rest_8_), channel_id=1, source_target_pairs={{0,8},{8,16},{16,24},{24,28},{28,20},{20,12},{12,4},{4,0},{1,9},{9... | collective-permute-start | bytes 491528 | tf_op jit(solution)/shard_map/ppermute | solution.py:786
  17.9 15.2 %collective-permute-start.3 = (bf16[64,1280]{1,0:T(8,128)(2,1)}, bf16[64,1280]{1,0:T(8,128)(2,1)}, u32[]{:S(2)}, u32[]{:S(2)}) collective-permute-start(bf16[64,1280]{1,0:T(8,128)(2,1)} %get-tuple-element.52.rest_8_), channel_id=1, source_target_pairs={{8,0},{16,8},{24,16},{28,24},{20,28},{12,20},{4,12},{0,4},{9,1},{1... | collective-permute-start | bytes 491528 | tf_op jit(solution)/shard_map/ppermute | solution.py:787
  17.9 31.2 %collective-permute-start.4 = (bf16[512,640]{1,0:T(8,128)(2,1)S(1)}, bf16[512,640]{1,0:T(8,128)(2,1)}, u32[]{:S(2)}, u32[]{:S(2)}) collective-permute-start(bf16[512,640]{1,0:T(8,128)(2,1)S(1)} %copy-done), channel_id=1, source_target_pairs={{0,2},{1,3},{2,0},{3,1},{4,6},{5,7},{6,4},{7,5},{8,10},{9,11},{10,... | collective-permute-start | bytes 1966088 | tf_op jit(solution)/shard_map/ppermute | solution.py:823
  22.6 1.3 copy-start.28
  27.1 4.4 %copy-start.39 = (s32[4]{0:T(128)S(1)}, s32[4]{0:T(128)}, u32[]{:S(2)}) copy-start(s32[4]{0:T(128)} %constant.73.clone) | copy-start | bytes 52
  27.1 5.9 %copy-start.38 = (s32[8]{0:T(128)S(1)}, s32[8]{0:T(128)}, u32[]{:S(2)}) copy-start(s32[8]{0:T(128)} %constant.72.clone) | copy-start | bytes 100
  27.2 9.7 %copy-start.37 = (f32[1280]{0:T(1024)S(1)}, f32[1280]{0:T(1024)}, u32[]{:S(2)}) copy-start(f32[1280]{0:T(1024)} %param.19) | copy-start | bytes 15364
  31.5 12.3 %collective-permute-start.7 = (bf16[512,320]{1,0:T(8,128)(2,1)}, bf16[512,320]{1,0:T(8,128)(2,1)S(1)}, u32[]{:S(2)}, u32[]{:S(2)}) collective-permute-start(bf16[512,320]{1,0:T(8,128)(2,1)} %copy-done.1), channel_id=1, source_target_pairs={{0,4},{4,0},{8,12},{12,8},{16,20},{20,16},{24,28},{28,24},{1,5},{5... | collective-permute-start | bytes 983048 | tf_op jit(solution)/shard_map/ppermute | solution.py:869
  33.1 13.9 %collective-permute-start.13 = (bf16[64,1280]{1,0:T(8,128)(2,1)}, bf16[64,1280]{1,0:T(8,128)(2,1)S(1)}, u32[]{:S(2)}, u32[]{:S(2)}) collective-permute-start(bf16[64,1280]{1,0:T(8,128)(2,1)} %collective-permute-done.2.rest_3_.rest_9_), channel_id=1, source_target_pairs={{0,8},{8,16},{16,24},{24,28},{28,20},{20,12},{12,4},{4,0},{1,9},{9... | collective-permute-start | bytes 491528 | tf_op jit(solution)/shard_map/ppermute | solution.py:786
  34.7 12.2 %collective-permute-start.14 = (bf16[64,1280]{1,0:T(8,128)(2,1)}, bf16[64,1280]{1,0:T(8,128)(2,1)S(1)}, u32[]{:S(2)}, u32[]{:S(2)}) collective-permute-start(bf16[64,1280]{1,0:T(8,128)(2,1)} %collective-permute-done.3.rest_4_.rest_10_), channel_id=1, source_target_pairs={{8,0},{16,8},{24,16},{28,24},{20,28},{12,20},{4,12},{0,4},{9,1},{1... | collective-permute-start | bytes 491528 | tf_op jit(solution)/shard_map/ppermute | solution.py:787
  35.2 14.0 %collective-permute-start.11 = (bf16[80,1280]{1,0:T(8,128)(2,1)}, bf16[80,1280]{1,0:T(8,128)(2,1)S(1)}, u32[]{:S(2)}, u32[]{:S(2)}) collective-permute-start(bf16[80,1280]{1,0:T(8,128)(2,1)} %collective-permute-done.rest_1_), channel_id=1, source_target_pairs={{0,8},{8,16},{16,24},{24,28},{28,20},{20,12},{12,4},{4,0},{1,9},{9... | collective-permute-start | bytes 614408 | tf_op jit(solution)/shard_map/ppermute | solution.py:786
  43.8 23.2 %collective-permute-start.5 = (bf16[512,640]{1,0:T(8,128)(2,1)S(1)}, bf16[512,640]{1,0:T(8,128)(2,1)S(1)}, u32[]{:S(2)}, u32[]{:S(2)}) collective-permute-start(bf16[512,640]{1,0:T(8,128)(2,1)S(1)} %copy-done), channel_id=1, source_target_pairs={{0,1},{1,0},{2,3},{3,2},{4,5},{5,4},{6,7},{7,6},{8,9},{9,8},{10,11... | collective-permute-start | bytes 1966088 | tf_op jit(solution)/shard_map/ppermute | solution.py:823
  46.9 9.6 %collective-permute-start.12 = (bf16[80,1280]{1,0:T(8,128)(2,1)}, bf16[80,1280]{1,0:T(8,128)(2,1)S(1)}, u32[]{:S(2)}, u32[]{:S(2)}) collective-permute-start(bf16[80,1280]{1,0:T(8,128)(2,1)} %collective-permute-done.1.rest_2_), channel_id=1, source_target_pairs={{8,0},{16,8},{24,16},{28,24},{20,28},{12,20},{4,12},{0,4},{9,1},{1... | collective-permute-start | bytes 614408 | tf_op jit(solution)/shard_map/ppermute | solution.py:787
  46.9 12.1 %collective-permute-start.8 = (bf16[512,320]{1,0:T(8,128)(2,1)S(1)}, bf16[512,320]{1,0:T(8,128)(2,1)S(1)}, u32[]{:S(2)}, u32[]{:S(2)}) collective-permute-start(bf16[512,320]{1,0:T(8,128)(2,1)S(1)} %collective-permute-done.7.refs_6_), channel_id=1, source_target_pairs={{0,2},{1,3},{2,0},{3,1},{4,6},{5,7},{6,4},{7,5},{8,10},{9,11},{10,... | collective-permute-start | bytes 983048 | tf_op jit(solution)/shard_map/ppermute | solution.py:823
  49.1 7.9 %collective-permute-start.19 = (bf16[64,1280]{1,0:T(8,128)(2,1)S(1)}, bf16[64,1280]{1,0:T(8,128)(2,1)S(1)}, u32[]{:S(2)}, u32[]{:S(2)}) collective-permute-start(bf16[64,1280]{1,0:T(8,128)(2,1)S(1)} %collective-permute-done.14.refs_14_.rest_12_), channel_id=1, source_target_pairs={{8,0},{16,8},{24,16},{28,24},{20,28},{12,20},{4,12},{0,4},{9,1},{1... | collective-permute-start | bytes 491528 | tf_op jit(solution)/shard_map/ppermute | solution.py:787
  49.1 19.8 %collective-permute-start.6 = (bf16[512,640]{1,0:T(8,128)(2,1)}, bf16[512,640]{1,0:T(8,128)(2,1)S(1)}, u32[]{:S(2)}, u32[]{:S(2)}) collective-permute-start(bf16[512,640]{1,0:T(8,128)(2,1)} %collective-permute-done.4.refs_3_), channel_id=1, source_target_pairs={{0,1},{1,0},{2,3},{3,2},{4,5},{5,4},{6,7},{7,6},{8,9},{9,8},{10,11... | collective-permute-start | bytes 1966088 | tf_op jit(solution)/shard_map/ppermute | solution.py:823
  51.9 1.3 copy-start.29
  54.2 4.9 %copy-start.11 = (bf16[512,128]{1,0:T(8,128)(2,1)S(1)}, bf16[512,128]{1,0:T(8,128)(2,1)}, u32[]{:S(2)}) copy-start(bf16[512,128]{1,0:T(8,128)(2,1)} %read.15) | copy-start | bytes 393220
  54.2 4.9 %copy-start.15 = (bf16[512,128]{1,0:T(8,128)(2,1)S(1)}, bf16[512,128]{1,0:T(8,128)(2,1)}, u32[]{:S(2)}) copy-start(bf16[512,128]{1,0:T(8,128)(2,1)} %refs_5_.1) | copy-start | bytes 393220
  54.2 4.9 %copy-start.22 = (f32[512,128]{1,0:T(8,128)S(1)}, f32[512,128]{1,0:T(8,128)}, u32[]{:S(2)}) copy-start(f32[512,128]{1,0:T(8,128)} %copy-done.19) | copy-start | bytes 786436
  54.2 4.9 %copy-start.30 = (bf16[512,1280]{1,0:T(8,128)(2,1)S(1)}, bf16[512,1280]{1,0:T(8,128)(2,1)}, u32[]{:S(2)}) copy-start(bf16[512,1280]{1,0:T(8,128)(2,1)} %copy-done.27) | copy-start | bytes 3932164
  54.2 4.9 %copy-start.36 = (f32[128,512]{1,0:T(8,128)S(1)}, f32[128,512]{1,0:T(8,128)}, u32[]{:S(2)}) copy-start(f32[128,512]{1,0:T(8,128)} %copy-done.33) | copy-start | bytes 786436
  54.2 14.8 %slice-start = ((s8[6553600]{0:T(1024)(128)(4,1)}), s8[4194304]{0:T(1024)(128)(4,1)S(1)}, s32[]{:S(2)}) async-start(s8[6553600]{0:T(1024)(128)(4,1)} %bitcast.12), calls=%async_computation | async-start | bytes 8388608
  56.5 12.5 %slice-start.1 = ((s8[6553600]{0:T(1024)(128)(4,1)}), s8[2359296]{0:T(1024)(128)(4,1)S(1)}, s32[]{:S(2)}) async-start(s8[6553600]{0:T(1024)(128)(4,1)} %bitcast.12), calls=%async_computation.1 | async-start | bytes 4718592
  56.5 9.6 %collective-permute-start.9 = (bf16[512,320]{1,0:T(8,128)(2,1)S(1)}, bf16[512,320]{1,0:T(8,128)(2,1)S(1)}, u32[]{:S(2)}, u32[]{:S(2)}) collective-permute-start(bf16[512,320]{1,0:T(8,128)(2,1)S(1)} %collective-permute-done.7.refs_6_), channel_id=1, source_target_pairs={{0,1},{1,0},{2,3},{3,2},{4,5},{5,4},{6,7},{7,6},{8,9},{9,8},{10,11... | collective-permute-start | bytes 983048 | tf_op jit(solution)/shard_map/ppermute | solution.py:823
  57.1 7.1 %collective-permute-start.15 = (bf16[80,1280]{1,0:T(8,128)(2,1)S(1)}, bf16[80,1280]{1,0:T(8,128)(2,1)S(1)}, u32[]{:S(2)}, u32[]{:S(2)}) collective-permute-start(bf16[80,1280]{1,0:T(8,128)(2,1)S(1)} %collective-permute-done.11.refs_11_.rest_3_), channel_id=1, source_target_pairs={{0,8},{8,16},{16,24},{24,28},{28,20},{20,12},{12,4},{4,0},{1,9},{9... | collective-permute-start | bytes 614408 | tf_op jit(solution)/shard_map/ppermute | solution.py:786
  59.1 9.9 %collective-permute-start.10 = (bf16[512,320]{1,0:T(8,128)(2,1)S(1)}, bf16[512,320]{1,0:T(8,128)(2,1)S(1)}, u32[]{:S(2)}, u32[]{:S(2)}) collective-permute-start(bf16[512,320]{1,0:T(8,128)(2,1)S(1)} %collective-permute-done.8.refs_7_), channel_id=1, source_target_pairs={{0,1},{1,0},{2,3},{3,2},{4,5},{5,4},{6,7},{7,6},{8,9},{9,8},{10,11... | collective-permute-start | bytes 983048 | tf_op jit(solution)/shard_map/ppermute | solution.py:823
  62.4 15.2 %copy-start.2 = (bf16[512,1280]{1,0:T(8,128)(2,1)S(1)}, bf16[512,1280]{1,0:T(8,128)(2,1)}, u32[]{:S(2)}) copy-start(bf16[512,1280]{1,0:T(8,128)(2,1)} %gate.3) | copy-start | bytes 3932164
  62.4 15.2 %copy-start.26 = (bf16[256,1280]{1,0:T(8,128)(2,1)S(1)}, bf16[256,1280]{1,0:T(8,128)(2,1)}, u32[]{:S(2)}) copy-start(bf16[256,1280]{1,0:T(8,128)(2,1)} %copy-done.25) | copy-start | bytes 1966084
  64.1 13.4 %collective-permute-start.18 = (bf16[64,1280]{1,0:T(8,128)(2,1)S(1)}, bf16[64,1280]{1,0:T(8,128)(2,1)S(1)}, u32[]{:S(2)}, u32[]{:S(2)}) collective-permute-start(bf16[64,1280]{1,0:T(8,128)(2,1)S(1)} %collective-permute-done.13.refs_13_.rest_11_), channel_id=1, source_target_pairs={{0,8},{8,16},{16,24},{24,28},{28,20},{20,12},{12,4},{4,0},{1,9},{9... | collective-permute-start | bytes 491528 | tf_op jit(solution)/shard_map/ppermute | solution.py:786
  66.2 11.4 %collective-permute-start.16 = (bf16[80,1280]{1,0:T(8,128)(2,1)S(1)}, bf16[80,1280]{1,0:T(8,128)(2,1)S(1)}, u32[]{:S(2)}, u32[]{:S(2)}) collective-permute-start(bf16[80,1280]{1,0:T(8,128)(2,1)S(1)} %collective-permute-done.12.refs_12_.rest_4_), channel_id=1, source_target_pairs={{8,0},{16,8},{24,16},{28,24},{20,28},{12,20},{4,12},{0,4},{9,1},{1... | collective-permute-start | bytes 614408 | tf_op jit(solution)/shard_map/ppermute | solution.py:787
  66.9 10.6 %collective-permute-start.20 = (bf16[64,1280]{1,0:T(8,128)(2,1)S(1)}, bf16[64,1280]{1,0:T(8,128)(2,1)S(1)}, u32[]{:S(2)}, u32[]{:S(2)}) collective-permute-start(bf16[64,1280]{1,0:T(8,128)(2,1)S(1)} %collective-permute-done.19.rest_14_), channel_id=1, source_target_pairs={{8,0},{16,8},{24,16},{28,24},{20,28},{12,20},{4,12},{0,4},{9,1},{1... | collective-permute-start | bytes 491528 | tf_op jit(solution)/shard_map/ppermute | solution.py:787
  69.0 8.6 %collective-permute-start.17 = (bf16[80,1280]{1,0:T(8,128)(2,1)S(1)}, bf16[80,1280]{1,0:T(8,128)(2,1)S(1)}, u32[]{:S(2)}, u32[]{:S(2)}) collective-permute-start(bf16[80,1280]{1,0:T(8,128)(2,1)S(1)} %collective-permute-done.15.rest_5_), channel_id=1, source_target_pairs={{0,8},{8,16},{16,24},{24,28},{28,20},{20,12},{12,4},{4,0},{1,9},{9... | collective-permute-start | bytes 614408 | tf_op jit(solution)/shard_map/ppermute | solution.py:786
  83.8 1.2 collective-permute-start.21
  85.0 3.7 %collective-permute-start.22 = (f32[8,512]{1,0:T(8,128)S(1)}, f32[8,512]{1,0:T(8,128)S(1)}, u32[]{:S(2)}, u32[]{:S(2)}) collective-permute-start(f32[8,512]{1,0:T(8,128)S(1)} %add.63), channel_id=1, source_target_pairs={{0,2},{1,3},{2,0},{3,1},{4,6},{5,7},{6,4},{7,5},{8,10},{9,11},{10,... | collective-permute-start | bytes 49160 | tf_op jit(solution)/shard_map/ppermute | solution.py:812
  88.8 2.5 %copy-start.32 = (bf16[128,512]{1,0:T(8,128)(2,1)S(1)}, bf16[128,512]{1,0:T(8,128)(2,1)}, u32[]{:S(2)}) copy-start(bf16[128,512]{1,0:T(8,128)(2,1)} %copy-done.31) | copy-start | bytes 393220
  89.2 17.7 %collective-permute-start.27 = (bf16[640,512]{1,0:T(8,128)(2,1)S(1)}, bf16[640,512]{1,0:T(8,128)(2,1)S(1)}, u32[]{:S(2)}, u32[]{:S(2)}) collective-permute-start(bf16[640,512]{1,0:T(8,128)(2,1)S(1)} %get-tuple-element.89.mine), channel_id=1, source_target_pairs={{0,4},{4,0},{8,12},{12,8},{16,20},{20,16},{24,28},{28,24},{1,5},{5... | collective-permute-start | bytes 1966088 | tf_op jit(solution)/shard_map/ppermute | solution.py:900
  91.2 29.7 %collective-permute-start.30 = (bf16[640,512]{1,0:T(8,128)(2,1)S(1)}, bf16[640,512]{1,0:T(8,128)(2,1)S(1)}, u32[]{:S(2)}, u32[]{:S(2)}) collective-permute-start(bf16[640,512]{1,0:T(8,128)(2,1)S(1)} %get-tuple-element.88.mine), channel_id=1, source_target_pairs={{0,4},{4,0},{8,12},{12,8},{16,20},{20,16},{24,28},{28,24},{1,5},{5... | collective-permute-start | bytes 1966088 | tf_op jit(solution)/shard_map/ppermute | solution.py:900
  96.9 32.5 %collective-permute-start.23 = (bf16[64,1280]{1,0:T(8,128)(2,1)S(1)}, bf16[64,1280]{1,0:T(8,128)(2,1)S(1)}, u32[]{:S(2)}, u32[]{:S(2)}) collective-permute-start(bf16[64,1280]{1,0:T(8,128)(2,1)S(1)} %get-tuple-element.67), channel_id=1, source_target_pairs={{0,4},{4,0},{8,12},{12,8},{16,20},{20,16},{24,28},{28,24},{1,5},{5... | collective-permute-start | bytes 491528 | tf_op jit(solution)/shard_map/ppermute | solution.py:593
  111.4 9.3 %copy-start.23 = (f32[320,640]{1,0:T(8,128)}, f32[320,640]{1,0:T(8,128)S(1)}, u32[]{:S(2)}) copy-start(f32[320,640]{1,0:T(8,128)S(1)} %get-tuple-element.84.own) | copy-start | bytes 2457604
  111.4 22.8 %collective-permute-start.28 = (bf16[320,640]{1,0:T(8,128)(2,1)S(1)}, bf16[320,640]{1,0:T(8,128)(2,1)S(1)}, u32[]{:S(2)}, u32[]{:S(2)}) collective-permute-start(bf16[320,640]{1,0:T(8,128)(2,1)S(1)} %get-tuple-element.72), channel_id=1, source_target_pairs={{0,8},{4,12},{24,16},{28,20},{1,9},{5,13},{25,17},{29,21},{2,10},{... | collective-permute-start | bytes 1228808 | tf_op jit(solution)/shard_map/ppermute | solution.py:835
  125.8 25.3 %collective-permute-start.31 = (bf16[320,640]{1,0:T(8,128)(2,1)}, bf16[320,640]{1,0:T(8,128)(2,1)S(1)}, u32[]{:S(2)}, u32[]{:S(2)}) collective-permute-start(bf16[320,640]{1,0:T(8,128)(2,1)} %get-tuple-element.76), channel_id=1, source_target_pairs={{0,8},{4,12},{24,16},{28,20},{1,9},{5,13},{25,17},{29,21},{2,10},{... | collective-permute-start | bytes 1228808 | tf_op jit(solution)/shard_map/ppermute | solution.py:835
  130.1 7.3 %collective-permute-start.24 = (bf16[64,1280]{1,0:T(8,128)(2,1)S(1)}, bf16[64,1280]{1,0:T(8,128)(2,1)S(1)}, u32[]{:S(2)}, u32[]{:S(2)}) collective-permute-start(bf16[64,1280]{1,0:T(8,128)(2,1)S(1)} %shard_map.179), channel_id=1, source_target_pairs={{8,0},{12,4},{16,8},{20,12},{24,16},{28,20},{9,1},{13,5},{17,9},{2... | collective-permute-start | bytes 491528 | tf_op jit(solution)/shard_map/ppermute | solution.py:599
  131.4 9.9 %collective-permute-start.25 = (bf16[64,1280]{1,0:T(8,128)(2,1)S(1)}, bf16[64,1280]{1,0:T(8,128)(2,1)S(1)}, u32[]{:S(2)}, u32[]{:S(2)}) collective-permute-start(bf16[64,1280]{1,0:T(8,128)(2,1)S(1)} %shard_map.179), channel_id=1, source_target_pairs={{16,0},{20,4},{24,8},{28,12},{17,1},{21,5},{25,9},{29,13},{18,2},{... | collective-permute-start | bytes 491528 | tf_op jit(solution)/shard_map/ppermute | solution.py:599
  132.7 16.1 %collective-permute-start.26 = (bf16[64,1280]{1,0:T(8,128)(2,1)S(1)}, bf16[64,1280]{1,0:T(8,128)(2,1)S(1)}, u32[]{:S(2)}, u32[]{:S(2)}) collective-permute-start(bf16[64,1280]{1,0:T(8,128)(2,1)S(1)} %shard_map.179), channel_id=1, source_target_pairs={{24,0},{28,4},{25,1},{29,5},{26,2},{30,6},{27,3},{31,7}} | collective-permute-start | bytes 491528 | tf_op jit(solution)/shard_map/ppermute | solution.py:599
  149.6 5.4 %collective-permute-start.29 = (bf16[64,1280]{1,0:T(8,128)(2,1)S(1)}, bf16[64,1280]{1,0:T(8,128)(2,1)S(1)}, u32[]{:S(2)}, u32[]{:S(2)}) collective-permute-start(bf16[64,1280]{1,0:T(8,128)(2,1)S(1)} %get-tuple-element.74), channel_id=1, source_target_pairs={{0,4},{4,0},{8,12},{12,8},{16,20},{20,16},{24,28},{28,24},{1,5},{5... | collective-permute-start | bytes 491528 | tf_op jit(solution)/shard_map/ppermute | solution.py:610
  162.1 23.6 %collective-permute-start.32 = (f32[2,512,128]{2,1,0:T(8,128)S(1)}, f32[2,512,128]{2,1,0:T(8,128)S(1)}, u32[]{:S(2)}, u32[]{:S(2)}) collective-permute-start(f32[2,512,128]{2,1,0:T(8,128)S(1)} %get-tuple-element.79), channel_id=1, source_target_pairs={{0,1},{1,0},{2,3},{3,2},{4,5},{5,4},{6,7},{7,6},{8,9},{9,8},{10,11... | collective-permute-start | bytes 1572872 | tf_op jit(solution)/shard_map/ppermute | solution.py:812
  162.1 32.0 %collective-permute-start.40 = (bf16[320,640]{1,0:T(8,128)(2,1)S(1)}, bf16[320,640]{1,0:T(8,128)(2,1)S(1)}, u32[]{:S(2)}, u32[]{:S(2)}) collective-permute-start(bf16[320,640]{1,0:T(8,128)(2,1)S(1)} %get-tuple-element.72), channel_id=1, source_target_pairs={{8,16},{12,20},{16,8},{20,12},{9,17},{13,21},{17,9},{21,13},{10,18... | collective-permute-start | bytes 1228808 | tf_op jit(solution)/shard_map/ppermute | solution.py:835
  162.8 33.4 %collective-permute-start.41 = (bf16[320,640]{1,0:T(8,128)(2,1)S(1)}, bf16[320,640]{1,0:T(8,128)(2,1)S(1)}, u32[]{:S(2)}, u32[]{:S(2)}) collective-permute-start(bf16[320,640]{1,0:T(8,128)(2,1)S(1)} %get-tuple-element.85), channel_id=1, source_target_pairs={{0,8},{4,12},{8,0},{12,4},{16,24},{20,28},{24,16},{28,20},{1,9},{5... | collective-permute-start | bytes 1228808 | tf_op jit(solution)/shard_map/ppermute | solution.py:835
  162.9 4.0 %collective-permute-start.34 = (f32[8,1280]{1,0:T(8,128)S(1)}, f32[8,1280]{1,0:T(8,128)S(1)}, u32[]{:S(2)}, u32[]{:S(2)}) collective-permute-start(f32[8,1280]{1,0:T(8,128)S(1)} %get-tuple-element.81), channel_id=1, source_target_pairs={{0,4},{4,0},{8,12},{12,8},{16,20},{20,16},{24,28},{28,24},{1,5},{5... | collective-permute-start | bytes 122888 | tf_op jit(solution)/shard_map/ppermute | solution.py:812
  164.4 34.4 %collective-permute-start.42 = (bf16[320,640]{1,0:T(8,128)(2,1)S(1)}, bf16[320,640]{1,0:T(8,128)(2,1)}, u32[]{:S(2)}, u32[]{:S(2)}) collective-permute-start(bf16[320,640]{1,0:T(8,128)(2,1)S(1)} %add_convert_fusion.1.refs_8_), channel_id=1, source_target_pairs={{0,16},{4,20},{8,24},{12,28},{16,0},{20,4},{24,8},{28,12},{1,17},{... | collective-permute-start | bytes 1228808 | tf_op jit(solution)/shard_map/ppermute | solution.py:835
  166.9 15.3 %collective-permute-start.35 = (f32[8,1280]{1,0:T(8,128)S(1)}, f32[8,1280]{1,0:T(8,128)S(1)}, u32[]{:S(2)}, u32[]{:S(2)}) collective-permute-start(f32[8,1280]{1,0:T(8,128)S(1)} %add.71), channel_id=1, source_target_pairs={{0,8},{4,12},{8,0},{12,4},{16,24},{20,28},{24,16},{28,20},{1,9},{5... | collective-permute-start | bytes 122888 | tf_op jit(solution)/shard_map/ppermute | solution.py:812
  182.2 11.2 %collective-permute-start.36 = (f32[8,1280]{1,0:T(8,128)S(1)}, f32[8,1280]{1,0:T(8,128)S(1)}, u32[]{:S(2)}, u32[]{:S(2)}) collective-permute-start(f32[8,1280]{1,0:T(8,128)S(1)} %add.72), channel_id=1, source_target_pairs={{0,16},{4,20},{8,24},{12,28},{16,0},{20,4},{24,8},{28,12},{1,17},{... | collective-permute-start | bytes 122888 | tf_op jit(solution)/shard_map/ppermute | solution.py:812
  186.5 36.7 %collective-permute-start.33 = (f32[2,512,128]{2,1,0:T(8,128)}, f32[2,512,128]{2,1,0:T(8,128)}, u32[]{:S(2)}, u32[]{:S(2)}) collective-permute-start(f32[2,512,128]{2,1,0:T(8,128)} %add.69), channel_id=1, source_target_pairs={{0,2},{1,3},{2,0},{3,1},{4,6},{5,7},{6,4},{7,5},{8,10},{9,11},{10,... | collective-permute-start | bytes 1572872 | tf_op jit(solution)/shard_map/ppermute | solution.py:812
  193.4 10.6 %collective-permute-start.37 = (bf16[320,640]{1,0:T(8,128)(2,1)}, bf16[320,640]{1,0:T(8,128)(2,1)S(1)}, u32[]{:S(2)}, u32[]{:S(2)}) collective-permute-start(bf16[320,640]{1,0:T(8,128)(2,1)} %get-tuple-element.76), channel_id=1, source_target_pairs={{8,16},{12,20},{16,8},{20,12},{9,17},{13,21},{17,9},{21,13},{10,18... | collective-permute-start | bytes 1228808 | tf_op jit(solution)/shard_map/ppermute | solution.py:835
  194.9 12.9 %collective-permute-start.38 = (bf16[320,640]{1,0:T(8,128)(2,1)S(1)}, bf16[320,640]{1,0:T(8,128)(2,1)S(1)}, u32[]{:S(2)}, u32[]{:S(2)}) collective-permute-start(bf16[320,640]{1,0:T(8,128)(2,1)S(1)} %get-tuple-element.83), channel_id=1, source_target_pairs={{0,8},{4,12},{8,0},{12,4},{16,24},{20,28},{24,16},{28,20},{1,9},{5... | collective-permute-start | bytes 1228808 | tf_op jit(solution)/shard_map/ppermute | solution.py:835
  197.0 25.2 %collective-permute-start.39 = (bf16[320,640]{1,0:T(8,128)(2,1)S(1)}, bf16[320,640]{1,0:T(8,128)(2,1)S(1)}, u32[]{:S(2)}, u32[]{:S(2)}) collective-permute-start(bf16[320,640]{1,0:T(8,128)(2,1)S(1)} %add_convert_fusion.refs_15_), channel_id=1, source_target_pairs={{0,16},{4,20},{8,24},{12,28},{16,0},{20,4},{24,8},{28,12},{1,17},{... | collective-permute-start | bytes 1228808 | tf_op jit(solution)/shard_map/ppermute | solution.py:835
  198.8 1.0 copy-start.4
  199.8 1.0 copy-start.6
  200.8 1.1 copy-start.24
  (21 other events, 17.6 us)

commit v3 on v2

--- a/solution.py
+++ b/solution.py
@@ -41,6 +41,9 @@
 
 def spread(values, spread2):
     return mm(jnp.concatenate(split2(values), axis=1), spread2)
+
+
+FULL_GRANT = 67_043_328
 
 
 def params(limit=24 << 20):
@@ -121,7 +124,7 @@
         name="prepare",
         out_shape=shapes,
         scratch_shapes=[pltpu.VMEM((LANES, length), F32), pltpu.VMEM((8, LANES), F32)],
-        compiler_params=params(),
+        compiler_params=params(FULL_GRANT),
         cost_estimate=cost(3e9, 8e6),
     )(packed, expo, decay, skip, write, read)
 
@@ -131,12 +134,12 @@
     for sub in range(per_half):
         even_part = shard[:, 2 * sub * columns : (2 * sub + 1) * columns]
         odd_part = shard[:, (2 * sub + 1) * columns : (2 * sub + 2) * columns]
-        out[:, sub * columns : (sub + 1) * columns] = jnp.where(odd_wanted, odd_part, even_part)
+        out[sub * columns : (sub + 1) * columns, :] = jnp.where(odd_wanted, odd_part, even_part).T
 
 
 def pick(parity, shard, columns):
     length, shard_width = shard.shape
-    out = (length, shard_width // 2)
+    out = (shard_width // 2, length)
     return pl.pallas_call(
         functools.partial(pick_kernel, shard_width // (2 * columns), columns),
         name="pick",
@@ -151,8 +154,7 @@
 
 def cotangent_kernel(shards, per_half, owners, weight, *rest):
     mine = rest[:shards]
-    theirs = rest[shards : 2 * shards]
-    grad_v, cot_mine, cot_theirs, full = rest[2 * shards :]
+    grad_v, cot_mine, full = rest[shards:]
     shard_width = mine[0].shape[1]
     columns = cot_mine.shape[1]
 
@@ -167,46 +169,65 @@
             for sub in range(per_half):
                 even_part = mine[m][:, 2 * sub * columns : (2 * sub + 1) * columns]
                 odd_part = mine[m][:, (2 * sub + 1) * columns : (2 * sub + 2) * columns]
-                spot = owners[m] * per_half + sub
-                cot_mine[spot] = jnp.where(odd, odd_part, even_part).T
-                cot_theirs[spot] = theirs[m][:, sub * columns : (sub + 1) * columns].T
+                cot_mine[owners[m] * per_half + sub] = jnp.where(odd, odd_part, even_part).T
 
     grad_v[...] = mm_t(full[...], weight[...])
 
 
-def cotangent(owners, weight, mine, theirs, columns, waits):
+def cotangent(owners, weight, mine, columns, waits):
     shards = len(mine)
     length, shard_width = mine[0].shape
     width, model_width = weight.shape
     per_half = shard_width // (2 * columns)
-    groups = shards * per_half
     block = 2 * LANES if width % (2 * LANES) == 0 else LANES
-    stacked = (groups, columns, length)
-    return pl.pallas_call(
-        skipping(
-            functools.partial(cotangent_kernel, shards, per_half), 2 + 2 * shards, len(waits)
-        ),
+    stacked = (shards * per_half, columns, length)
+    return pl.pallas_call(
+        skipping(functools.partial(cotangent_kernel, shards, per_half), 2 + shards, len(waits)),
         name="cotangent",
         grid_spec=pltpu.PrefetchScalarGridSpec(
             num_scalar_prefetch=1,
             grid=(width // block,),
             in_specs=[pl.BlockSpec((block, model_width), lambda i, *_: (i, 0))]
             + [whole(mine[0].shape)] * shards
-            + [whole(theirs[0].shape)] * shards
             + [WAIT] * len(waits),
-            out_specs=[
-                pl.BlockSpec((length, block), lambda i, *_: (0, i)), whole(stacked), whole(stacked),
-            ],
+            out_specs=[pl.BlockSpec((length, block), lambda i, *_: (0, i)), whole(stacked)],
             scratch_shapes=[pltpu.VMEM((length, model_width), BF16)],
         ),
         out_shape=(
             jax.ShapeDtypeStruct((length, width), F32),
             jax.ShapeDtypeStruct(stacked, BF16),
-            jax.ShapeDtypeStruct(stacked, BF16),
         ),
         compiler_params=params(),
         cost_estimate=cost(2.0 * length * width * model_width, 20e6),
-    )(owners, weight, *mine, *theirs, *waits)
+    )(owners, weight, *mine, *waits)
+
+
+def stack_kernel(shards, owners, *rest):
+    theirs, out = rest[:shards], rest[shards]
+    columns = out.shape[1]
+    per_half = theirs[0].shape[0] // columns
+    for m in range(shards):
+        for sub in range(per_half):
+            rows = slice(sub * columns, (sub + 1) * columns)
+            out[owners[m] * per_half + sub] = theirs[m][rows, :]
+
+
+def stack(owners, theirs, columns):
+    rows, length = theirs[0].shape
+    out = (len(theirs) * rows // columns, columns, length)
+    return pl.pallas_call(
+        functools.partial(stack_kernel, len(theirs)),
+        name="stack",
+        grid_spec=pltpu.PrefetchScalarGridSpec(
+            num_scalar_prefetch=1,
+            grid=(1,),
+            in_specs=[whole(theirs[0].shape)] * len(theirs),
+            out_specs=whole(out),
+        ),
+        out_shape=jax.ShapeDtypeStruct(out, BF16),
+        compiler_params=params(),
+        cost_estimate=cost(1e8, 3e6),
+    )(owners, *theirs)
 
 
 def pair_columns(seg_t, seg, step):
@@ -806,11 +827,10 @@
     return jnp.concatenate([found, position[None]]).astype(jnp.int32)
 
 
-def butterfly_sum(value, axis, size):
-    stride = 1
-    while stride < size:
+def butterfly_sum(value, axis, size, first=1):
+    strides = [1 << k for k in range(size.bit_length() - 1)]
+    for stride in [v for v in strides if v >= first] + [v for v in strides if v < first]:
         value = value + lax.ppermute(value, axis, [(i, i ^ stride) for i in range(size)])
-        stride *= 2
     return value
 
 
@@ -873,19 +893,18 @@
     owners = jnp.concatenate([owners, parity[None]]).astype(jnp.int32)
 
     pairs = width // LANES
-    calls = min(4, pairs)
+    calls = min(2, pairs)
     y_local = None
     hops = seq_size // 2
     for call in range(calls):
         start, stop = call * pairs // calls, (call + 1) * pairs // calls
-        waits = (*near[1:3], *far[1:3]) if call == 2 and hops > 2 else ()
+        waits = (*near[1:3], *far[1:3]) if call == 1 and hops > 2 else ()
         y_local = inside(
             heads, start, stop, seg_t, seg, state_write, state_read, x, skip, y_local, waits
         )
     waits = (y_local, *near[3:5], *far[3:5]) if hops > 2 else (y_local,)
-    grad_v, cot_mine, cot_theirs = cotangent(
-        owners, out_weight, all_mine, all_theirs, columns, waits
-    )
+    grad_v, cot_mine = cotangent(owners, out_weight, all_mine, columns, waits)
+    cot_theirs = stack(owners, all_theirs, columns)
 
     y, scaled_t, stats, state, totals = enter(
         sources, y_local, gate_input, grad_v, gain, state_read, seg_t, spread2, near, far
@@ -920,13 +939,13 @@
     )
     grad_input, maps, grad_decay = leave(
         heads, sources, y, x, grad_y, inner, state_write, seg_t, spread2, skip, state,
-        write_part, read_part, own, other, tuple(merges[-1]),
+        write_part, read_part, own, other, (),
     )
     grad_out_weight = None
     for part in range(NORMED_PARTS):
         grad_out_weight = finish(part, NORMED_PARTS, own_part[part], arrived[part], grad_out_weight)
     maps = butterfly_sum(maps, "tp", tp_size)
-    sums = butterfly_sum(sums, "seq", seq_size)
+    sums = butterfly_sum(sums, "seq", seq_size, 2)
     grad_skip = jnp.sum(sums[1].reshape(heads, width // heads), axis=1)
     return (
         grad_input, grad_gate, maps[0], maps[1], grad_decay, grad_skip, sums[0], grad_out_weight.T,

time: 226 us -> 220 us (0.973)
  local copies, waits for them, and re-layouts: 26 us -> 14 us
  waiting for transfers between devices: 77.6 us -> 85 us
    unnamed x84 -> x60, local copies, waits for them, and re-layouts: 24.5 us -> 12.5 us
    ppermute x8, waiting for transfers between devices: 18.2 us -> 29.3 us  [move(): return lax.ppermute(value, 'seq', pairs)]
    ppermute x7, waiting for transfers between devices: 0.02 us -> 8.52 us  [ring_gather(): lax.ppermute(v, 'seq', behind)]
    ppermute x1, waiting for transfers between devices: 6.86 us -> 0.01 us  [on_device(): theirs = lax.ppermute(other_half, 'seq', partner)]
    ppermute x7, starting transfers between devices: 3.26 us -> 7.45 us  [ring_gather(): lax.ppermute(v, 'seq', behind)]
    ppermute x7, starting transfers between devices: 12.3 us -> 8.36 us  [ring_gather(): up = [lax.ppermute(v, 'seq', ahead) for v in (up[:1] if last else up)]]
    ppermute x7, waiting for transfers between devices: 6.77 us -> 2.84 us  [ring_gather(): up = [lax.ppermute(v, 'seq', ahead) for v in (up[:1] if last else up)]]
    ppermute x7, starting transfers between devices: 8.88 us -> 5.95 us  [butterfly_sum(): lax.ppermute(value, axis, [(i, i ^ stride) for i in range(size)])]
  transfers between devices with their start and end apart: 43 -> 43, of which waited for: 17 -> 18; matrix products, arithmetic and copies ran while one was open for 1% -> 2% of each run, Pallas kernels for 22% -> 27%
where the time goes in v3:
time: 220 us; the launch traced here: 219 us
  waiting for transfers between devices  85 us (39%)
  Pallas kernels  65.3 us (30%)
  starting transfers between devices  49.2 us (22%)
  local copies, waits for them, and re-layouts  14 us (6%)
  other arithmetic  4.38 us (2%)
    ppermute x8, waiting for transfers between devices, move(): return lax.ppermute(value, 'seq', pairs)  29.3 us
    ppermute x7, waiting for transfers between devices, butterfly_sum(): lax.ppermute(value, axis, [(i, i ^ stride) for i in range(size)])  22.8 us
    ppermute x3, waiting for transfers between devices, pair_state(): later.append(lax.ppermute(pair, 'seq', moves))  13.7 us
    ppermute x8, starting transfers between devices, move(): return lax.ppermute(value, 'seq', pairs)  13.3 us
    unnamed x60, local copies, waits for them, and re-layouts  12.5 us
    pallas_call x2, Pallas kernels, inside_back(): pl.pallas_call(functools.partial(inside_back_kernel, width // heads, star...  10.6 us
    pallas_call x2, Pallas kernels, inside(): pl.pallas_call(functools.partial(inside_kernel, width // heads, start), n...  10.2 us
    pallas_call x2, Pallas kernels, products(): pl.pallas_call(functools.partial(product_kernel, masks), name='product',...  9.05 us
  transfers between devices with their start and end apart: 43, of which 18 were waited for; matrix products, arithmetic and copies ran while one was open for 2% of the time, Pallas kernels for 27%

profile of v3, /device:TPU:0, one launch (start us, length us, event | category | flops | bytes accessed | tf_op | source)
XLA Modules:
  0.0 219.2 jit_solution(7403049604381987150)
XLA Ops:
  0.6 5.1 %prepare.1 = (bf16[512,1280]{1,0:T(8,128)(2,1)}, bf16[80,1280]{1,0:T(8,128)(2,1)}, bf16[64,1280]{1,0:T(8,128)(2,1)}, f32[512,128]{1,0:T(8,128)}, f32[128,512]{1,...) custom-call(s32[64,1280]{1,0:T(8,128)} %packed.1, s32[10,512]{1,0:T(8,128)} %expo.1, ...), custom_call_target="tpu_custom_call" | custom-call | flops 3000000000 | bytes 8000000 | tf_op jit(solution)/shard_map/prepare/pallas_call | solution.py:122
  5.7 3.1 %collective-permute-start = (bf16[80,1280]{1,0:T(8,128)(2,1)}, bf16[80,1280]{1,0:T(8,128)(2,1)S(1)}, u32[]{:S(2)}, u32[]{:S(2)}) collective-permute-start(bf16[80,1280]{1,0:T(8,128)(2,1)} %get-tuple-element.50.rest_0_), channel_id=1, source_target_pairs={{0,8},{8,16},{16,24},{24,28},{28,20},{20,12},{12,4},{4,0},{1,9},{9... | collective-permute-start | bytes 614408 | tf_op jit(solution)/shard_map/ppermute | solution.py:807
  8.8 2.0 collective-permute-start.2
  10.8 2.0 collective-permute-start.4
  12.8 1.1 copy-done
  14.3 0.9 copy-done.9
  15.2 0.9 copy-done.11
  16.1 0.9 copy-done.13
  17.1 1.3 copy-done.18
  18.4 0.9 copy-done.21
  20.2 5.1 %inside.2.rest_0_ = f32[512,1280]{1,0:T(8,128)S(1)} custom-call(f32[512,128]{1,0:T(8,128)S(1)} %copy-done.13, f32[128,512]{1,0:T(8,128)S(1)} %copy-done.21, bf16[512,128]{1,0:T(8,128)(2,1)S(1)} %copy-done.11, bf16[512,128]{1,0:T(8,128)(2,1)S(1)} %copy-done.9, bf16[512,1280]{1,0:T(8,128)(2,1)S(1)} %copy-done.18, f32[8,1280]{1,0:T(8,128)S(1)} %copy-done.23), custom_call_target="tpu_custom_call" | custom-call | flops 10000000000 | bytes 2500000 | tf_op jit(solution)/shard_map/inside/pallas_call | solution.py:290
  25.3 1.6 collective-permute-start.24
  27.4 1.5 collective-permute-start.9
  29.0 1.6 collective-permute-start.7
  30.6 5.4 %collective-permute-done.10.refs_10_.rest_12_ = bf16[64,1280]{1,0:T(8,128)(2,1)S(1)} collective-permute-done((bf16[64,1280]{1,0:T(8,128)(2,1)S(1)}, bf16[64,1280]{1,0:T(8,128)(2,1)S(1)}, u32[]{:S(2)}, u32[]{:S(2)}) %collective-permute-start.10) | collective-permute-done | bytes 163872 | tf_op jit(solution)/shard_map/ppermute | solution.py:808
  36.0 2.5 %collective-permute-start.8 = (bf16[80,1280]{1,0:T(8,128)(2,1)S(1)}, bf16[80,1280]{1,0:T(8,128)(2,1)S(1)}, u32[]{:S(2)}, u32[]{:S(2)}) collective-permute-start(bf16[80,1280]{1,0:T(8,128)(2,1)S(1)} %collective-permute-done.1.rest_2_), channel_id=1, source_target_pairs={{8,0},{16,8},{24,16},{28,24},{20,28},{12,20},{4,12},{0,4},{9,1},{1... | collective-permute-start | bytes 614408 | tf_op jit(solution)/shard_map/ppermute | solution.py:808
  39.4 1.9 collective-permute-done.7.refs_7_.rest_3_
  42.8 1.7 collective-permute-done.15.rest_14_
  44.5 5.1 %inside.3.refs_6_.y_local = f32[512,1280]{1,0:T(8,128)S(1)} custom-call(f32[512,128]{1,0:T(8,128)S(1)} %copy-done.14, f32[128,512]{1,0:T(8,128)S(1)} %copy-done.22, bf16[512,128]{1,0:T(8,128)(2,1)S(1)} %copy-done.12, bf16[512,128]{1,0:T(8,128)(2,1)S(1)} %copy-done.10, bf16[512,1280]{1,0:T(8,128)(2,1)S(1)} %copy-done.18, ...), custom_call_target="tpu_custom_call", output_to_operand_aliasing={{}: (6, {})} | custom-call | flops 10000000000 | bytes 2500000 | tf_op jit(solution)/shard_map/inside/pallas_call | solution.py:290
  50.5 1.9 collective-permute-start.12
  52.3 2.6 %collective-permute-start.16 = (bf16[64,1280]{1,0:T(8,128)(2,1)S(1)}, bf16[64,1280]{1,0:T(8,128)(2,1)S(1)}, u32[]{:S(2)}, u32[]{:S(2)}) collective-permute-start(bf16[64,1280]{1,0:T(8,128)(2,1)S(1)} %collective-permute-done.15.rest_14_), channel_id=1, source_target_pairs={{8,0},{16,8},{24,16},{28,24},{20,28},{12,20},{4,12},{0,4},{9,1},{1... | collective-permute-start | bytes 491528 | tf_op jit(solution)/shard_map/ppermute | solution.py:808
  55.0 7.0 %cotangent.1 = (f32[512,1280]{1,0:T(8,128)S(1)}, bf16[4,320,512]{2,1,0:T(8,128)(2,1)S(1)}) custom-call(s32[5]{0:T(128)S(1)} %pad_add_fusion.1.refs_0_.owners, bf16[1280,2560]{1,0:T(8,128)(2,1)S(1)} %bitcast.13, bf16[512,640]{1,0:T(8,128)(2,1)S(1)} %copy-done.1, bf16[512,640]{1,0:T(8,128)(2,1)S(1)} %collective-permute-done.4.refs_3_, ...), custom_call_target="tpu_custom_call" | custom-call | flops 3355443200 | bytes 20000000 | tf_op jit(solution)/shard_map/cotangent/pallas_call | solution.py:184
  62.7 5.2 %enter.1 = (f32[512,1280]{1,0:T(8,128)S(1)}, f32[1280,512]{1,0:T(8,128)S(1)}, f32[8,512]{1,0:T(8,128)S(1)}, f32[128,1280]{1,0:T(8,128)S(1)}, f32[8,1280]{1,0:T(8,128)S(1)}) custom-call(s32[9]{0:T(128)S(1)} %pad_add_fusion.sources.refs_0_, f32[512,1280]{1,0:T(8,128)S(1)} %inside.3.refs_6_.y_local, bf16[512,1280]{1,0:T(8,128)(2,1)S(1)} %copy-done.2, ...), custom_call_target="tpu_custom_call" | custom-call | flops 3000000000 | bytes 15000000 | tf_op jit(solution)/shard_map/enter/pallas_call | solution.py:371
  67.9 1.2 collective-permute-done.17
  70.2 2.6 %collective-permute-done.18 = f32[8,512]{1,0:T(8,128)S(1)} collective-permute-done((f32[8,512]{1,0:T(8,128)S(1)}, f32[8,512]{1,0:T(8,128)S(1)}, u32[]{:S(2)}, u32[]{:S(2)}) %collective-permute-start.18) | collective-permute-done | bytes 16416 | tf_op jit(solution)/shard_map/ppermute | solution.py:833
  73.2 1.5 collective-permute-start.23
  75.3 5.6 %gate_grads.1 = (bf16[512,1280]{1,0:T(8,128)(2,1)}, f32[512,1280]{1,0:T(8,128)S(1)}, bf16[64,1280]{1,0:T(8,128)(2,1)S(1)}, f32[64,1280]{1,0:T(8,128)S(1)}, f32[8,1280]{1,0:T(8,128)S(1)}) custom-call(s32[9]{0:T(128)S(1)} %pad_add_fusion.sources.refs_0_, f32[512,1280]{1,0:T(8,128)S(1)} %get-tuple-element.54.y_ref.refs_1_, bf16[512,1280]{1,0:T(8,128)(2,1)S(1)} %copy-done.2, ...), custom_call_target="tpu_custom_call" | custom-call | flops 3000000000 | bytes 15000000 | tf_op jit(solution)/shard_map/gate_grads/pallas_call | solution.py:452
  81.0 1.5 collective-permute-start.19
  82.5 4.9 %inside_back.2 = (f32[512,1280]{1,0:T(8,128)S(1)}, f32[512,512]{1,0:T(8,128)S(1)}) custom-call(f32[512,128]{1,0:T(8,128)S(1)} %copy-done.14, f32[128,512]{1,0:T(8,128)S(1)} %copy-done.22, bf16[512,128]{1,0:T(8,128)(2,1)S(1)} %copy-done.12, bf16[512,128]{1,0:T(8,128)(2,1)S(1)} %copy-done.10, bf16[512,1280]{1,0:T(8,128)(2,1)S(1)} %copy-done.19, ...), custom_call_target="tpu_custom_call" | custom-call | flops 10000000000 | bytes 4000000 | tf_op jit(solution)/shard_map/inside_back/pallas_call | solution.py:548
  87.4 3.5 %collective-permute-done.23.theirs = bf16[640,512]{1,0:T(8,128)(2,1)S(1)} collective-permute-done((bf16[640,512]{1,0:T(8,128)(2,1)S(1)}, bf16[640,512]{1,0:T(8,128)(2,1)S(1)}, u32[]{:S(2)}, u32[]{:S(2)}) %collective-permute-start.23) | collective-permute-done | bytes 655392 | tf_op jit(solution)/shard_map/ppermute | solution.py:919
  90.9 4.5 %product.2 = (bf16[320,640]{1,0:T(8,128)(2,1)S(1)}, bf16[320,640]{1,0:T(8,128)(2,1)S(1)}, bf16[320,640]{1,0:T(8,128)(2,1)S(1)}, f32[320,640]{1,0:T(8,128)S(1)}) custom-call(s32[1]{0:T(128)} %bitcast.4.group, bf16[640,512]{1,0:T(8,128)(2,1)S(1)} %get-tuple-element.87.mine, bf16[640,512]{1,0:T(8,128)(2,1)S(1)} %collective-permute-done.23.theirs, ...), custom_call_target="tpu_custom_call" | custom-call | flops 1677721600 | bytes 5000000 | tf_op jit(solution)/shard_map/product/pallas_call | solution.py:748
  95.5 0.9 copy-done.15
  96.4 3.7 %collective-permute-start.28 = (bf16[320,640]{1,0:T(8,128)(2,1)S(1)}, bf16[320,640]{1,0:T(8,128)(2,1)S(1)}, u32[]{:S(2)}, u32[]{:S(2)}) collective-permute-start(bf16[320,640]{1,0:T(8,128)(2,1)S(1)} %get-tuple-element.70), channel_id=1, source_target_pairs={{0,8},{4,12},{24,16},{28,20},{1,9},{5,13},{25,17},{29,21},{2,10},{... | collective-permute-start | bytes 1228808 | tf_op jit(solution)/shard_map/ppermute | solution.py:855
  100.0 5.6 %inside_back.3 = (f32[512,1280]{1,0:T(8,128)S(1)}, f32[512,128]{1,0:T(8,128)S(1)}, f32[512,128]{1,0:T(8,128)S(1)}) custom-call(f32[512,128]{1,0:T(8,128)S(1)} %copy-done.14, f32[128,512]{1,0:T(8,128)S(1)} %copy-done.22, bf16[512,128]{1,0:T(8,128)(2,1)S(1)} %copy-done.12, bf16[512,128]{1,0:T(8,128)(2,1)S(1)} %copy-done.10, ...), custom_call_target="tpu_custom_call", output_to_operand_aliasing={{0}: (6, {})} | custom-call | flops 10000000000 | bytes 4000000 | tf_op jit(solution)/shard_map/inside_back/pallas_call | solution.py:548
  105.7 0.9 collective-permute-done.19.refs_3_
  107.2 1.3 collective-permute-start.20
  108.5 1.3 collective-permute-start.21
  109.8 1.5 collective-permute-start.22
  111.4 4.2 %collective-permute-done.20.refs_4_ = bf16[64,1280]{1,0:T(8,128)(2,1)S(1)} collective-permute-done((bf16[64,1280]{1,0:T(8,128)(2,1)S(1)}, bf16[64,1280]{1,0:T(8,128)(2,1)S(1)}, u32[]{:S(2)}, u32[]{:S(2)}) %collective-permute-start.20) | collective-permute-done | bytes 163872 | tf_op jit(solution)/shard_map/ppermute | solution.py:620
  115.6 9.5 %collective-permute-done.21.refs_5_ = bf16[64,1280]{1,0:T(8,128)(2,1)S(1)} collective-permute-done((bf16[64,1280]{1,0:T(8,128)(2,1)S(1)}, bf16[64,1280]{1,0:T(8,128)(2,1)S(1)}, u32[]{:S(2)}, u32[]{:S(2)}) %collective-permute-start.21) | collective-permute-done | bytes 163872 | tf_op jit(solution)/shard_map/ppermute | solution.py:620
  125.8 1.8 collective-permute-start.29
  127.7 3.5 %collective-permute-done.29.refs_14_ = bf16[64,1280]{1,0:T(8,128)(2,1)S(1)} collective-permute-done((bf16[64,1280]{1,0:T(8,128)(2,1)S(1)}, bf16[64,1280]{1,0:T(8,128)(2,1)S(1)}, u32[]{:S(2)}, u32[]{:S(2)}) %collective-permute-start.29) | collective-permute-done | bytes 163872 | tf_op jit(solution)/shard_map/ppermute | solution.py:631
  131.2 7.1 %leave.1 = (bf16[512,1280]{1,0:T(8,128)(2,1)}, f32[2,512,128]{2,1,0:T(8,128)S(1)}, f32[20,512]{1,0:T(8,128)}) custom-call(s32[9]{0:T(128)S(1)} %pad_add_fusion.sources.refs_0_, f32[512,1280]{1,0:T(8,128)S(1)} %get-tuple-element.54.y_ref.refs_1_, bf16[512,1280]{1,0:T(8,128)(2,1)S(1)} %copy-done.19, f32[512,1280]{1,0:T(8,128)S(1)} %get-tuple-element.57.grad_y.refs_3_, ...), custom_call_target="tpu_custom_call" | custom-call | flops 5000000000 | bytes 20000000 | tf_op jit(solution)/shard_map/leave/pallas_call | solution.py:699
  138.4 4.5 %product.3 = (bf16[320,640]{1,0:T(8,128)(2,1)S(1)}, bf16[320,640]{1,0:T(8,128)(2,1)S(1)}, bf16[320,640]{1,0:T(8,128)(2,1)S(1)}, f32[320,640]{1,0:T(8,128)S(1)}) custom-call(s32[1]{0:T(128)} %bitcast.4.group, bf16[640,512]{1,0:T(8,128)(2,1)S(1)} %get-tuple-element.86.mine, bf16[640,512]{1,0:T(8,128)(2,1)S(1)} %collective-permute-done.35.theirs, ...), custom_call_target="tpu_custom_call" | custom-call | flops 1677721600 | bytes 5000000 | tf_op jit(solution)/shard_map/product/pallas_call | solution.py:748
  142.9 1.3 collective-permute-start.38
  144.9 1.4 collective-permute-start.41
  147.0 16.5 %collective-permute-done.32 = f32[8,1280]{1,0:T(8,128)S(1)} collective-permute-done((f32[8,1280]{1,0:T(8,128)S(1)}, f32[8,1280]{1,0:T(8,128)S(1)}, u32[]{:S(2)}, u32[]{:S(2)}) %collective-permute-start.32) | collective-permute-done | bytes 40992 | tf_op jit(solution)/shard_map/ppermute | solution.py:833
  163.5 2.4 %collective-permute-start.33 = (f32[8,1280]{1,0:T(8,128)S(1)}, f32[8,1280]{1,0:T(8,128)S(1)}, u32[]{:S(2)}, u32[]{:S(2)}) collective-permute-start(f32[8,1280]{1,0:T(8,128)S(1)} %add.70), channel_id=1, source_target_pairs={{0,16},{4,20},{8,24},{12,28},{16,0},{20,4},{24,8},{28,12},{1,17},{... | collective-permute-start | bytes 122888 | tf_op jit(solution)/shard_map/ppermute | solution.py:833
  165.9 2.5 %collective-permute-done.33 = f32[8,1280]{1,0:T(8,128)S(1)} collective-permute-done((f32[8,1280]{1,0:T(8,128)S(1)}, f32[8,1280]{1,0:T(8,128)S(1)}, u32[]{:S(2)}, u32[]{:S(2)}) %collective-permute-start.33) | collective-permute-done | bytes 40992 | tf_op jit(solution)/shard_map/ppermute | solution.py:833
  168.4 1.8 collective-permute-start.34
  170.2 2.4 %collective-permute-start.42 = (bf16[320,640]{1,0:T(8,128)(2,1)S(1)}, bf16[320,640]{1,0:T(8,128)(2,1)}, u32[]{:S(2)}, u32[]{:S(2)}) collective-permute-start(bf16[320,640]{1,0:T(8,128)(2,1)S(1)} %add_convert_fusion.1.refs_8_), channel_id=1, source_target_pairs={{0,16},{4,20},{8,24},{12,28},{16,0},{20,4},{24,8},{28,12},{1,17},{... | collective-permute-start | bytes 1228808 | tf_op jit(solution)/shard_map/ppermute | solution.py:855
  172.5 0.9 add.68
  174.0 0.9 add_convert_fusion
  176.3 2.4 %collective-permute-start.37 = (bf16[320,640]{1,0:T(8,128)(2,1)S(1)}, bf16[320,640]{1,0:T(8,128)(2,1)S(1)}, u32[]{:S(2)}, u32[]{:S(2)}) collective-permute-start(bf16[320,640]{1,0:T(8,128)(2,1)S(1)} %get-tuple-element.80), channel_id=1, source_target_pairs={{0,8},{4,12},{8,0},{12,4},{16,24},{20,28},{24,16},{28,20},{1,9},{5... | collective-permute-start | bytes 1228808 | tf_op jit(solution)/shard_map/ppermute | solution.py:855
  179.4 0.9 collective-permute-start.39
  181.6 12.7 %collective-permute-done.42.rest_2_ = bf16[320,640]{1,0:T(8,128)(2,1)} collective-permute-done((bf16[320,640]{1,0:T(8,128)(2,1)S(1)}, bf16[320,640]{1,0:T(8,128)(2,1)}, u32[]{:S(2)}, u32[]{:S(2)}) %collective-permute-start.42) | collective-permute-done | bytes 409632 | tf_op jit(solution)/shard_map/ppermute | solution.py:855
  194.3 1.0 copy-done.4
  195.3 1.0 copy-done.6
  196.3 1.1 copy-done.16
  197.5 2.1 finish.2.rest_3_
  199.5 16.5 %collective-permute-done.39.rest_2_ = bf16[320,640]{1,0:T(8,128)(2,1)S(1)} collective-permute-done((bf16[320,640]{1,0:T(8,128)(2,1)}, bf16[320,640]{1,0:T(8,128)(2,1)S(1)}, u32[]{:S(2)}, u32[]{:S(2)}) %collective-permute-start.39) | collective-permute-done | bytes 409632 | tf_op jit(solution)/shard_map/ppermute | solution.py:855
  216.1 1.1 finish.3
  217.1 1.3 add.69
  218.4 0.8 slice_bitcast_fusion
  (122 shorter events, 14.8 us)
Async XLA Ops:
  5.7 21.7 %collective-permute-start = (bf16[80,1280]{1,0:T(8,128)(2,1)}, bf16[80,1280]{1,0:T(8,128)(2,1)S(1)}, u32[]{:S(2)}, u32[]{:S(2)}) collective-permute-start(bf16[80,1280]{1,0:T(8,128)(2,1)} %get-tuple-element.50.rest_0_), channel_id=1, source_target_pairs={{0,8},{8,16},{16,24},{24,28},{28,20},{20,12},{12,4},{4,0},{1,9},{9... | collective-permute-start | bytes 614408 | tf_op jit(solution)/shard_map/ppermute | solution.py:807
  8.8 20.2 %collective-permute-start.1 = (bf16[80,1280]{1,0:T(8,128)(2,1)}, bf16[80,1280]{1,0:T(8,128)(2,1)S(1)}, u32[]{:S(2)}, u32[]{:S(2)}) collective-permute-start(bf16[80,1280]{1,0:T(8,128)(2,1)} %get-tuple-element.50.rest_0_), channel_id=1, source_target_pairs={{8,0},{16,8},{24,16},{28,24},{20,28},{12,20},{4,12},{0,4},{9,1},{1... | collective-permute-start | bytes 614408 | tf_op jit(solution)/shard_map/ppermute | solution.py:808
  8.8 16.6 %collective-permute-start.2 = (bf16[64,1280]{1,0:T(8,128)(2,1)}, bf16[64,1280]{1,0:T(8,128)(2,1)S(1)}, u32[]{:S(2)}, u32[]{:S(2)}) collective-permute-start(bf16[64,1280]{1,0:T(8,128)(2,1)} %get-tuple-element.51.rest_8_), channel_id=1, source_target_pairs={{0,8},{8,16},{16,24},{24,28},{28,20},{20,12},{12,4},{4,0},{1,9},{9... | collective-permute-start | bytes 491528 | tf_op jit(solution)/shard_map/ppermute | solution.py:807
  10.8 16.1 %collective-permute-start.3 = (bf16[64,1280]{1,0:T(8,128)(2,1)}, bf16[64,1280]{1,0:T(8,128)(2,1)S(1)}, u32[]{:S(2)}, u32[]{:S(2)}) collective-permute-start(bf16[64,1280]{1,0:T(8,128)(2,1)} %get-tuple-element.51.rest_8_), channel_id=1, source_target_pairs={{8,0},{16,8},{24,16},{28,24},{20,28},{12,20},{4,12},{0,4},{9,1},{1... | collective-permute-start | bytes 491528 | tf_op jit(solution)/shard_map/ppermute | solution.py:808
  10.8 33.7 %collective-permute-start.4 = (bf16[512,640]{1,0:T(8,128)(2,1)}, bf16[512,640]{1,0:T(8,128)(2,1)S(1)}, u32[]{:S(2)}, u32[]{:S(2)}) collective-permute-start(bf16[512,640]{1,0:T(8,128)(2,1)} %shard.1), channel_id=1, source_target_pairs={{0,2},{1,3},{2,0},{3,1},{4,6},{5,7},{6,4},{7,5},{8,10},{9,11},{10,... | collective-permute-start | bytes 1966088 | tf_op jit(solution)/shard_map/ppermute | solution.py:843
  12.8 1.1 copy-start
  17.1 1.3 copy-start.18
  20.1 5.2 %copy-start.27 = (s32[4]{0:T(128)S(1)}, s32[4]{0:T(128)}, u32[]{:S(2)}) copy-start(s32[4]{0:T(128)} %constant.73.clone) | copy-start | bytes 52
  20.1 8.8 %copy-start.26 = (s32[8]{0:T(128)S(1)}, s32[8]{0:T(128)}, u32[]{:S(2)}) copy-start(s32[8]{0:T(128)} %constant.72.clone) | copy-start | bytes 100
  20.1 19.1 %copy-start.25 = (f32[1280]{0:T(1024)S(1)}, f32[1280]{0:T(1024)}, u32[]{:S(2)}) copy-start(f32[1280]{0:T(1024)} %param.19) | copy-start | bytes 15364
  20.1 19.2 %copy-start.1 = (bf16[512,640]{1,0:T(8,128)(2,1)S(1)}, bf16[512,640]{1,0:T(8,128)(2,1)}, u32[]{:S(2)}) copy-start(bf16[512,640]{1,0:T(8,128)(2,1)} %shard.1) | copy-start | bytes 1966084
  20.1 24.4 %copy-start.10 = (bf16[512,128]{1,0:T(8,128)(2,1)S(1)}, bf16[512,128]{1,0:T(8,128)(2,1)}, u32[]{:S(2)}) copy-start(bf16[512,128]{1,0:T(8,128)(2,1)} %read.11) | copy-start | bytes 393220
  20.1 24.4 %copy-start.12 = (bf16[512,128]{1,0:T(8,128)(2,1)S(1)}, bf16[512,128]{1,0:T(8,128)(2,1)}, u32[]{:S(2)}) copy-start(bf16[512,128]{1,0:T(8,128)(2,1)} %refs_5_.1) | copy-start | bytes 393220
  20.2 24.4 %copy-start.14 = (f32[512,128]{1,0:T(8,128)S(1)}, f32[512,128]{1,0:T(8,128)}, u32[]{:S(2)}) copy-start(f32[512,128]{1,0:T(8,128)} %get-tuple-element.46.seg_t.refs_6_) | copy-start | bytes 786436
  20.2 24.4 %copy-start.22 = (f32[128,512]{1,0:T(8,128)S(1)}, f32[128,512]{1,0:T(8,128)}, u32[]{:S(2)}) copy-start(f32[128,512]{1,0:T(8,128)} %get-tuple-element.47.seg) | copy-start | bytes 786436
  20.2 24.4 %copy-start.24 = (f32[8,1280]{1,0:T(8,128)S(1)}, f32[8,1280]{1,0:T(8,128)}, u32[]{:S(2)}) copy-start(f32[8,1280]{1,0:T(8,128)} %get-tuple-element.49.skip.refs_9_) | copy-start | bytes 122884
  25.3 14.0 %collective-permute-start.24 = (bf16[320,512]{1,0:T(8,128)(2,1)S(1)}, bf16[320,512]{1,0:T(8,128)(2,1)S(1)}, u32[]{:S(2)}, u32[]{:S(2)}) collective-permute-start(bf16[320,512]{1,0:T(8,128)(2,1)S(1)} %pick.1), channel_id=1, source_target_pairs={{0,4},{4,0},{8,12},{12,8},{16,20},{20,16},{24,28},{28,24},{1,5},{5... | collective-permute-start | bytes 983048 | tf_op jit(solution)/shard_map/ppermute | solution.py:889
  26.9 9.1 %collective-permute-start.10 = (bf16[64,1280]{1,0:T(8,128)(2,1)S(1)}, bf16[64,1280]{1,0:T(8,128)(2,1)S(1)}, u32[]{:S(2)}, u32[]{:S(2)}) collective-permute-start(bf16[64,1280]{1,0:T(8,128)(2,1)S(1)} %collective-permute-done.3.rest_4_.rest_10_), channel_id=1, source_target_pairs={{8,0},{16,8},{24,16},{28,24},{20,28},{12,20},{4,12},{0,4},{9,1},{1... | collective-permute-start | bytes 491528 | tf_op jit(solution)/shard_map/ppermute | solution.py:808
  27.4 11.7 %collective-permute-start.9 = (bf16[64,1280]{1,0:T(8,128)(2,1)S(1)}, bf16[64,1280]{1,0:T(8,128)(2,1)S(1)}, u32[]{:S(2)}, u32[]{:S(2)}) collective-permute-start(bf16[64,1280]{1,0:T(8,128)(2,1)S(1)} %collective-permute-done.2.rest_3_.rest_9_), channel_id=1, source_target_pairs={{0,8},{8,16},{16,24},{24,28},{28,20},{20,12},{12,4},{4,0},{1,9},{9... | collective-permute-start | bytes 491528 | tf_op jit(solution)/shard_map/ppermute | solution.py:807
  29.0 12.4 %collective-permute-start.7 = (bf16[80,1280]{1,0:T(8,128)(2,1)S(1)}, bf16[80,1280]{1,0:T(8,128)(2,1)S(1)}, u32[]{:S(2)}, u32[]{:S(2)}) collective-permute-start(bf16[80,1280]{1,0:T(8,128)(2,1)S(1)} %collective-permute-done.rest_1_), channel_id=1, source_target_pairs={{0,8},{8,16},{16,24},{24,28},{28,20},{20,12},{12,4},{4,0},{1,9},{9... | collective-permute-start | bytes 614408 | tf_op jit(solution)/shard_map/ppermute | solution.py:807
  36.0 6.3 %collective-permute-start.8 = (bf16[80,1280]{1,0:T(8,128)(2,1)S(1)}, bf16[80,1280]{1,0:T(8,128)(2,1)S(1)}, u32[]{:S(2)}, u32[]{:S(2)}) collective-permute-start(bf16[80,1280]{1,0:T(8,128)(2,1)S(1)} %collective-permute-done.1.rest_2_), channel_id=1, source_target_pairs={{8,0},{16,8},{24,16},{28,24},{20,28},{12,20},{4,12},{0,4},{9,1},{1... | collective-permute-start | bytes 614408 | tf_op jit(solution)/shard_map/ppermute | solution.py:808
  39.2 5.3 %collective-permute-start.15 = (bf16[64,1280]{1,0:T(8,128)(2,1)S(1)}, bf16[64,1280]{1,0:T(8,128)(2,1)S(1)}, u32[]{:S(2)}, u32[]{:S(2)}) collective-permute-start(bf16[64,1280]{1,0:T(8,128)(2,1)S(1)} %collective-permute-done.10.refs_10_.rest_12_), channel_id=1, source_target_pairs={{8,0},{16,8},{24,16},{28,24},{20,28},{12,20},{4,12},{0,4},{9,1},{1... | collective-permute-start | bytes 491528 | tf_op jit(solution)/shard_map/ppermute | solution.py:808
  39.2 15.7 %slice-start = ((s8[6553600]{0:T(1024)(128)(4,1)}), s8[4194304]{0:T(1024)(128)(4,1)S(1)}, s32[]{:S(2)}) async-start(s8[6553600]{0:T(1024)(128)(4,1)} %bitcast.12), calls=%async_computation | async-start | bytes 8388608
  39.3 15.7 %slice-start.1 = ((s8[6553600]{0:T(1024)(128)(4,1)}), s8[2359296]{0:T(1024)(128)(4,1)S(1)}, s32[]{:S(2)}) async-start(s8[6553600]{0:T(1024)(128)(4,1)} %bitcast.12), calls=%async_computation.1 | async-start | bytes 4718592
  39.3 13.0 %collective-permute-start.5 = (bf16[512,640]{1,0:T(8,128)(2,1)S(1)}, bf16[512,640]{1,0:T(8,128)(2,1)S(1)}, u32[]{:S(2)}, u32[]{:S(2)}) collective-permute-start(bf16[512,640]{1,0:T(8,128)(2,1)S(1)} %copy-done.1), channel_id=1, source_target_pairs={{0,1},{1,0},{2,3},{3,2},{4,5},{5,4},{6,7},{7,6},{8,9},{9,8},{10,11... | collective-permute-start | bytes 1966088 | tf_op jit(solution)/shard_map/ppermute | solution.py:843
  41.4 8.4 %collective-permute-start.14 = (bf16[64,1280]{1,0:T(8,128)(2,1)S(1)}, bf16[64,1280]{1,0:T(8,128)(2,1)S(1)}, u32[]{:S(2)}, u32[]{:S(2)}) collective-permute-start(bf16[64,1280]{1,0:T(8,128)(2,1)S(1)} %collective-permute-done.9.refs_9_.rest_11_), channel_id=1, source_target_pairs={{0,8},{8,16},{16,24},{24,28},{28,20},{20,12},{12,4},{4,0},{1,9},{9... | collective-permute-start | bytes 491528 | tf_op jit(solution)/shard_map/ppermute | solution.py:807
  42.3 12.6 %collective-permute-start.25 = (bf16[320,512]{1,0:T(8,128)(2,1)S(1)}, bf16[320,512]{1,0:T(8,128)(2,1)S(1)}, u32[]{:S(2)}, u32[]{:S(2)}) collective-permute-start(bf16[320,512]{1,0:T(8,128)(2,1)S(1)} %collective-permute-done.24.rest_0_), channel_id=1, source_target_pairs={{0,2},{1,3},{2,0},{3,1},{4,6},{5,7},{6,4},{7,5},{8,10},{9,11},{10,... | collective-permute-start | bytes 983048 | tf_op jit(solution)/shard_map/ppermute | solution.py:843
  44.5 6.0 %collective-permute-start.11 = (bf16[80,1280]{1,0:T(8,128)(2,1)S(1)}, bf16[80,1280]{1,0:T(8,128)(2,1)S(1)}, u32[]{:S(2)}, u32[]{:S(2)}) collective-permute-start(bf16[80,1280]{1,0:T(8,128)(2,1)S(1)} %collective-permute-done.7.refs_7_.rest_3_), channel_id=1, source_target_pairs={{0,8},{8,16},{16,24},{24,28},{28,20},{20,12},{12,4},{4,0},{1,9},{9... | collective-permute-start | bytes 614408 | tf_op jit(solution)/shard_map/ppermute | solution.py:807
  44.5 10.4 %collective-permute-start.6 = (bf16[512,640]{1,0:T(8,128)(2,1)S(1)}, bf16[512,640]{1,0:T(8,128)(2,1)S(1)}, u32[]{:S(2)}, u32[]{:S(2)}) collective-permute-start(bf16[512,640]{1,0:T(8,128)(2,1)S(1)} %collective-permute-done.4.refs_3_), channel_id=1, source_target_pairs={{0,1},{1,0},{2,3},{3,2},{4,5},{5,4},{6,7},{7,6},{8,9},{9,8},{10,11... | collective-permute-start | bytes 1966088 | tf_op jit(solution)/shard_map/ppermute | solution.py:843
  49.7 13.0 %copy-start.2 = (bf16[512,1280]{1,0:T(8,128)(2,1)S(1)}, bf16[512,1280]{1,0:T(8,128)(2,1)}, u32[]{:S(2)}) copy-start(bf16[512,1280]{1,0:T(8,128)(2,1)} %gate.3) | copy-start | bytes 3932164
  49.7 13.0 %copy-start.7 = (bf16[80,1280]{1,0:T(8,128)(2,1)S(1)}, bf16[80,1280]{1,0:T(8,128)(2,1)}, u32[]{:S(2)}) copy-start(bf16[80,1280]{1,0:T(8,128)(2,1)} %get-tuple-element.50.rest_0_) | copy-start | bytes 614404
  49.7 13.0 %copy-start.8 = (bf16[64,1280]{1,0:T(8,128)(2,1)S(1)}, bf16[64,1280]{1,0:T(8,128)(2,1)}, u32[]{:S(2)}) copy-start(bf16[64,1280]{1,0:T(8,128)(2,1)} %get-tuple-element.51.rest_8_) | copy-start | bytes 491524
  49.7 13.0 %copy-start.17 = (bf16[256,1280]{1,0:T(8,128)(2,1)S(1)}, bf16[256,1280]{1,0:T(8,128)(2,1)}, u32[]{:S(2)}) copy-start(bf16[256,1280]{1,0:T(8,128)(2,1)} %get-tuple-element.53.spread2.refs_8_) | copy-start | bytes 1966084
  49.7 19.9 %collective-permute-start.26 = (bf16[320,512]{1,0:T(8,128)(2,1)S(1)}, bf16[320,512]{1,0:T(8,128)(2,1)S(1)}, u32[]{:S(2)}, u32[]{:S(2)}) collective-permute-start(bf16[320,512]{1,0:T(8,128)(2,1)S(1)} %collective-permute-done.24.rest_0_), channel_id=1, source_target_pairs={{0,1},{1,0},{2,3},{3,2},{4,5},{5,4},{6,7},{7,6},{8,9},{9,8},{10,11... | collective-permute-start | bytes 983048 | tf_op jit(solution)/shard_map/ppermute | solution.py:843
  50.5 11.5 %collective-permute-start.12 = (bf16[80,1280]{1,0:T(8,128)(2,1)S(1)}, bf16[80,1280]{1,0:T(8,128)(2,1)S(1)}, u32[]{:S(2)}, u32[]{:S(2)}) collective-permute-start(bf16[80,1280]{1,0:T(8,128)(2,1)S(1)} %collective-permute-done.8.refs_8_.rest_4_), channel_id=1, source_target_pairs={{8,0},{16,8},{24,16},{28,24},{20,28},{12,20},{4,12},{0,4},{9,1},{1... | collective-permute-start | bytes 614408 | tf_op jit(solution)/shard_map/ppermute | solution.py:808
  52.3 10.3 %collective-permute-start.16 = (bf16[64,1280]{1,0:T(8,128)(2,1)S(1)}, bf16[64,1280]{1,0:T(8,128)(2,1)S(1)}, u32[]{:S(2)}, u32[]{:S(2)}) collective-permute-start(bf16[64,1280]{1,0:T(8,128)(2,1)S(1)} %collective-permute-done.15.rest_14_), channel_id=1, source_target_pairs={{8,0},{16,8},{24,16},{28,24},{20,28},{12,20},{4,12},{0,4},{9,1},{1... | collective-permute-start | bytes 491528 | tf_op jit(solution)/shard_map/ppermute | solution.py:808
  54.9 7.8 %collective-permute-start.13 = (bf16[80,1280]{1,0:T(8,128)(2,1)S(1)}, bf16[80,1280]{1,0:T(8,128)(2,1)S(1)}, u32[]{:S(2)}, u32[]{:S(2)}) collective-permute-start(bf16[80,1280]{1,0:T(8,128)(2,1)S(1)} %collective-permute-done.11.rest_5_), channel_id=1, source_target_pairs={{0,8},{8,16},{16,24},{24,28},{28,20},{20,12},{12,4},{4,0},{1,9},{9... | collective-permute-start | bytes 614408 | tf_op jit(solution)/shard_map/ppermute | solution.py:807
  54.9 14.7 %collective-permute-start.27 = (bf16[320,512]{1,0:T(8,128)(2,1)S(1)}, bf16[320,512]{1,0:T(8,128)(2,1)S(1)}, u32[]{:S(2)}, u32[]{:S(2)}) collective-permute-start(bf16[320,512]{1,0:T(8,128)(2,1)S(1)} %collective-permute-done.25.rest_1_), channel_id=1, source_target_pairs={{0,1},{1,0},{2,3},{3,2},{4,5},{5,4},{6,7},{7,6},{8,9},{9,8},{10,11... | collective-permute-start | bytes 983048 | tf_op jit(solution)/shard_map/ppermute | solution.py:843
  67.8 1.2 collective-permute-start.17
  69.1 3.7 %collective-permute-start.18 = (f32[8,512]{1,0:T(8,128)S(1)}, f32[8,512]{1,0:T(8,128)S(1)}, u32[]{:S(2)}, u32[]{:S(2)}) collective-permute-start(f32[8,512]{1,0:T(8,128)S(1)} %add.63), channel_id=1, source_target_pairs={{0,2},{1,3},{2,0},{3,1},{4,6},{5,7},{6,4},{7,5},{8,10},{9,11},{10,... | collective-permute-start | bytes 49160 | tf_op jit(solution)/shard_map/ppermute | solution.py:833
  72.8 2.5 %copy-start.19 = (bf16[512,1280]{1,0:T(8,128)(2,1)S(1)}, bf16[512,1280]{1,0:T(8,128)(2,1)}, u32[]{:S(2)}) copy-start(bf16[512,1280]{1,0:T(8,128)(2,1)} %get-tuple-element.48.x.refs_2_) | copy-start | bytes 3932164
  72.9 2.5 %copy-start.20 = (bf16[128,512]{1,0:T(8,128)(2,1)S(1)}, bf16[128,512]{1,0:T(8,128)(2,1)}, u32[]{:S(2)}) copy-start(bf16[128,512]{1,0:T(8,128)(2,1)} %get-tuple-element.56.read_t) | copy-start | bytes 393220
  73.2 17.7 %collective-permute-start.23 = (bf16[640,512]{1,0:T(8,128)(2,1)S(1)}, bf16[640,512]{1,0:T(8,128)(2,1)S(1)}, u32[]{:S(2)}, u32[]{:S(2)}) collective-permute-start(bf16[640,512]{1,0:T(8,128)(2,1)S(1)} %get-tuple-element.87.mine), channel_id=1, source_target_pairs={{0,4},{4,0},{8,12},{12,8},{16,20},{20,16},{24,28},{28,24},{1,5},{5... | collective-permute-start | bytes 1966088 | tf_op jit(solution)/shard_map/ppermute | solution.py:919
  74.8 63.6 %collective-permute-start.35 = (bf16[640,512]{1,0:T(8,128)(2,1)S(1)}, bf16[640,512]{1,0:T(8,128)(2,1)S(1)}, u32[]{:S(2)}, u32[]{:S(2)}) collective-permute-start(bf16[640,512]{1,0:T(8,128)(2,1)S(1)} %get-tuple-element.86.mine), channel_id=1, source_target_pairs={{0,4},{4,0},{8,12},{12,8},{16,20},{20,16},{24,28},{28,24},{1,5},{5... | collective-permute-start | bytes 1966088 | tf_op jit(solution)/shard_map/ppermute | solution.py:919
  81.0 25.5 %collective-permute-start.19 = (bf16[64,1280]{1,0:T(8,128)(2,1)S(1)}, bf16[64,1280]{1,0:T(8,128)(2,1)S(1)}, u32[]{:S(2)}, u32[]{:S(2)}) collective-permute-start(bf16[64,1280]{1,0:T(8,128)(2,1)S(1)} %get-tuple-element.66), channel_id=1, source_target_pairs={{0,4},{4,0},{8,12},{12,8},{16,20},{20,16},{24,28},{28,24},{1,5},{5... | collective-permute-start | bytes 491528 | tf_op jit(solution)/shard_map/ppermute | solution.py:614
  96.4 14.9 %collective-permute-start.28 = (bf16[320,640]{1,0:T(8,128)(2,1)S(1)}, bf16[320,640]{1,0:T(8,128)(2,1)S(1)}, u32[]{:S(2)}, u32[]{:S(2)}) collective-permute-start(bf16[320,640]{1,0:T(8,128)(2,1)S(1)} %get-tuple-element.70), channel_id=1, source_target_pairs={{0,8},{4,12},{24,16},{28,20},{1,9},{5,13},{25,17},{29,21},{2,10},{... | collective-permute-start | bytes 1228808 | tf_op jit(solution)/shard_map/ppermute | solution.py:855
  107.2 8.5 %collective-permute-start.20 = (bf16[64,1280]{1,0:T(8,128)(2,1)S(1)}, bf16[64,1280]{1,0:T(8,128)(2,1)S(1)}, u32[]{:S(2)}, u32[]{:S(2)}) collective-permute-start(bf16[64,1280]{1,0:T(8,128)(2,1)S(1)} %shard_map.179), channel_id=1, source_target_pairs={{8,0},{12,4},{16,8},{20,12},{24,16},{28,20},{9,1},{13,5},{17,9},{2... | collective-permute-start | bytes 491528 | tf_op jit(solution)/shard_map/ppermute | solution.py:620
  108.5 16.6 %collective-permute-start.21 = (bf16[64,1280]{1,0:T(8,128)(2,1)S(1)}, bf16[64,1280]{1,0:T(8,128)(2,1)S(1)}, u32[]{:S(2)}, u32[]{:S(2)}) collective-permute-start(bf16[64,1280]{1,0:T(8,128)(2,1)S(1)} %shard_map.179), channel_id=1, source_target_pairs={{16,0},{20,4},{24,8},{28,12},{17,1},{21,5},{25,9},{29,13},{18,2},{... | collective-permute-start | bytes 491528 | tf_op jit(solution)/shard_map/ppermute | solution.py:620
  109.8 15.3 %collective-permute-start.22 = (bf16[64,1280]{1,0:T(8,128)(2,1)S(1)}, bf16[64,1280]{1,0:T(8,128)(2,1)S(1)}, u32[]{:S(2)}, u32[]{:S(2)}) collective-permute-start(bf16[64,1280]{1,0:T(8,128)(2,1)S(1)} %shard_map.179), channel_id=1, source_target_pairs={{24,0},{28,4},{25,1},{29,5},{26,2},{30,6},{27,3},{31,7}} | collective-permute-start | bytes 491528 | tf_op jit(solution)/shard_map/ppermute | solution.py:620
  125.8 5.4 %collective-permute-start.29 = (bf16[64,1280]{1,0:T(8,128)(2,1)S(1)}, bf16[64,1280]{1,0:T(8,128)(2,1)S(1)}, u32[]{:S(2)}, u32[]{:S(2)}) collective-permute-start(bf16[64,1280]{1,0:T(8,128)(2,1)S(1)} %get-tuple-element.72), channel_id=1, source_target_pairs={{0,4},{4,0},{8,12},{12,8},{16,20},{20,16},{24,28},{28,24},{1,5},{5... | collective-permute-start | bytes 491528 | tf_op jit(solution)/shard_map/ppermute | solution.py:631
  138.4 31.8 %collective-permute-start.30 = (f32[2,512,128]{2,1,0:T(8,128)S(1)}, f32[2,512,128]{2,1,0:T(8,128)S(1)}, u32[]{:S(2)}, u32[]{:S(2)}) collective-permute-start(f32[2,512,128]{2,1,0:T(8,128)S(1)} %get-tuple-element.75), channel_id=1, source_target_pairs={{0,1},{1,0},{2,3},{3,2},{4,5},{5,4},{6,7},{7,6},{8,9},{9,8},{10,11... | collective-permute-start | bytes 1572872 | tf_op jit(solution)/shard_map/ppermute | solution.py:833
  142.9 30.5 %collective-permute-start.38 = (bf16[320,640]{1,0:T(8,128)(2,1)S(1)}, bf16[320,640]{1,0:T(8,128)(2,1)S(1)}, u32[]{:S(2)}, u32[]{:S(2)}) collective-permute-start(bf16[320,640]{1,0:T(8,128)(2,1)S(1)} %get-tuple-element.79), channel_id=1, source_target_pairs={{0,8},{4,12},{24,16},{28,20},{1,9},{5,13},{25,17},{29,21},{2,10},{... | collective-permute-start | bytes 1228808 | tf_op jit(solution)/shard_map/ppermute | solution.py:855
  144.2 31.3 %collective-permute-start.40 = (bf16[320,640]{1,0:T(8,128)(2,1)S(1)}, bf16[320,640]{1,0:T(8,128)(2,1)S(1)}, u32[]{:S(2)}, u32[]{:S(2)}) collective-permute-start(bf16[320,640]{1,0:T(8,128)(2,1)S(1)} %get-tuple-element.70), channel_id=1, source_target_pairs={{8,16},{12,20},{16,8},{20,12},{9,17},{13,21},{17,9},{21,13},{10,18... | collective-permute-start | bytes 1228808 | tf_op jit(solution)/shard_map/ppermute | solution.py:855
  144.9 33.7 %collective-permute-start.41 = (bf16[320,640]{1,0:T(8,128)(2,1)S(1)}, bf16[320,640]{1,0:T(8,128)(2,1)S(1)}, u32[]{:S(2)}, u32[]{:S(2)}) collective-permute-start(bf16[320,640]{1,0:T(8,128)(2,1)S(1)} %get-tuple-element.83), channel_id=1, source_target_pairs={{0,8},{4,12},{8,0},{12,4},{16,24},{20,28},{24,16},{28,20},{1,9},{5... | collective-permute-start | bytes 1228808 | tf_op jit(solution)/shard_map/ppermute | solution.py:855
  146.3 17.2 %collective-permute-start.32 = (f32[8,1280]{1,0:T(8,128)S(1)}, f32[8,1280]{1,0:T(8,128)S(1)}, u32[]{:S(2)}, u32[]{:S(2)}) collective-permute-start(f32[8,1280]{1,0:T(8,128)S(1)} %get-tuple-element.77), channel_id=1, source_target_pairs={{0,8},{4,12},{8,0},{12,4},{16,24},{20,28},{24,16},{28,20},{1,9},{5... | collective-permute-start | bytes 122888 | tf_op jit(solution)/shard_map/ppermute | solution.py:833
  163.5 4.9 %collective-permute-start.33 = (f32[8,1280]{1,0:T(8,128)S(1)}, f32[8,1280]{1,0:T(8,128)S(1)}, u32[]{:S(2)}, u32[]{:S(2)}) collective-permute-start(f32[8,1280]{1,0:T(8,128)S(1)} %add.70), channel_id=1, source_target_pairs={{0,16},{4,20},{8,24},{12,28},{16,0},{20,4},{24,8},{28,12},{1,17},{... | collective-permute-start | bytes 122888 | tf_op jit(solution)/shard_map/ppermute | solution.py:833
  168.4 6.4 %collective-permute-start.34 = (f32[8,1280]{1,0:T(8,128)S(1)}, f32[8,1280]{1,0:T(8,128)S(1)}, u32[]{:S(2)}, u32[]{:S(2)}) collective-permute-start(f32[8,1280]{1,0:T(8,128)S(1)} %add.71), channel_id=1, source_target_pairs={{0,4},{4,0},{8,12},{12,8},{16,20},{20,16},{24,28},{28,24},{1,5},{5... | collective-permute-start | bytes 122888 | tf_op jit(solution)/shard_map/ppermute | solution.py:833
  170.2 24.1 %collective-permute-start.42 = (bf16[320,640]{1,0:T(8,128)(2,1)S(1)}, bf16[320,640]{1,0:T(8,128)(2,1)}, u32[]{:S(2)}, u32[]{:S(2)}) collective-permute-start(bf16[320,640]{1,0:T(8,128)(2,1)S(1)} %add_convert_fusion.1.refs_8_), channel_id=1, source_target_pairs={{0,16},{4,20},{8,24},{12,28},{16,0},{20,4},{24,8},{28,12},{1,17},{... | collective-permute-start | bytes 1228808 | tf_op jit(solution)/shard_map/ppermute | solution.py:855
  173.5 43.7 %collective-permute-start.31 = (f32[2,512,128]{2,1,0:T(8,128)}, f32[2,512,128]{2,1,0:T(8,128)}, u32[]{:S(2)}, u32[]{:S(2)}) collective-permute-start(f32[2,512,128]{2,1,0:T(8,128)} %add.68), channel_id=1, source_target_pairs={{0,2},{1,3},{2,0},{3,1},{4,6},{5,7},{6,4},{7,5},{8,10},{9,11},{10,... | collective-permute-start | bytes 1572872 | tf_op jit(solution)/shard_map/ppermute | solution.py:833
  174.8 24.7 %collective-permute-start.36 = (bf16[320,640]{1,0:T(8,128)(2,1)S(1)}, bf16[320,640]{1,0:T(8,128)(2,1)S(1)}, u32[]{:S(2)}, u32[]{:S(2)}) collective-permute-start(bf16[320,640]{1,0:T(8,128)(2,1)S(1)} %get-tuple-element.79), channel_id=1, source_target_pairs={{8,16},{12,20},{16,8},{20,12},{9,17},{13,21},{17,9},{21,13},{10,18... | collective-permute-start | bytes 1228808 | tf_op jit(solution)/shard_map/ppermute | solution.py:855
  176.3 23.2 %collective-permute-start.37 = (bf16[320,640]{1,0:T(8,128)(2,1)S(1)}, bf16[320,640]{1,0:T(8,128)(2,1)S(1)}, u32[]{:S(2)}, u32[]{:S(2)}) collective-permute-start(bf16[320,640]{1,0:T(8,128)(2,1)S(1)} %get-tuple-element.80), channel_id=1, source_target_pairs={{0,8},{4,12},{8,0},{12,4},{16,24},{20,28},{24,16},{28,20},{1,9},{5... | collective-permute-start | bytes 1228808 | tf_op jit(solution)/shard_map/ppermute | solution.py:855
  179.4 36.7 %collective-permute-start.39 = (bf16[320,640]{1,0:T(8,128)(2,1)}, bf16[320,640]{1,0:T(8,128)(2,1)S(1)}, u32[]{:S(2)}, u32[]{:S(2)}) collective-permute-start(bf16[320,640]{1,0:T(8,128)(2,1)} %add_convert_fusion), channel_id=1, source_target_pairs={{0,16},{4,20},{8,24},{12,28},{16,0},{20,4},{24,8},{28,12},{1,17},{... | collective-permute-start | bytes 1228808 | tf_op jit(solution)/shard_map/ppermute | solution.py:855
  194.3 1.0 copy-start.4
  196.3 1.1 copy-start.16
  (9 other events, 7.9 us)

commit v4 on v3

--- a/solution.py
+++ b/solution.py
@@ -11,7 +11,6 @@
 LANES = 128
 EXTRA = 16
 EPSILON = 1e-05
-NORMED_PARTS = 2
 HALF = LANES // 2
 
 
@@ -276,6 +275,8 @@
     column = pl.BlockSpec((length, LANES), lambda j: (0, j + start))
     share = (stop - start) / (width // LANES)
     operands = (seg_t, seg, write, read, x, skip)
+    if held is None:
+        operands = tuple(pltpu.with_memory_space_constraint(v, pltpu.HBM) for v in operands)
     specs = [
         whole((length, LANES)), whole((LANES, length)), whole(write.shape), whole(read.shape),
         column, pl.BlockSpec((8, LANES), lambda j: (0, j + start)),
@@ -743,7 +744,7 @@
     rows, length = mine.shape
     groups, columns, _ = cot_mine.shape
     masks = list(range(groups - 1, -1, -1))
-    block = LANES if rows % LANES == 0 else rows
+    block = 2 * LANES if rows % (2 * LANES) == 0 else LANES
     side = pl.BlockSpec((block, length), lambda i, *_: (i, 0))
     return pl.pallas_call(
         functools.partial(product_kernel, masks),
@@ -769,12 +770,10 @@
     rest[-1][...] = total
 
 
-def finish(part, parts, own, received, held):
+def finish(start, width, own, received, held):
     columns, rows = own.shape
-    if rows % LANES:
-        total = own + sum(piece.astype(F32) for piece in received)
-        return total if held is None else jnp.concatenate([held, total], axis=1)
-    small = pl.BlockSpec((columns, rows), lambda i: (0, 0))
+    block = 2 * LANES if rows % (2 * LANES) == 0 and start % (2 * LANES) == 0 else LANES
+    small = pl.BlockSpec((columns, block), lambda i: (0, i))
     operands = [own, *received]
     specs = [small] * len(operands)
     aliases = {}
@@ -785,10 +784,10 @@
     return pl.pallas_call(
         functools.partial(finish_kernel, len(received)),
         name="finish",
-        grid=(1,),
+        grid=(rows // block,),
         in_specs=specs,
-        out_specs=pl.BlockSpec((columns, rows), lambda i: (0, part)),
-        out_shape=jax.ShapeDtypeStruct((columns, parts * rows), F32),
+        out_specs=pl.BlockSpec((columns, block), lambda i: (0, start // block + i)),
+        out_shape=jax.ShapeDtypeStruct((columns, width), F32),
         input_output_aliases=aliases,
         compiler_params=params(),
         cost_estimate=cost(1e9, 4e6),
@@ -804,12 +803,18 @@
     up = down = [near, far]
     for hop in range(1, half + 1):
         last = hop == half
-        up = [lax.ppermute(v, "seq", ahead) for v in (up[:1] if last else up)]
-        down = [lax.ppermute(v, "seq", behind) for v in (down[1:] if last else down)]
+
+        def move(value, moves):
+            return lax.ppermute(value, "seq", moves)
+
+        up = [move(up[0], ahead)] + ([] if last else [move(up[1], ahead)])
+        down = ([] if last else [move(down[0], behind)]) + [move(down[1], behind)]
+        if last:
+            down = [None] + down[-1:]
         shifts.append(-hop)
         all_near.append(up[0])
         if last:
-            all_far.append(down[0])
+            all_far.append(down[1])
         else:
             all_far.append(up[1])
             shifts.append(hop)
@@ -911,10 +916,12 @@
     )
     stats = butterfly_sum(stats, "tp", tp_size)
     scale = lax.rsqrt(stats[0:1, :] / total_width + EPSILON)
-    part_rows = width // NORMED_PARTS
+    first = (2 * width // 5) // LANES * LANES
+    bounds = (0, first, width)
+    parts = len(bounds) - 1
     normed, normed_theirs = [], []
-    for part in range(NORMED_PARTS):
-        rows = scaled_t[part * part_rows : (part + 1) * part_rows]
+    for part in range(parts):
+        rows = scaled_t[bounds[part] : bounds[part + 1]]
         normed.append((rows * scale).astype(BF16))
         normed_theirs.append(lax.ppermute(normed[part], "seq", partner))
 
@@ -928,7 +935,7 @@
     inner, write_part, read_part = inside_back(heads, middle, pairs, *operands, inner, grad_cross)
     group = (lax.axis_index("seq") // 2)[None].astype(jnp.int32)
     arrived, own_part, merges = [], [], []
-    for part in range(NORMED_PARTS):
+    for part in range(parts):
         *pieces, last = products(group, normed[part], normed_theirs[part], cot_mine, cot_theirs)
         got, merged = send_products(pieces, seq_size)
         arrived.append(got)
@@ -942,8 +949,10 @@
         write_part, read_part, own, other, (),
     )
     grad_out_weight = None
-    for part in range(NORMED_PARTS):
-        grad_out_weight = finish(part, NORMED_PARTS, own_part[part], arrived[part], grad_out_weight)
+    for part in range(parts):
+        grad_out_weight = finish(
+            bounds[part], width, own_part[part], arrived[part], grad_out_weight
+        )
     maps = butterfly_sum(maps, "tp", tp_size)
     sums = butterfly_sum(sums, "seq", seq_size, 2)
     grad_skip = jnp.sum(sums[1].reshape(heads, width // heads), axis=1)

time: 220 us -> 205 us (0.932)
  starting transfers between devices: 49.2 us -> 41.8 us
  local copies, waits for them, and re-layouts: 14 us -> 8.07 us
    ppermute x8, waiting for transfers between devices: 29.3 us -> 40.8 us  [move(): return lax.ppermute(value, 'seq', pairs)]
    ppermute x7, waiting for transfers between devices: 22.8 us -> 12.4 us  [butterfly_sum(): lax.ppermute(value, axis, [(i, i ^ stride) for i in range(size)])]
    unnamed x60 -> x48, local copies, waits for them, and re-layouts: 12.5 us -> 6.55 us
    ppermute x1, waiting for transfers between devices: 0.85 us -> 6.49 us  [pair_state(): received = lax.ppermute(send, 'seq', partner)]
    pallas_call x2, Pallas kernels: 9.05 us -> 5.31 us  [products(): pl.pallas_call(functools.partial(product_kernel, masks), name='product',...]
    ppermute x1, waiting for transfers between devices: 3.54 us -> 0.01 us  [join_states(): return (own, lax.ppermute(other, 'seq', [(i, i ^ 1) for i in range(size)]))]
    ppermute x7, starting transfers between devices: 5.95 us -> 2.74 us  [butterfly_sum(): lax.ppermute(value, axis, [(i, i ^ stride) for i in range(size)])]
    ppermute x8, starting transfers between devices: 13.3 us -> 10.7 us  [move(): return lax.ppermute(value, 'seq', pairs)]
  transfers between devices with their start and end apart: 43 -> 43, of which waited for: 18 -> 16; matrix products, arithmetic and copies ran while one was open for 2% -> 2% of each run, Pallas kernels for 27% -> 28%
where the time goes in v4:
time: 205 us
  waiting for transfers between devices  85.9 us (42%)
  Pallas kernels  63.4 us (31%)
  starting transfers between devices  41.8 us (20%)
  local copies, waits for them, and re-layouts  8.07 us (4%)
  other arithmetic  4.31 us (2%)
    ppermute x8, waiting for transfers between devices, move(): return lax.ppermute(value, 'seq', pairs)  40.8 us
    ppermute x14, starting transfers between devices, move(): return lax.ppermute(value, 'seq', moves)  16.8 us
    ppermute x3, waiting for transfers between devices, pair_state(): later.append(lax.ppermute(pair, 'seq', moves))  13.7 us
    ppermute x7, waiting for transfers between devices, butterfly_sum(): lax.ppermute(value, axis, [(i, i ^ stride) for i in range(size)])  12.4 us
    pallas_call x2, Pallas kernels, inside(): pl.pallas_call(functools.partial(inside_kernel, width // heads, start), n...  11.5 us
    ppermute x8, starting transfers between devices, move(): return lax.ppermute(value, 'seq', pairs)  10.7 us
    ppermute x14, waiting for transfers between devices, move(): return lax.ppermute(value, 'seq', moves)  10.6 us
    pallas_call x2, Pallas kernels, inside_back(): pl.pallas_call(functools.partial(inside_back_kernel, width // heads, star...  10.6 us
  transfers between devices with their start and end apart: 43, of which 16 were waited for; matrix products, arithmetic and copies ran while one was open for 2% of the time, Pallas kernels for 28%

profile of v4, /device:TPU:0, one launch (start us, length us, event | category | flops | bytes accessed | tf_op | source)
XLA Modules:
  0.0 204.6 jit_solution(1050555106150276474)
XLA Ops:
  0.6 5.1 %prepare.1 = (bf16[512,1280]{1,0:T(8,128)(2,1)}, bf16[80,1280]{1,0:T(8,128)(2,1)}, bf16[64,1280]{1,0:T(8,128)(2,1)}, f32[512,128]{1,0:T(8,128)}, f32[128,512]{1,...) custom-call(s32[64,1280]{1,0:T(8,128)} %packed.1, s32[10,512]{1,0:T(8,128)} %expo.1, ...), custom_call_target="tpu_custom_call" | custom-call | flops 3000000000 | bytes 8000000 | tf_op jit(solution)/shard_map/prepare/pallas_call | solution.py:121
  5.7 3.1 %collective-permute-start = (bf16[80,1280]{1,0:T(8,128)(2,1)}, bf16[80,1280]{1,0:T(8,128)(2,1)S(1)}, u32[]{:S(2)}, u32[]{:S(2)}) collective-permute-start(bf16[80,1280]{1,0:T(8,128)(2,1)} %get-tuple-element.50.rest_0_), channel_id=1, source_target_pairs={{0,8},{8,16},{16,24},{24,28},{28,20},{20,12},{12,4},{4,0},{1,9},{9... | collective-permute-start | bytes 614408 | tf_op jit(solution)/shard_map/ppermute | solution.py:808
  8.8 2.0 collective-permute-start.2
  10.8 2.0 collective-permute-start.4
  12.8 1.1 copy-done
  14.4 6.4 %inside.2.rest_0_ = f32[512,1280]{1,0:T(8,128)S(1)} custom-call(f32[512,128]{1,0:T(8,128)} %get-tuple-element.46.seg_t.refs_6_, f32[128,512]{1,0:T(8,128)} %get-tuple-element.47.seg, bf16[512,128]{1,0:T(8,128)(2,1)} %refs_5_.1, bf16[512,128]{1,0:T(8,128)(2,1)} %read.11, bf16[512,1280]{1,0:T(8,128)(2,1)} %get-tuple-element.48.x.refs_2_, ...), custom_call_target="tpu_custom_call" | custom-call | flops 10000000000 | bytes 2500000 | tf_op jit(solution)/shard_map/inside/pallas_call | solution.py:291
  20.9 1.6 collective-permute-start.24
  23.0 1.5 collective-permute-start.9
  24.6 1.6 collective-permute-start.7
  26.1 5.4 %collective-permute-done.10.refs_10_.rest_12_ = bf16[64,1280]{1,0:T(8,128)(2,1)S(1)} collective-permute-done((bf16[64,1280]{1,0:T(8,128)(2,1)S(1)}, bf16[64,1280]{1,0:T(8,128)(2,1)S(1)}, u32[]{:S(2)}, u32[]{:S(2)}) %collective-permute-start.10) | collective-permute-done | bytes 163872 | tf_op jit(solution)/shard_map/ppermute | solution.py:808
  31.5 2.5 %collective-permute-start.8 = (bf16[80,1280]{1,0:T(8,128)(2,1)S(1)}, bf16[80,1280]{1,0:T(8,128)(2,1)S(1)}, u32[]{:S(2)}, u32[]{:S(2)}) collective-permute-start(bf16[80,1280]{1,0:T(8,128)(2,1)S(1)} %collective-permute-done.1.rest_2_), channel_id=1, source_target_pairs={{8,0},{16,8},{24,16},{28,24},{20,28},{12,20},{4,12},{0,4},{9,1},{1... | collective-permute-start | bytes 614408 | tf_op jit(solution)/shard_map/ppermute | solution.py:808
  34.8 2.1 %collective-permute-done.7.refs_7_.rest_3_ = bf16[80,1280]{1,0:T(8,128)(2,1)S(1)} collective-permute-done((bf16[80,1280]{1,0:T(8,128)(2,1)S(1)}, bf16[80,1280]{1,0:T(8,128)(2,1)S(1)}, u32[]{:S(2)}, u32[]{:S(2)}) %collective-permute-start.7) | collective-permute-done | bytes 204832 | tf_op jit(solution)/shard_map/ppermute | solution.py:808
  37.2 1.7 collective-permute-done.8.refs_8_.rest_4_
  39.0 5.1 %inside.3.refs_6_.y_local = f32[512,1280]{1,0:T(8,128)S(1)} custom-call(f32[512,128]{1,0:T(8,128)S(1)} %copy-done.11, f32[128,512]{1,0:T(8,128)S(1)} %copy-done.17, bf16[512,128]{1,0:T(8,128)(2,1)S(1)} %copy-done.10, bf16[512,128]{1,0:T(8,128)(2,1)S(1)} %copy-done.9, bf16[512,1280]{1,0:T(8,128)(2,1)S(1)} %copy-done.15, ...), custom_call_target="tpu_custom_call", output_to_operand_aliasing={{}: (6, {})} | custom-call | flops 10000000000 | bytes 2500000 | tf_op jit(solution)/shard_map/inside/pallas_call | solution.py:291
  44.2 3.2 %collective-permute-start.14 = (bf16[64,1280]{1,0:T(8,128)(2,1)S(1)}, bf16[64,1280]{1,0:T(8,128)(2,1)S(1)}, u32[]{:S(2)}, u32[]{:S(2)}) collective-permute-start(bf16[64,1280]{1,0:T(8,128)(2,1)S(1)} %collective-permute-done.9.refs_9_.rest_11_), channel_id=1, source_target_pairs={{0,8},{8,16},{16,24},{24,28},{28,20},{20,12},{12,4},{4,0},{1,9},{9... | collective-permute-start | bytes 491528 | tf_op jit(solution)/shard_map/ppermute | solution.py:808
  47.4 1.4 collective-permute-start.16
  48.8 0.9 collective-permute-start.13
  49.7 7.0 %cotangent.1 = (f32[512,1280]{1,0:T(8,128)S(1)}, bf16[4,320,512]{2,1,0:T(8,128)(2,1)S(1)}) custom-call(s32[5]{0:T(128)S(1)} %pad_add_fusion.1.refs_0_.owners, bf16[1280,2560]{1,0:T(8,128)(2,1)S(1)} %bitcast.13, bf16[512,640]{1,0:T(8,128)(2,1)S(1)} %copy-done.1, bf16[512,640]{1,0:T(8,128)(2,1)S(1)} %collective-permute-done.4.refs_3_, ...), custom_call_target="tpu_custom_call" | custom-call | flops 3355443200 | bytes 20000000 | tf_op jit(solution)/shard_map/cotangent/pallas_call | solution.py:183
  57.3 0.8 collective-permute-done.16.rest_15_
  58.2 5.2 %enter.1 = (f32[512,1280]{1,0:T(8,128)S(1)}, f32[1280,512]{1,0:T(8,128)S(1)}, f32[8,512]{1,0:T(8,128)S(1)}, f32[128,1280]{1,0:T(8,128)S(1)}, f32[8,1280]{1,0:T(8,128)S(1)}) custom-call(s32[9]{0:T(128)S(1)} %pad_add_fusion.sources.refs_0_, f32[512,1280]{1,0:T(8,128)S(1)} %inside.3.refs_6_.y_local, bf16[512,1280]{1,0:T(8,128)(2,1)S(1)} %copy-done.2, ...), custom_call_target="tpu_custom_call" | custom-call | flops 3000000000 | bytes 15000000 | tf_op jit(solution)/shard_map/enter/pallas_call | solution.py:372
  63.4 1.2 collective-permute-done.17
  65.1 0.6 stack.1.cot_theirs
  65.7 2.6 %collective-permute-done.18 = f32[8,512]{1,0:T(8,128)S(1)} collective-permute-done((f32[8,512]{1,0:T(8,128)S(1)}, f32[8,512]{1,0:T(8,128)S(1)}, u32[]{:S(2)}, u32[]{:S(2)}) %collective-permute-start.18) | collective-permute-done | bytes 16416 | tf_op jit(solution)/shard_map/ppermute | solution.py:838
  69.1 1.7 collective-permute-start.35
  70.8 5.6 %gate_grads.1 = (bf16[512,1280]{1,0:T(8,128)(2,1)}, f32[512,1280]{1,0:T(8,128)S(1)}, bf16[64,1280]{1,0:T(8,128)(2,1)S(1)}, f32[64,1280]{1,0:T(8,128)S(1)}, f32[8,1280]{1,0:T(8,128)S(1)}) custom-call(s32[9]{0:T(128)S(1)} %pad_add_fusion.sources.refs_0_, f32[512,1280]{1,0:T(8,128)S(1)} %get-tuple-element.54.y_ref.refs_1_, bf16[512,1280]{1,0:T(8,128)(2,1)S(1)} %copy-done.2, ...), custom_call_target="tpu_custom_call" | custom-call | flops 3000000000 | bytes 15000000 | tf_op jit(solution)/shard_map/gate_grads/pallas_call | solution.py:453
  76.7 4.9 %inside_back.2 = (f32[512,1280]{1,0:T(8,128)S(1)}, f32[512,512]{1,0:T(8,128)S(1)}) custom-call(f32[512,128]{1,0:T(8,128)S(1)} %copy-done.11, f32[128,512]{1,0:T(8,128)S(1)} %copy-done.17, bf16[512,128]{1,0:T(8,128)(2,1)S(1)} %copy-done.10, bf16[512,128]{1,0:T(8,128)(2,1)S(1)} %copy-done.9, bf16[512,1280]{1,0:T(8,128)(2,1)S(1)} %copy-done.15, ...), custom_call_target="tpu_custom_call" | custom-call | flops 10000000000 | bytes 4000000 | tf_op jit(solution)/shard_map/inside_back/pallas_call | solution.py:549
  81.6 1.9 collective-permute-done.23.theirs
  83.5 2.0 product.2
  85.5 0.8 copy-done.12
  86.4 3.5 %collective-permute-start.28 = (bf16[320,512]{1,0:T(8,128)(2,1)S(1)}, bf16[320,512]{1,0:T(8,128)(2,1)S(1)}, u32[]{:S(2)}, u32[]{:S(2)}) collective-permute-start(bf16[320,512]{1,0:T(8,128)(2,1)S(1)} %get-tuple-element.70), channel_id=1, source_target_pairs={{0,8},{4,12},{24,16},{28,20},{1,9},{5,13},{25,17},{29,21},{2,10},{... | collective-permute-start | bytes 983048 | tf_op jit(solution)/shard_map/ppermute | solution.py:860
  89.8 5.6 %inside_back.3 = (f32[512,1280]{1,0:T(8,128)S(1)}, f32[512,128]{1,0:T(8,128)S(1)}, f32[512,128]{1,0:T(8,128)S(1)}) custom-call(f32[512,128]{1,0:T(8,128)S(1)} %copy-done.11, f32[128,512]{1,0:T(8,128)S(1)} %copy-done.17, bf16[512,128]{1,0:T(8,128)(2,1)S(1)} %copy-done.10, bf16[512,128]{1,0:T(8,128)(2,1)S(1)} %copy-done.9, ...), custom_call_target="tpu_custom_call", output_to_operand_aliasing={{0}: (6, {})} | custom-call | flops 10000000000 | bytes 4000000 | tf_op jit(solution)/shard_map/inside_back/pallas_call | solution.py:549
  95.5 6.5 %collective-permute-done.19.refs_3_ = bf16[64,1280]{1,0:T(8,128)(2,1)S(1)} collective-permute-done((bf16[64,1280]{1,0:T(8,128)(2,1)S(1)}, bf16[64,1280]{1,0:T(8,128)(2,1)S(1)}, u32[]{:S(2)}, u32[]{:S(2)}) %collective-permute-start.19) | collective-permute-done | bytes 163872 | tf_op jit(solution)/shard_map/ppermute | solution.py:615
  102.0 0.6 shard_map.179
  102.6 1.3 collective-permute-start.20
  103.9 1.3 collective-permute-start.21
  105.2 1.3 collective-permute-start.22
  106.6 4.8 %collective-permute-done.20.refs_4_ = bf16[64,1280]{1,0:T(8,128)(2,1)S(1)} collective-permute-done((bf16[64,1280]{1,0:T(8,128)(2,1)S(1)}, bf16[64,1280]{1,0:T(8,128)(2,1)S(1)}, u32[]{:S(2)}, u32[]{:S(2)}) %collective-permute-start.20) | collective-permute-done | bytes 163872 | tf_op jit(solution)/shard_map/ppermute | solution.py:621
  111.4 8.9 %collective-permute-done.21.refs_5_ = bf16[64,1280]{1,0:T(8,128)(2,1)S(1)} collective-permute-done((bf16[64,1280]{1,0:T(8,128)(2,1)S(1)}, bf16[64,1280]{1,0:T(8,128)(2,1)S(1)}, u32[]{:S(2)}, u32[]{:S(2)}) %collective-permute-start.21) | collective-permute-done | bytes 163872 | tf_op jit(solution)/shard_map/ppermute | solution.py:621
  120.3 0.7 shard_map.180
  121.0 0.8 collective-permute-start.29
  121.9 3.3 %product.3 = (bf16[320,768]{1,0:T(8,128)(2,1)}, bf16[320,768]{1,0:T(8,128)(2,1)S(1)}, bf16[320,768]{1,0:T(8,128)(2,1)S(1)}, f32[320,768]{1,0:T(8,128)S(1)}) custom-call(s32[1]{0:T(128)} %bitcast.4.group, bf16[768,512]{1,0:T(8,128)(2,1)S(1)} %multiply_convert_fusion.mine, bf16[768,512]{1,0:T(8,128)(2,1)S(1)} %collective-permute-done.35.theirs, ...), custom_call_target="tpu_custom_call" | custom-call | flops 2013265920 | bytes 5000000 | tf_op jit(solution)/shard_map/product/pallas_call | solution.py:749
  125.2 1.5 collective-permute-start.38
  126.8 7.1 %leave.1 = (bf16[512,1280]{1,0:T(8,128)(2,1)}, f32[2,512,128]{2,1,0:T(8,128)S(1)}, f32[20,512]{1,0:T(8,128)}) custom-call(s32[9]{0:T(128)S(1)} %pad_add_fusion.sources.refs_0_, f32[512,1280]{1,0:T(8,128)S(1)} %get-tuple-element.54.y_ref.refs_1_, bf16[512,1280]{1,0:T(8,128)(2,1)S(1)} %copy-done.15, f32[512,1280]{1,0:T(8,128)S(1)} %get-tuple-element.57.grad_y.refs_3_, ...), custom_call_target="tpu_custom_call" | custom-call | flops 5000000000 | bytes 20000000 | tf_op jit(solution)/shard_map/leave/pallas_call | solution.py:700
  133.9 4.0 %collective-permute-done.32 = f32[8,1280]{1,0:T(8,128)S(1)} collective-permute-done((f32[8,1280]{1,0:T(8,128)S(1)}, f32[8,1280]{1,0:T(8,128)S(1)}, u32[]{:S(2)}, u32[]{:S(2)}) %collective-permute-start.32) | collective-permute-done | bytes 40992 | tf_op jit(solution)/shard_map/ppermute | solution.py:838
  138.3 0.7 collective-permute-start.40
  139.0 3.9 %collective-permute-done.33 = f32[8,1280]{1,0:T(8,128)S(1)} collective-permute-done((f32[8,1280]{1,0:T(8,128)S(1)}, f32[8,1280]{1,0:T(8,128)S(1)}, u32[]{:S(2)}, u32[]{:S(2)}) %collective-permute-start.33) | collective-permute-done | bytes 40992 | tf_op jit(solution)/shard_map/ppermute | solution.py:838
  142.9 1.2 collective-permute-start.34
  144.6 0.7 collective-permute-start.36
  145.3 0.9 add_convert_fusion
  146.2 0.7 collective-permute-done.34
  146.9 2.8 %collective-permute-start.37 = (bf16[320,768]{1,0:T(8,128)(2,1)S(1)}, bf16[320,768]{1,0:T(8,128)(2,1)S(1)}, u32[]{:S(2)}, u32[]{:S(2)}) collective-permute-start(bf16[320,768]{1,0:T(8,128)(2,1)S(1)} %get-tuple-element.80), channel_id=1, source_target_pairs={{0,8},{4,12},{8,0},{12,4},{16,24},{20,28},{24,16},{28,20},{1,9},{5... | collective-permute-start | bytes 1474568 | tf_op jit(solution)/shard_map/ppermute | solution.py:860
  149.8 0.8 collective-permute-start.39
  150.6 0.9 add.68
  151.4 0.7 copy-done.3
  152.7 2.1 %collective-permute-done.41.rest_1_ = bf16[320,512]{1,0:T(8,128)(2,1)S(1)} collective-permute-done((bf16[320,512]{1,0:T(8,128)(2,1)S(1)}, bf16[320,512]{1,0:T(8,128)(2,1)S(1)}, u32[]{:S(2)}, u32[]{:S(2)}) %collective-permute-start.41) | collective-permute-done | bytes 327712 | tf_op jit(solution)/shard_map/ppermute | solution.py:860
  154.8 0.7 copy-done.5
  157.1 38.7 %collective-permute-done.42.rest_2_ = bf16[320,512]{1,0:T(8,128)(2,1)} collective-permute-done((bf16[320,512]{1,0:T(8,128)(2,1)S(1)}, bf16[320,512]{1,0:T(8,128)(2,1)}, u32[]{:S(2)}, u32[]{:S(2)}) %collective-permute-start.42) | collective-permute-done | bytes 327712 | tf_op jit(solution)/shard_map/ppermute | solution.py:860
  195.8 1.0 copy-done.4
  196.8 1.0 copy-done.6
  197.8 1.1 copy-done.13
  198.9 1.9 finish.2.rest_3_
  200.7 1.7 finish.3
  202.5 1.3 add.69
  203.7 0.8 slice_bitcast_fusion
  (111 shorter events, 7.5 us)
Async XLA Ops:
  5.7 17.3 %collective-permute-start = (bf16[80,1280]{1,0:T(8,128)(2,1)}, bf16[80,1280]{1,0:T(8,128)(2,1)S(1)}, u32[]{:S(2)}, u32[]{:S(2)}) collective-permute-start(bf16[80,1280]{1,0:T(8,128)(2,1)} %get-tuple-element.50.rest_0_), channel_id=1, source_target_pairs={{0,8},{8,16},{16,24},{24,28},{28,20},{20,12},{12,4},{4,0},{1,9},{9... | collective-permute-start | bytes 614408 | tf_op jit(solution)/shard_map/ppermute | solution.py:808
  8.8 15.8 %collective-permute-start.1 = (bf16[80,1280]{1,0:T(8,128)(2,1)}, bf16[80,1280]{1,0:T(8,128)(2,1)S(1)}, u32[]{:S(2)}, u32[]{:S(2)}) collective-permute-start(bf16[80,1280]{1,0:T(8,128)(2,1)} %get-tuple-element.50.rest_0_), channel_id=1, source_target_pairs={{8,0},{16,8},{24,16},{28,24},{20,28},{12,20},{4,12},{0,4},{9,1},{1... | collective-permute-start | bytes 614408 | tf_op jit(solution)/shard_map/ppermute | solution.py:808
  8.8 12.1 %collective-permute-start.2 = (bf16[64,1280]{1,0:T(8,128)(2,1)}, bf16[64,1280]{1,0:T(8,128)(2,1)S(1)}, u32[]{:S(2)}, u32[]{:S(2)}) collective-permute-start(bf16[64,1280]{1,0:T(8,128)(2,1)} %get-tuple-element.51.rest_8_), channel_id=1, source_target_pairs={{0,8},{8,16},{16,24},{24,28},{28,20},{20,12},{12,4},{4,0},{1,9},{9... | collective-permute-start | bytes 491528 | tf_op jit(solution)/shard_map/ppermute | solution.py:808
  10.8 11.6 %collective-permute-start.3 = (bf16[64,1280]{1,0:T(8,128)(2,1)}, bf16[64,1280]{1,0:T(8,128)(2,1)S(1)}, u32[]{:S(2)}, u32[]{:S(2)}) collective-permute-start(bf16[64,1280]{1,0:T(8,128)(2,1)} %get-tuple-element.51.rest_8_), channel_id=1, source_target_pairs={{8,0},{16,8},{24,16},{28,24},{20,28},{12,20},{4,12},{0,4},{9,1},{1... | collective-permute-start | bytes 491528 | tf_op jit(solution)/shard_map/ppermute | solution.py:808
  10.8 28.1 %collective-permute-start.4 = (bf16[512,640]{1,0:T(8,128)(2,1)}, bf16[512,640]{1,0:T(8,128)(2,1)S(1)}, u32[]{:S(2)}, u32[]{:S(2)}) collective-permute-start(bf16[512,640]{1,0:T(8,128)(2,1)} %shard.1), channel_id=1, source_target_pairs={{0,2},{1,3},{2,0},{3,1},{4,6},{5,7},{6,4},{7,5},{8,10},{9,11},{10,... | collective-permute-start | bytes 1966088 | tf_op jit(solution)/shard_map/ppermute | solution.py:848
  12.8 1.1 copy-start
  14.3 6.5 %copy-start.21 = (s32[4]{0:T(128)S(1)}, s32[4]{0:T(128)}, u32[]{:S(2)}) copy-start(s32[4]{0:T(128)} %constant.73.clone) | copy-start | bytes 52
  14.3 8.6 %copy-start.20 = (s32[8]{0:T(128)S(1)}, s32[8]{0:T(128)}, u32[]{:S(2)}) copy-start(s32[8]{0:T(128)} %constant.72.clone) | copy-start | bytes 100
  14.3 19.7 %copy-start.19 = (f32[1280]{0:T(1024)S(1)}, f32[1280]{0:T(1024)}, u32[]{:S(2)}) copy-start(f32[1280]{0:T(1024)} %param.19) | copy-start | bytes 15364
  14.4 20.3 %copy-start.1 = (bf16[512,640]{1,0:T(8,128)(2,1)S(1)}, bf16[512,640]{1,0:T(8,128)(2,1)}, u32[]{:S(2)}) copy-start(bf16[512,640]{1,0:T(8,128)(2,1)} %shard.1) | copy-start | bytes 1966084
  14.4 24.6 %copy-start.9 = (bf16[512,128]{1,0:T(8,128)(2,1)S(1)}, bf16[512,128]{1,0:T(8,128)(2,1)}, u32[]{:S(2)}) copy-start(bf16[512,128]{1,0:T(8,128)(2,1)} %read.11) | copy-start | bytes 393220
  14.4 24.6 %copy-start.10 = (bf16[512,128]{1,0:T(8,128)(2,1)S(1)}, bf16[512,128]{1,0:T(8,128)(2,1)}, u32[]{:S(2)}) copy-start(bf16[512,128]{1,0:T(8,128)(2,1)} %refs_5_.1) | copy-start | bytes 393220
  14.4 24.6 %copy-start.11 = (f32[512,128]{1,0:T(8,128)S(1)}, f32[512,128]{1,0:T(8,128)}, u32[]{:S(2)}) copy-start(f32[512,128]{1,0:T(8,128)} %get-tuple-element.46.seg_t.refs_6_) | copy-start | bytes 786436
  14.4 24.6 %copy-start.15 = (bf16[512,1280]{1,0:T(8,128)(2,1)S(1)}, bf16[512,1280]{1,0:T(8,128)(2,1)}, u32[]{:S(2)}) copy-start(bf16[512,1280]{1,0:T(8,128)(2,1)} %get-tuple-element.48.x.refs_2_) | copy-start | bytes 3932164
  14.4 24.6 %copy-start.17 = (f32[128,512]{1,0:T(8,128)S(1)}, f32[128,512]{1,0:T(8,128)}, u32[]{:S(2)}) copy-start(f32[128,512]{1,0:T(8,128)} %get-tuple-element.47.seg) | copy-start | bytes 786436
  14.4 24.6 %copy-start.18 = (f32[8,1280]{1,0:T(8,128)S(1)}, f32[8,1280]{1,0:T(8,128)}, u32[]{:S(2)}) copy-start(f32[8,1280]{1,0:T(8,128)} %get-tuple-element.49.skip.refs_9_) | copy-start | bytes 122884
  20.9 13.8 %collective-permute-start.24 = (bf16[320,512]{1,0:T(8,128)(2,1)S(1)}, bf16[320,512]{1,0:T(8,128)(2,1)S(1)}, u32[]{:S(2)}, u32[]{:S(2)}) collective-permute-start(bf16[320,512]{1,0:T(8,128)(2,1)S(1)} %pick.1), channel_id=1, source_target_pairs={{0,4},{4,0},{8,12},{12,8},{16,20},{20,16},{24,28},{28,24},{1,5},{5... | collective-permute-start | bytes 983048 | tf_op jit(solution)/shard_map/ppermute | solution.py:894
  22.4 9.1 %collective-permute-start.10 = (bf16[64,1280]{1,0:T(8,128)(2,1)S(1)}, bf16[64,1280]{1,0:T(8,128)(2,1)S(1)}, u32[]{:S(2)}, u32[]{:S(2)}) collective-permute-start(bf16[64,1280]{1,0:T(8,128)(2,1)S(1)} %collective-permute-done.3.rest_4_.rest_10_), channel_id=1, source_target_pairs={{8,0},{16,8},{24,16},{28,24},{20,28},{12,20},{4,12},{0,4},{9,1},{1... | collective-permute-start | bytes 491528 | tf_op jit(solution)/shard_map/ppermute | solution.py:808
  23.0 11.7 %collective-permute-start.9 = (bf16[64,1280]{1,0:T(8,128)(2,1)S(1)}, bf16[64,1280]{1,0:T(8,128)(2,1)S(1)}, u32[]{:S(2)}, u32[]{:S(2)}) collective-permute-start(bf16[64,1280]{1,0:T(8,128)(2,1)S(1)} %collective-permute-done.2.rest_3_.rest_9_), channel_id=1, source_target_pairs={{0,8},{8,16},{16,24},{24,28},{28,20},{20,12},{12,4},{4,0},{1,9},{9... | collective-permute-start | bytes 491528 | tf_op jit(solution)/shard_map/ppermute | solution.py:808
  24.6 12.3 %collective-permute-start.7 = (bf16[80,1280]{1,0:T(8,128)(2,1)S(1)}, bf16[80,1280]{1,0:T(8,128)(2,1)S(1)}, u32[]{:S(2)}, u32[]{:S(2)}) collective-permute-start(bf16[80,1280]{1,0:T(8,128)(2,1)S(1)} %collective-permute-done.rest_1_), channel_id=1, source_target_pairs={{0,8},{8,16},{16,24},{24,28},{28,20},{20,12},{12,4},{4,0},{1,9},{9... | collective-permute-start | bytes 614408 | tf_op jit(solution)/shard_map/ppermute | solution.py:808
  31.5 7.4 %collective-permute-start.8 = (bf16[80,1280]{1,0:T(8,128)(2,1)S(1)}, bf16[80,1280]{1,0:T(8,128)(2,1)S(1)}, u32[]{:S(2)}, u32[]{:S(2)}) collective-permute-start(bf16[80,1280]{1,0:T(8,128)(2,1)S(1)} %collective-permute-done.1.rest_2_), channel_id=1, source_target_pairs={{8,0},{16,8},{24,16},{28,24},{20,28},{12,20},{4,12},{0,4},{9,1},{1... | collective-permute-start | bytes 614408 | tf_op jit(solution)/shard_map/ppermute | solution.py:808
  34.1 15.6 %slice-start = ((s8[6553600]{0:T(1024)(128)(4,1)}), s8[4194304]{0:T(1024)(128)(4,1)S(1)}, s32[]{:S(2)}) async-start(s8[6553600]{0:T(1024)(128)(4,1)} %bitcast.12), calls=%async_computation | async-start | bytes 8388608
  34.2 15.5 %slice-start.1 = ((s8[6553600]{0:T(1024)(128)(4,1)}), s8[2359296]{0:T(1024)(128)(4,1)S(1)}, s32[]{:S(2)}) async-start(s8[6553600]{0:T(1024)(128)(4,1)} %bitcast.12), calls=%async_computation.1 | async-start | bytes 4718592
  34.7 12.7 %collective-permute-start.5 = (bf16[512,640]{1,0:T(8,128)(2,1)S(1)}, bf16[512,640]{1,0:T(8,128)(2,1)S(1)}, u32[]{:S(2)}, u32[]{:S(2)}) collective-permute-start(bf16[512,640]{1,0:T(8,128)(2,1)S(1)} %copy-done.1), channel_id=1, source_target_pairs={{0,1},{1,0},{2,3},{3,2},{4,5},{5,4},{6,7},{7,6},{8,9},{9,8},{10,11... | collective-permute-start | bytes 1966088 | tf_op jit(solution)/shard_map/ppermute | solution.py:848
  34.7 9.5 %collective-permute-start.15 = (bf16[64,1280]{1,0:T(8,128)(2,1)S(1)}, bf16[64,1280]{1,0:T(8,128)(2,1)S(1)}, u32[]{:S(2)}, u32[]{:S(2)}) collective-permute-start(bf16[64,1280]{1,0:T(8,128)(2,1)S(1)} %collective-permute-done.10.refs_10_.rest_12_), channel_id=1, source_target_pairs={{8,0},{16,8},{24,16},{28,24},{20,28},{12,20},{4,12},{0,4},{9,1},{1... | collective-permute-start | bytes 491528 | tf_op jit(solution)/shard_map/ppermute | solution.py:808
  36.9 19.9 %collective-permute-start.25 = (bf16[320,512]{1,0:T(8,128)(2,1)S(1)}, bf16[320,512]{1,0:T(8,128)(2,1)S(1)}, u32[]{:S(2)}, u32[]{:S(2)}) collective-permute-start(bf16[320,512]{1,0:T(8,128)(2,1)S(1)} %collective-permute-done.24.rest_0_), channel_id=1, source_target_pairs={{0,2},{1,3},{2,0},{3,1},{4,6},{5,7},{6,4},{7,5},{8,10},{9,11},{10,... | collective-permute-start | bytes 983048 | tf_op jit(solution)/shard_map/ppermute | solution.py:848
  38.9 8.5 %collective-permute-start.11 = (bf16[80,1280]{1,0:T(8,128)(2,1)S(1)}, bf16[80,1280]{1,0:T(8,128)(2,1)S(1)}, u32[]{:S(2)}, u32[]{:S(2)}) collective-permute-start(bf16[80,1280]{1,0:T(8,128)(2,1)S(1)} %collective-permute-done.7.refs_7_.rest_3_), channel_id=1, source_target_pairs={{0,8},{8,16},{16,24},{24,28},{28,20},{20,12},{12,4},{4,0},{1,9},{9... | collective-permute-start | bytes 614408 | tf_op jit(solution)/shard_map/ppermute | solution.py:808
  38.9 9.9 %collective-permute-start.6 = (bf16[512,640]{1,0:T(8,128)(2,1)S(1)}, bf16[512,640]{1,0:T(8,128)(2,1)S(1)}, u32[]{:S(2)}, u32[]{:S(2)}) collective-permute-start(bf16[512,640]{1,0:T(8,128)(2,1)S(1)} %collective-permute-done.4.refs_3_), channel_id=1, source_target_pairs={{0,1},{1,0},{2,3},{3,2},{4,5},{5,4},{6,7},{7,6},{8,9},{9,8},{10,11... | collective-permute-start | bytes 1966088 | tf_op jit(solution)/shard_map/ppermute | solution.py:848
  44.1 14.0 %copy-start.2 = (bf16[512,1280]{1,0:T(8,128)(2,1)S(1)}, bf16[512,1280]{1,0:T(8,128)(2,1)}, u32[]{:S(2)}) copy-start(bf16[512,1280]{1,0:T(8,128)(2,1)} %gate.3) | copy-start | bytes 3932164
  44.1 14.0 %copy-start.7 = (bf16[80,1280]{1,0:T(8,128)(2,1)S(1)}, bf16[80,1280]{1,0:T(8,128)(2,1)}, u32[]{:S(2)}) copy-start(bf16[80,1280]{1,0:T(8,128)(2,1)} %get-tuple-element.50.rest_0_) | copy-start | bytes 614404
  44.1 14.0 %copy-start.8 = (bf16[64,1280]{1,0:T(8,128)(2,1)S(1)}, bf16[64,1280]{1,0:T(8,128)(2,1)}, u32[]{:S(2)}) copy-start(bf16[64,1280]{1,0:T(8,128)(2,1)} %get-tuple-element.51.rest_8_) | copy-start | bytes 491524
  44.2 14.0 %copy-start.14 = (bf16[256,1280]{1,0:T(8,128)(2,1)S(1)}, bf16[256,1280]{1,0:T(8,128)(2,1)}, u32[]{:S(2)}) copy-start(bf16[256,1280]{1,0:T(8,128)(2,1)} %get-tuple-element.53.spread2.refs_8_) | copy-start | bytes 1966084
  44.2 12.5 %collective-permute-start.14 = (bf16[64,1280]{1,0:T(8,128)(2,1)S(1)}, bf16[64,1280]{1,0:T(8,128)(2,1)S(1)}, u32[]{:S(2)}, u32[]{:S(2)}) collective-permute-start(bf16[64,1280]{1,0:T(8,128)(2,1)S(1)} %collective-permute-done.9.refs_9_.rest_11_), channel_id=1, source_target_pairs={{0,8},{8,16},{16,24},{24,28},{28,20},{20,12},{12,4},{4,0},{1,9},{9... | collective-permute-start | bytes 491528 | tf_op jit(solution)/shard_map/ppermute | solution.py:808
  47.4 9.9 %collective-permute-start.12 = (bf16[80,1280]{1,0:T(8,128)(2,1)S(1)}, bf16[80,1280]{1,0:T(8,128)(2,1)S(1)}, u32[]{:S(2)}, u32[]{:S(2)}) collective-permute-start(bf16[80,1280]{1,0:T(8,128)(2,1)S(1)} %collective-permute-done.8.refs_8_.rest_4_), channel_id=1, source_target_pairs={{8,0},{16,8},{24,16},{28,24},{20,28},{12,20},{4,12},{0,4},{9,1},{1... | collective-permute-start | bytes 614408 | tf_op jit(solution)/shard_map/ppermute | solution.py:808
  47.4 10.7 %collective-permute-start.16 = (bf16[64,1280]{1,0:T(8,128)(2,1)S(1)}, bf16[64,1280]{1,0:T(8,128)(2,1)S(1)}, u32[]{:S(2)}, u32[]{:S(2)}) collective-permute-start(bf16[64,1280]{1,0:T(8,128)(2,1)S(1)} %collective-permute-done.15.rest_14_), channel_id=1, source_target_pairs={{8,0},{16,8},{24,16},{28,24},{20,28},{12,20},{4,12},{0,4},{9,1},{1... | collective-permute-start | bytes 491528 | tf_op jit(solution)/shard_map/ppermute | solution.py:808
  48.8 9.3 %collective-permute-start.13 = (bf16[80,1280]{1,0:T(8,128)(2,1)S(1)}, bf16[80,1280]{1,0:T(8,128)(2,1)S(1)}, u32[]{:S(2)}, u32[]{:S(2)}) collective-permute-start(bf16[80,1280]{1,0:T(8,128)(2,1)S(1)} %collective-permute-done.11.rest_5_), channel_id=1, source_target_pairs={{0,8},{8,16},{16,24},{24,28},{28,20},{20,12},{12,4},{4,0},{1,9},{9... | collective-permute-start | bytes 614408 | tf_op jit(solution)/shard_map/ppermute | solution.py:808
  56.7 8.4 %collective-permute-start.26 = (bf16[320,512]{1,0:T(8,128)(2,1)S(1)}, bf16[320,512]{1,0:T(8,128)(2,1)S(1)}, u32[]{:S(2)}, u32[]{:S(2)}) collective-permute-start(bf16[320,512]{1,0:T(8,128)(2,1)S(1)} %collective-permute-done.24.rest_0_), channel_id=1, source_target_pairs={{0,1},{1,0},{2,3},{3,2},{4,5},{5,4},{6,7},{7,6},{8,9},{9,8},{10,11... | collective-permute-start | bytes 983048 | tf_op jit(solution)/shard_map/ppermute | solution.py:848
  56.8 8.3 %collective-permute-start.27 = (bf16[320,512]{1,0:T(8,128)(2,1)S(1)}, bf16[320,512]{1,0:T(8,128)(2,1)S(1)}, u32[]{:S(2)}, u32[]{:S(2)}) collective-permute-start(bf16[320,512]{1,0:T(8,128)(2,1)S(1)} %collective-permute-done.25.rest_1_), channel_id=1, source_target_pairs={{0,1},{1,0},{2,3},{3,2},{4,5},{5,4},{6,7},{7,6},{8,9},{9,8},{10,11... | collective-permute-start | bytes 983048 | tf_op jit(solution)/shard_map/ppermute | solution.py:848
  63.3 1.2 collective-permute-start.17
  64.6 3.7 %collective-permute-start.18 = (f32[8,512]{1,0:T(8,128)S(1)}, f32[8,512]{1,0:T(8,128)S(1)}, u32[]{:S(2)}, u32[]{:S(2)}) collective-permute-start(f32[8,512]{1,0:T(8,128)S(1)} %add.63), channel_id=1, source_target_pairs={{0,2},{1,3},{2,0},{3,1},{4,6},{5,7},{6,4},{7,5},{8,10},{9,11},{10,... | collective-permute-start | bytes 49160 | tf_op jit(solution)/shard_map/ppermute | solution.py:838
  65.7 5.0 %copy-start.16 = (bf16[128,512]{1,0:T(8,128)(2,1)S(1)}, bf16[128,512]{1,0:T(8,128)(2,1)}, u32[]{:S(2)}) copy-start(bf16[128,512]{1,0:T(8,128)(2,1)} %get-tuple-element.56.read_t) | copy-start | bytes 393220
  68.7 14.9 %collective-permute-start.23 = (bf16[512,512]{1,0:T(8,128)(2,1)S(1)}, bf16[512,512]{1,0:T(8,128)(2,1)S(1)}, u32[]{:S(2)}, u32[]{:S(2)}) collective-permute-start(bf16[512,512]{1,0:T(8,128)(2,1)S(1)} %multiply_convert_fusion.1.mine), channel_id=1, source_target_pairs={{0,4},{4,0},{8,12},{12,8},{16,20},{20,16},{24,28},{28,24},{1,5},{5... | collective-permute-start | bytes 1572872 | tf_op jit(solution)/shard_map/ppermute | solution.py:926
  69.1 52.8 %collective-permute-start.35 = (bf16[768,512]{1,0:T(8,128)(2,1)S(1)}, bf16[768,512]{1,0:T(8,128)(2,1)S(1)}, u32[]{:S(2)}, u32[]{:S(2)}) collective-permute-start(bf16[768,512]{1,0:T(8,128)(2,1)S(1)} %multiply_convert_fusion.mine), channel_id=1, source_target_pairs={{0,4},{4,0},{8,12},{12,8},{16,20},{20,16},{24,28},{28,24},{1,5},{5... | collective-permute-start | bytes 2359304 | tf_op jit(solution)/shard_map/ppermute | solution.py:926
  76.4 25.6 %collective-permute-start.19 = (bf16[64,1280]{1,0:T(8,128)(2,1)S(1)}, bf16[64,1280]{1,0:T(8,128)(2,1)S(1)}, u32[]{:S(2)}, u32[]{:S(2)}) collective-permute-start(bf16[64,1280]{1,0:T(8,128)(2,1)S(1)} %get-tuple-element.66), channel_id=1, source_target_pairs={{0,4},{4,0},{8,12},{12,8},{16,20},{20,16},{24,28},{28,24},{1,5},{5... | collective-permute-start | bytes 491528 | tf_op jit(solution)/shard_map/ppermute | solution.py:615
  86.4 20.1 %collective-permute-start.28 = (bf16[320,512]{1,0:T(8,128)(2,1)S(1)}, bf16[320,512]{1,0:T(8,128)(2,1)S(1)}, u32[]{:S(2)}, u32[]{:S(2)}) collective-permute-start(bf16[320,512]{1,0:T(8,128)(2,1)S(1)} %get-tuple-element.70), channel_id=1, source_target_pairs={{0,8},{4,12},{24,16},{28,20},{1,9},{5,13},{25,17},{29,21},{2,10},{... | collective-permute-start | bytes 983048 | tf_op jit(solution)/shard_map/ppermute | solution.py:860
  102.6 8.8 %collective-permute-start.20 = (bf16[64,1280]{1,0:T(8,128)(2,1)S(1)}, bf16[64,1280]{1,0:T(8,128)(2,1)S(1)}, u32[]{:S(2)}, u32[]{:S(2)}) collective-permute-start(bf16[64,1280]{1,0:T(8,128)(2,1)S(1)} %shard_map.179), channel_id=1, source_target_pairs={{8,0},{12,4},{16,8},{20,12},{24,16},{28,20},{9,1},{13,5},{17,9},{2... | collective-permute-start | bytes 491528 | tf_op jit(solution)/shard_map/ppermute | solution.py:621
  103.9 16.4 %collective-permute-start.21 = (bf16[64,1280]{1,0:T(8,128)(2,1)S(1)}, bf16[64,1280]{1,0:T(8,128)(2,1)S(1)}, u32[]{:S(2)}, u32[]{:S(2)}) collective-permute-start(bf16[64,1280]{1,0:T(8,128)(2,1)S(1)} %shard_map.179), channel_id=1, source_target_pairs={{16,0},{20,4},{24,8},{28,12},{17,1},{21,5},{25,9},{29,13},{18,2},{... | collective-permute-start | bytes 491528 | tf_op jit(solution)/shard_map/ppermute | solution.py:621
  105.2 15.1 %collective-permute-start.22 = (bf16[64,1280]{1,0:T(8,128)(2,1)S(1)}, bf16[64,1280]{1,0:T(8,128)(2,1)S(1)}, u32[]{:S(2)}, u32[]{:S(2)}) collective-permute-start(bf16[64,1280]{1,0:T(8,128)(2,1)S(1)} %shard_map.179), channel_id=1, source_target_pairs={{24,0},{28,4},{25,1},{29,5},{26,2},{30,6},{27,3},{31,7}} | collective-permute-start | bytes 491528 | tf_op jit(solution)/shard_map/ppermute | solution.py:621
  121.0 5.7 %collective-permute-start.29 = (bf16[64,1280]{1,0:T(8,128)(2,1)S(1)}, bf16[64,1280]{1,0:T(8,128)(2,1)S(1)}, u32[]{:S(2)}, u32[]{:S(2)}) collective-permute-start(bf16[64,1280]{1,0:T(8,128)(2,1)S(1)} %get-tuple-element.72), channel_id=1, source_target_pairs={{0,4},{4,0},{8,12},{12,8},{16,20},{20,16},{24,28},{28,24},{1,5},{5... | collective-permute-start | bytes 491528 | tf_op jit(solution)/shard_map/ppermute | solution.py:632
  125.2 19.4 %collective-permute-start.38 = (bf16[320,768]{1,0:T(8,128)(2,1)}, bf16[320,768]{1,0:T(8,128)(2,1)S(1)}, u32[]{:S(2)}, u32[]{:S(2)}) collective-permute-start(bf16[320,768]{1,0:T(8,128)(2,1)} %get-tuple-element.79), channel_id=1, source_target_pairs={{0,8},{4,12},{24,16},{28,20},{1,9},{5,13},{25,17},{29,21},{2,10},{... | collective-permute-start | bytes 1474568 | tf_op jit(solution)/shard_map/ppermute | solution.py:860
  133.9 15.9 %collective-permute-start.30 = (f32[2,512,128]{2,1,0:T(8,128)S(1)}, f32[2,512,128]{2,1,0:T(8,128)S(1)}, u32[]{:S(2)}, u32[]{:S(2)}) collective-permute-start(f32[2,512,128]{2,1,0:T(8,128)S(1)} %get-tuple-element.75), channel_id=1, source_target_pairs={{0,1},{1,0},{2,3},{3,2},{4,5},{5,4},{6,7},{7,6},{8,9},{9,8},{10,11... | collective-permute-start | bytes 1572872 | tf_op jit(solution)/shard_map/ppermute | solution.py:838
  133.9 4.0 %collective-permute-start.32 = (f32[8,1280]{1,0:T(8,128)S(1)}, f32[8,1280]{1,0:T(8,128)S(1)}, u32[]{:S(2)}, u32[]{:S(2)}) collective-permute-start(f32[8,1280]{1,0:T(8,128)S(1)} %get-tuple-element.77), channel_id=1, source_target_pairs={{0,8},{4,12},{8,0},{12,4},{16,24},{20,28},{24,16},{28,20},{1,9},{5... | collective-permute-start | bytes 122888 | tf_op jit(solution)/shard_map/ppermute | solution.py:838
  137.9 5.0 %collective-permute-start.33 = (f32[8,1280]{1,0:T(8,128)S(1)}, f32[8,1280]{1,0:T(8,128)S(1)}, u32[]{:S(2)}, u32[]{:S(2)}) collective-permute-start(f32[8,1280]{1,0:T(8,128)S(1)} %add.70), channel_id=1, source_target_pairs={{0,16},{4,20},{8,24},{12,28},{16,0},{20,4},{24,8},{28,12},{1,17},{... | collective-permute-start | bytes 122888 | tf_op jit(solution)/shard_map/ppermute | solution.py:838
  138.3 13.1 %collective-permute-start.40 = (bf16[320,512]{1,0:T(8,128)(2,1)S(1)}, bf16[320,512]{1,0:T(8,128)(2,1)S(1)}, u32[]{:S(2)}, u32[]{:S(2)}) collective-permute-start(bf16[320,512]{1,0:T(8,128)(2,1)S(1)} %get-tuple-element.70), channel_id=1, source_target_pairs={{8,16},{12,20},{16,8},{20,12},{9,17},{13,21},{17,9},{21,13},{10,18... | collective-permute-start | bytes 983048 | tf_op jit(solution)/shard_map/ppermute | solution.py:860
  142.9 4.0 %collective-permute-start.34 = (f32[8,1280]{1,0:T(8,128)S(1)}, f32[8,1280]{1,0:T(8,128)S(1)}, u32[]{:S(2)}, u32[]{:S(2)}) collective-permute-start(f32[8,1280]{1,0:T(8,128)S(1)} %add.71), channel_id=1, source_target_pairs={{0,4},{4,0},{8,12},{12,8},{16,20},{20,16},{24,28},{28,24},{1,5},{5... | collective-permute-start | bytes 122888 | tf_op jit(solution)/shard_map/ppermute | solution.py:838
  144.2 10.6 %collective-permute-start.41 = (bf16[320,512]{1,0:T(8,128)(2,1)S(1)}, bf16[320,512]{1,0:T(8,128)(2,1)S(1)}, u32[]{:S(2)}, u32[]{:S(2)}) collective-permute-start(bf16[320,512]{1,0:T(8,128)(2,1)S(1)} %get-tuple-element.83), channel_id=1, source_target_pairs={{0,8},{4,12},{8,0},{12,4},{16,24},{20,28},{24,16},{28,20},{1,9},{5... | collective-permute-start | bytes 983048 | tf_op jit(solution)/shard_map/ppermute | solution.py:860
  144.6 56.1 %collective-permute-start.36 = (bf16[320,768]{1,0:T(8,128)(2,1)}, bf16[320,768]{1,0:T(8,128)(2,1)S(1)}, u32[]{:S(2)}, u32[]{:S(2)}) collective-permute-start(bf16[320,768]{1,0:T(8,128)(2,1)} %get-tuple-element.79), channel_id=1, source_target_pairs={{8,16},{12,20},{16,8},{20,12},{9,17},{13,21},{17,9},{21,13},{10,18... | collective-permute-start | bytes 1474568 | tf_op jit(solution)/shard_map/ppermute | solution.py:860
  146.9 53.8 %collective-permute-start.37 = (bf16[320,768]{1,0:T(8,128)(2,1)S(1)}, bf16[320,768]{1,0:T(8,128)(2,1)S(1)}, u32[]{:S(2)}, u32[]{:S(2)}) collective-permute-start(bf16[320,768]{1,0:T(8,128)(2,1)S(1)} %get-tuple-element.80), channel_id=1, source_target_pairs={{0,8},{4,12},{8,0},{12,4},{16,24},{20,28},{24,16},{28,20},{1,9},{5... | collective-permute-start | bytes 1474568 | tf_op jit(solution)/shard_map/ppermute | solution.py:860
  149.8 51.0 %collective-permute-start.39 = (bf16[320,768]{1,0:T(8,128)(2,1)}, bf16[320,768]{1,0:T(8,128)(2,1)S(1)}, u32[]{:S(2)}, u32[]{:S(2)}) collective-permute-start(bf16[320,768]{1,0:T(8,128)(2,1)} %add_convert_fusion), channel_id=1, source_target_pairs={{0,16},{4,20},{8,24},{12,28},{16,0},{20,4},{24,8},{28,12},{1,17},{... | collective-permute-start | bytes 1474568 | tf_op jit(solution)/shard_map/ppermute | solution.py:860
  152.2 50.3 %collective-permute-start.31 = (f32[2,512,128]{2,1,0:T(8,128)}, f32[2,512,128]{2,1,0:T(8,128)}, u32[]{:S(2)}, u32[]{:S(2)}) collective-permute-start(f32[2,512,128]{2,1,0:T(8,128)} %add.68), channel_id=1, source_target_pairs={{0,2},{1,3},{2,0},{3,1},{4,6},{5,7},{6,4},{7,5},{8,10},{9,11},{10,... | collective-permute-start | bytes 1572872 | tf_op jit(solution)/shard_map/ppermute | solution.py:838
  155.5 40.3 %collective-permute-start.42 = (bf16[320,512]{1,0:T(8,128)(2,1)S(1)}, bf16[320,512]{1,0:T(8,128)(2,1)}, u32[]{:S(2)}, u32[]{:S(2)}) collective-permute-start(bf16[320,512]{1,0:T(8,128)(2,1)S(1)} %add_convert_fusion.1.refs_8_), channel_id=1, source_target_pairs={{0,16},{4,20},{8,24},{12,28},{16,0},{20,4},{24,8},{28,12},{1,17},{... | collective-permute-start | bytes 983048 | tf_op jit(solution)/shard_map/ppermute | solution.py:860
  195.8 1.0 copy-start.4
  196.8 1.0 copy-start.6
  197.8 1.1 copy-start.13
  (3 other events, 2.3 us)

commit v5 on v4

--- a/solution.py
+++ b/solution.py
@@ -770,7 +770,7 @@
     rest[-1][...] = total
 
 
-def finish(start, width, own, received, held):
+def finish(start, width, own, received, held, waits=()):
     columns, rows = own.shape
     block = 2 * LANES if rows % (2 * LANES) == 0 and start % (2 * LANES) == 0 else LANES
     small = pl.BlockSpec((columns, block), lambda i: (0, i))
@@ -781,6 +781,8 @@
         aliases = {len(operands): 0}
         operands.append(held)
         specs = specs + [WAIT]
+    operands += list(waits)
+    specs = specs + [WAIT] * len(waits)
     return pl.pallas_call(
         functools.partial(finish_kernel, len(received)),
         name="finish",
@@ -916,7 +918,7 @@
     )
     stats = butterfly_sum(stats, "tp", tp_size)
     scale = lax.rsqrt(stats[0:1, :] / total_width + EPSILON)
-    first = (2 * width // 5) // LANES * LANES
+    first = (2*width//5) // LANES * LANES
     bounds = (0, first, width)
     parts = len(bounds) - 1
     normed, normed_theirs = [], []
@@ -948,16 +950,18 @@
         heads, sources, y, x, grad_y, inner, state_write, seg_t, spread2, skip, state,
         write_part, read_part, own, other, (),
     )
+    maps = butterfly_sum(maps, "tp", tp_size)
+    write_map, read_map = maps[0], maps[1]
+    sums = butterfly_sum(sums, "seq", seq_size, 2)
     grad_out_weight = None
     for part in range(parts):
         grad_out_weight = finish(
-            bounds[part], width, own_part[part], arrived[part], grad_out_weight
+            bounds[part], width, own_part[part], arrived[part], grad_out_weight,
+            (write_map, read_map) if part == parts - 1 else (),
         )
-    maps = butterfly_sum(maps, "tp", tp_size)
-    sums = butterfly_sum(sums, "seq", seq_size, 2)
     grad_skip = jnp.sum(sums[1].reshape(heads, width // heads), axis=1)
     return (
-        grad_input, grad_gate, maps[0], maps[1], grad_decay, grad_skip, sums[0], grad_out_weight.T,
+        grad_input, grad_gate, write_map, read_map, grad_decay, grad_skip, sums[0], grad_out_weight.T,
     )
 
 

time: 205 us -> 212 us (1.034)
  starting transfers between devices: 41.8 us -> 51.6 us
    ppermute x2, waiting for transfers between devices: 1.91 us -> 10.6 us  [on_device(): normed_theirs.append(lax.ppermute(normed[part], 'seq', partner))]
    ppermute x8, waiting for transfers between devices: 40.8 us -> 32.4 us  [move(): return lax.ppermute(value, 'seq', pairs)]
    ppermute x1, waiting for transfers between devices: 6.49 us -> 0.01 us  [pair_state(): received = lax.ppermute(send, 'seq', partner)]
    ppermute x8, starting transfers between devices: 10.7 us -> 16.4 us  [move(): return lax.ppermute(value, 'seq', pairs)]
    ppermute x7, starting transfers between devices: 2.74 us -> 7.4 us  [butterfly_sum(): lax.ppermute(value, axis, [(i, i ^ stride) for i in range(size)])]
    ppermute x1, waiting for transfers between devices: 0.01 us -> 3.56 us  [join_states(): return (own, lax.ppermute(other, 'seq', [(i, i ^ 1) for i in range(size)]))]
    ppermute x14, waiting for transfers between devices: 10.6 us -> 13.6 us  [move(): return lax.ppermute(value, 'seq', moves)]
    ppermute x3, waiting for transfers between devices: 13.7 us -> 10.7 us  [pair_state(): later.append(lax.ppermute(pair, 'seq', moves))]
  transfers between devices with their start and end apart: 43 -> 43, of which waited for: 16 -> 15; matrix products, arithmetic and copies ran while one was open for 2% -> 2% of each run, Pallas kernels for 28% -> 24%
where the time goes in v5:
time: 212 us
  waiting for transfers between devices  84.3 us (40%)
  Pallas kernels  63.2 us (30%)
  starting transfers between devices  51.6 us (24%)
  local copies, waits for them, and re-layouts  7.28 us (3%)
  other arithmetic  4.36 us (2%)
    ppermute x8, waiting for transfers between devices, move(): return lax.ppermute(value, 'seq', pairs)  32.4 us
    ppermute x8, starting transfers between devices, move(): return lax.ppermute(value, 'seq', pairs)  16.4 us
    ppermute x14, starting transfers between devices, move(): return lax.ppermute(value, 'seq', moves)  14.8 us
    ppermute x14, waiting for transfers between devices, move(): return lax.ppermute(value, 'seq', moves)  13.6 us
    ppermute x7, waiting for transfers between devices, butterfly_sum(): lax.ppermute(value, axis, [(i, i ^ stride) for i in range(size)])  13.4 us
    pallas_call x2, Pallas kernels, inside(): pl.pallas_call(functools.partial(inside_kernel, width // heads, start), n...  11.5 us
    ppermute x3, waiting for transfers between devices, pair_state(): later.append(lax.ppermute(pair, 'seq', moves))  10.7 us
    ppermute x2, waiting for transfers between devices, on_device(): normed_theirs.append(lax.ppermute(normed[part], 'seq', partner))  10.6 us
  transfers between devices with their start and end apart: 43, of which 15 were waited for; matrix products, arithmetic and copies ran while one was open for 2% of the time, Pallas kernels for 24%

profile of v5, /device:TPU:0, one launch (start us, length us, event | category | flops | bytes accessed | tf_op | source)
XLA Modules:
  0.0 211.9 jit_solution(3813533705398397576)
XLA Ops:
  0.6 5.1 %prepare.1 = (bf16[512,1280]{1,0:T(8,128)(2,1)}, bf16[80,1280]{1,0:T(8,128)(2,1)}, bf16[64,1280]{1,0:T(8,128)(2,1)}, f32[512,128]{1,0:T(8,128)}, f32[128,512]{1,...) custom-call(s32[64,1280]{1,0:T(8,128)} %packed.1, s32[10,512]{1,0:T(8,128)} %expo.1, ...), custom_call_target="tpu_custom_call" | custom-call | flops 3000000000 | bytes 8000000 | tf_op jit(solution)/shard_map/prepare/pallas_call | solution.py:121
  5.7 3.1 %collective-permute-start = (bf16[80,1280]{1,0:T(8,128)(2,1)}, bf16[80,1280]{1,0:T(8,128)(2,1)S(1)}, u32[]{:S(2)}, u32[]{:S(2)}) collective-permute-start(bf16[80,1280]{1,0:T(8,128)(2,1)} %get-tuple-element.50.rest_0_), channel_id=1, source_target_pairs={{0,8},{8,16},{16,24},{24,28},{28,20},{20,12},{12,4},{4,0},{1,9},{9... | collective-permute-start | bytes 614408 | tf_op jit(solution)/shard_map/ppermute | solution.py:810
  8.8 2.0 collective-permute-start.2
  10.8 2.0 collective-permute-start.4
  12.8 1.1 copy-done
  14.4 6.4 %inside.2.rest_0_ = f32[512,1280]{1,0:T(8,128)S(1)} custom-call(f32[512,128]{1,0:T(8,128)} %get-tuple-element.46.seg_t.refs_6_, f32[128,512]{1,0:T(8,128)} %get-tuple-element.47.seg, bf16[512,128]{1,0:T(8,128)(2,1)} %refs_5_.1, bf16[512,128]{1,0:T(8,128)(2,1)} %read.11, bf16[512,1280]{1,0:T(8,128)(2,1)} %get-tuple-element.48.x.refs_2_, ...), custom_call_target="tpu_custom_call" | custom-call | flops 10000000000 | bytes 2500000 | tf_op jit(solution)/shard_map/inside/pallas_call | solution.py:291
  20.9 1.6 collective-permute-start.24
  22.5 1.6 collective-permute-start.9
  24.5 1.6 collective-permute-start.7
  26.1 8.9 %collective-permute-done.9.refs_9_.rest_11_ = bf16[64,1280]{1,0:T(8,128)(2,1)S(1)} collective-permute-done((bf16[64,1280]{1,0:T(8,128)(2,1)S(1)}, bf16[64,1280]{1,0:T(8,128)(2,1)S(1)}, u32[]{:S(2)}, u32[]{:S(2)}) %collective-permute-start.9) | collective-permute-done | bytes 163872 | tf_op jit(solution)/shard_map/ppermute | solution.py:810
  35.1 2.0 collective-permute-start.14
  37.3 1.3 collective-permute-done.7.refs_7_.rest_3_
  38.7 2.5 %collective-permute-done.8.refs_8_.rest_4_ = bf16[80,1280]{1,0:T(8,128)(2,1)S(1)} collective-permute-done((bf16[80,1280]{1,0:T(8,128)(2,1)S(1)}, bf16[80,1280]{1,0:T(8,128)(2,1)S(1)}, u32[]{:S(2)}, u32[]{:S(2)}) %collective-permute-start.8) | collective-permute-done | bytes 204832 | tf_op jit(solution)/shard_map/ppermute | solution.py:810
  41.3 1.3 collective-permute-start.11
  42.6 5.1 %inside.3.refs_6_.y_local = f32[512,1280]{1,0:T(8,128)S(1)} custom-call(f32[512,128]{1,0:T(8,128)S(1)} %copy-done.13, f32[128,512]{1,0:T(8,128)S(1)} %copy-done.19, bf16[512,128]{1,0:T(8,128)(2,1)S(1)} %copy-done.12, bf16[512,128]{1,0:T(8,128)(2,1)S(1)} %copy-done.11, bf16[512,1280]{1,0:T(8,128)(2,1)S(1)} %copy-done.17, ...), custom_call_target="tpu_custom_call", output_to_operand_aliasing={{}: (6, {})} | custom-call | flops 10000000000 | bytes 2500000 | tf_op jit(solution)/shard_map/inside/pallas_call | solution.py:291
  48.4 0.7 collective-permute-start.12
  49.1 1.3 collective-permute-start.16
  50.4 0.7 collective-permute-start.13
  51.1 7.0 %cotangent.1 = (f32[512,1280]{1,0:T(8,128)S(1)}, bf16[4,320,512]{2,1,0:T(8,128)(2,1)S(1)}) custom-call(s32[5]{0:T(128)S(1)} %pad_add_fusion.1.refs_0_.owners, bf16[1280,2560]{1,0:T(8,128)(2,1)S(1)} %bitcast.13, bf16[512,640]{1,0:T(8,128)(2,1)S(1)} %copy-done.1, bf16[512,640]{1,0:T(8,128)(2,1)S(1)} %collective-permute-done.4.refs_3_, ...), custom_call_target="tpu_custom_call" | custom-call | flops 3355443200 | bytes 20000000 | tf_op jit(solution)/shard_map/cotangent/pallas_call | solution.py:183
  58.2 0.8 collective-permute-done.16.rest_15_
  59.0 5.2 %enter.1 = (f32[512,1280]{1,0:T(8,128)S(1)}, f32[1280,512]{1,0:T(8,128)S(1)}, f32[8,512]{1,0:T(8,128)S(1)}, f32[128,1280]{1,0:T(8,128)S(1)}, f32[8,1280]{1,0:T(8,128)S(1)}) custom-call(s32[9]{0:T(128)S(1)} %pad_add_fusion.sources.refs_0_, f32[512,1280]{1,0:T(8,128)S(1)} %inside.3.refs_6_.y_local, bf16[512,1280]{1,0:T(8,128)(2,1)S(1)} %copy-done.4, ...), custom_call_target="tpu_custom_call" | custom-call | flops 3000000000 | bytes 15000000 | tf_op jit(solution)/shard_map/enter/pallas_call | solution.py:372
  64.2 1.2 collective-permute-done.17
  65.4 1.3 collective-permute-start.18
  67.4 1.8 collective-permute-done.18
  69.5 5.6 %gate_grads.1 = (bf16[512,1280]{1,0:T(8,128)(2,1)}, f32[512,1280]{1,0:T(8,128)S(1)}, bf16[64,1280]{1,0:T(8,128)(2,1)S(1)}, f32[64,1280]{1,0:T(8,128)S(1)}, f32[8,1280]{1,0:T(8,128)S(1)}) custom-call(s32[9]{0:T(128)S(1)} %pad_add_fusion.sources.refs_0_, f32[512,1280]{1,0:T(8,128)S(1)} %get-tuple-element.54.y_ref.refs_1_, bf16[512,1280]{1,0:T(8,128)(2,1)S(1)} %copy-done.4, ...), custom_call_target="tpu_custom_call" | custom-call | flops 3000000000 | bytes 15000000 | tf_op jit(solution)/shard_map/gate_grads/pallas_call | solution.py:453
  75.1 0.8 collective-permute-start.19
  75.9 1.3 collective-permute-start.23
  77.1 0.8 collective-permute-start.35
  77.9 4.9 %inside_back.2 = (f32[512,1280]{1,0:T(8,128)S(1)}, f32[512,512]{1,0:T(8,128)S(1)}) custom-call(f32[512,128]{1,0:T(8,128)S(1)} %copy-done.13, f32[128,512]{1,0:T(8,128)S(1)} %copy-done.19, bf16[512,128]{1,0:T(8,128)(2,1)S(1)} %copy-done.12, bf16[512,128]{1,0:T(8,128)(2,1)S(1)} %copy-done.11, bf16[512,1280]{1,0:T(8,128)(2,1)S(1)} %copy-done.17, ...), custom_call_target="tpu_custom_call" | custom-call | flops 10000000000 | bytes 4000000 | tf_op jit(solution)/shard_map/inside_back/pallas_call | solution.py:549
  82.8 10.6 %collective-permute-done.23.theirs = bf16[512,512]{1,0:T(8,128)(2,1)S(1)} collective-permute-done((bf16[512,512]{1,0:T(8,128)(2,1)S(1)}, bf16[512,512]{1,0:T(8,128)(2,1)S(1)}, u32[]{:S(2)}, u32[]{:S(2)}) %collective-permute-start.23) | collective-permute-done | bytes 524320 | tf_op jit(solution)/shard_map/ppermute | solution.py:928
  93.4 1.9 product.2
  95.4 0.8 copy-done.14
  96.2 3.2 %collective-permute-start.28 = (bf16[320,512]{1,0:T(8,128)(2,1)S(1)}, bf16[320,512]{1,0:T(8,128)(2,1)S(1)}, u32[]{:S(2)}, u32[]{:S(2)}) collective-permute-start(bf16[320,512]{1,0:T(8,128)(2,1)S(1)} %get-tuple-element.70), channel_id=1, source_target_pairs={{0,8},{4,12},{24,16},{28,20},{1,9},{5,13},{25,17},{29,21},{2,10},{... | collective-permute-start | bytes 983048 | tf_op jit(solution)/shard_map/ppermute | solution.py:862
  99.4 5.6 %inside_back.3 = (f32[512,1280]{1,0:T(8,128)S(1)}, f32[512,128]{1,0:T(8,128)S(1)}, f32[512,128]{1,0:T(8,128)S(1)}) custom-call(f32[512,128]{1,0:T(8,128)S(1)} %copy-done.13, f32[128,512]{1,0:T(8,128)S(1)} %copy-done.19, bf16[512,128]{1,0:T(8,128)(2,1)S(1)} %copy-done.12, bf16[512,128]{1,0:T(8,128)(2,1)S(1)} %copy-done.11, ...), custom_call_target="tpu_custom_call", output_to_operand_aliasing={{0}: (6, {})} | custom-call | flops 10000000000 | bytes 4000000 | tf_op jit(solution)/shard_map/inside_back/pallas_call | solution.py:549
  105.7 1.3 collective-permute-start.20
  107.0 1.3 collective-permute-start.21
  108.3 1.5 collective-permute-start.22
  109.9 3.9 %collective-permute-done.20.refs_4_ = bf16[64,1280]{1,0:T(8,128)(2,1)S(1)} collective-permute-done((bf16[64,1280]{1,0:T(8,128)(2,1)S(1)}, bf16[64,1280]{1,0:T(8,128)(2,1)S(1)}, u32[]{:S(2)}, u32[]{:S(2)}) %collective-permute-start.20) | collective-permute-done | bytes 163872 | tf_op jit(solution)/shard_map/ppermute | solution.py:621
  113.8 6.9 %collective-permute-done.21.refs_5_ = bf16[64,1280]{1,0:T(8,128)(2,1)S(1)} collective-permute-done((bf16[64,1280]{1,0:T(8,128)(2,1)S(1)}, bf16[64,1280]{1,0:T(8,128)(2,1)S(1)}, u32[]{:S(2)}, u32[]{:S(2)}) %collective-permute-start.21) | collective-permute-done | bytes 163872 | tf_op jit(solution)/shard_map/ppermute | solution.py:621
  120.7 0.7 shard_map.180
  121.4 1.8 collective-permute-start.29
  123.3 3.6 %collective-permute-done.29.refs_14_ = bf16[64,1280]{1,0:T(8,128)(2,1)S(1)} collective-permute-done((bf16[64,1280]{1,0:T(8,128)(2,1)S(1)}, bf16[64,1280]{1,0:T(8,128)(2,1)S(1)}, u32[]{:S(2)}, u32[]{:S(2)}) %collective-permute-start.29) | collective-permute-done | bytes 163872 | tf_op jit(solution)/shard_map/ppermute | solution.py:632
  126.8 7.1 %leave.1 = (bf16[512,1280]{1,0:T(8,128)(2,1)}, f32[2,512,128]{2,1,0:T(8,128)S(1)}, f32[20,512]{1,0:T(8,128)}) custom-call(s32[9]{0:T(128)S(1)} %pad_add_fusion.sources.refs_0_, f32[512,1280]{1,0:T(8,128)S(1)} %get-tuple-element.54.y_ref.refs_1_, bf16[512,1280]{1,0:T(8,128)(2,1)S(1)} %copy-done.17, f32[512,1280]{1,0:T(8,128)S(1)} %get-tuple-element.57.grad_y.refs_3_, ...), custom_call_target="tpu_custom_call" | custom-call | flops 5000000000 | bytes 20000000 | tf_op jit(solution)/shard_map/leave/pallas_call | solution.py:700
  133.9 3.3 %product.3 = (bf16[320,768]{1,0:T(8,128)(2,1)}, bf16[320,768]{1,0:T(8,128)(2,1)S(1)}, bf16[320,768]{1,0:T(8,128)(2,1)S(1)}, f32[320,768]{1,0:T(8,128)S(1)}) custom-call(s32[1]{0:T(128)} %bitcast.4.group, bf16[768,512]{1,0:T(8,128)(2,1)S(1)} %multiply_convert_fusion.mine, bf16[768,512]{1,0:T(8,128)(2,1)S(1)} %collective-permute-done.35.theirs, ...), custom_call_target="tpu_custom_call" | custom-call | flops 2013265920 | bytes 5000000 | tf_op jit(solution)/shard_map/product/pallas_call | solution.py:749
  137.2 1.3 collective-permute-start.38
  139.3 4.0 %collective-permute-start.41 = (bf16[320,512]{1,0:T(8,128)(2,1)S(1)}, bf16[320,512]{1,0:T(8,128)(2,1)S(1)}, u32[]{:S(2)}, u32[]{:S(2)}) collective-permute-start(bf16[320,512]{1,0:T(8,128)(2,1)S(1)} %get-tuple-element.83), channel_id=1, source_target_pairs={{0,8},{4,12},{8,0},{12,4},{16,24},{20,28},{24,16},{28,20},{1,9},{5... | collective-permute-start | bytes 983048 | tf_op jit(solution)/shard_map/ppermute | solution.py:862
  143.3 7.9 %collective-permute-done.32 = f32[8,1280]{1,0:T(8,128)S(1)} collective-permute-done((f32[8,1280]{1,0:T(8,128)S(1)}, f32[8,1280]{1,0:T(8,128)S(1)}, u32[]{:S(2)}, u32[]{:S(2)}) %collective-permute-start.32) | collective-permute-done | bytes 40992 | tf_op jit(solution)/shard_map/ppermute | solution.py:840
  151.2 2.6 %collective-permute-start.33 = (f32[8,1280]{1,0:T(8,128)S(1)}, f32[8,1280]{1,0:T(8,128)S(1)}, u32[]{:S(2)}, u32[]{:S(2)}) collective-permute-start(f32[8,1280]{1,0:T(8,128)S(1)} %add.70), channel_id=1, source_target_pairs={{0,16},{4,20},{8,24},{12,28},{16,0},{20,4},{24,8},{28,12},{1,17},{... | collective-permute-start | bytes 122888 | tf_op jit(solution)/shard_map/ppermute | solution.py:840
  153.9 0.9 add.68
  154.8 1.5 collective-permute-start.31
  156.3 2.6 %collective-permute-done.33 = f32[8,1280]{1,0:T(8,128)S(1)} collective-permute-done((f32[8,1280]{1,0:T(8,128)S(1)}, f32[8,1280]{1,0:T(8,128)S(1)}, u32[]{:S(2)}, u32[]{:S(2)}) %collective-permute-start.33) | collective-permute-done | bytes 40992 | tf_op jit(solution)/shard_map/ppermute | solution.py:840
  158.9 1.8 collective-permute-start.34
  160.7 3.4 %collective-permute-start.42 = (bf16[320,512]{1,0:T(8,128)(2,1)S(1)}, bf16[320,512]{1,0:T(8,128)(2,1)}, u32[]{:S(2)}, u32[]{:S(2)}) collective-permute-start(bf16[320,512]{1,0:T(8,128)(2,1)S(1)} %add_convert_fusion.1.refs_8_), channel_id=1, source_target_pairs={{0,16},{4,20},{8,24},{12,28},{16,0},{20,4},{24,8},{28,12},{1,17},{... | collective-permute-start | bytes 983048 | tf_op jit(solution)/shard_map/ppermute | solution.py:862
  164.0 0.9 add_convert_fusion
  166.4 3.1 %collective-permute-start.37 = (bf16[320,768]{1,0:T(8,128)(2,1)S(1)}, bf16[320,768]{1,0:T(8,128)(2,1)S(1)}, u32[]{:S(2)}, u32[]{:S(2)}) collective-permute-start(bf16[320,768]{1,0:T(8,128)(2,1)S(1)} %get-tuple-element.80), channel_id=1, source_target_pairs={{0,8},{4,12},{8,0},{12,4},{16,24},{20,28},{24,16},{28,20},{1,9},{5... | collective-permute-start | bytes 1474568 | tf_op jit(solution)/shard_map/ppermute | solution.py:862
  169.5 0.7 copy-done.7
  171.6 7.7 %collective-permute-done.42.rest_2_ = bf16[320,512]{1,0:T(8,128)(2,1)} collective-permute-done((bf16[320,512]{1,0:T(8,128)(2,1)S(1)}, bf16[320,512]{1,0:T(8,128)(2,1)}, u32[]{:S(2)}, u32[]{:S(2)}) %collective-permute-start.42) | collective-permute-done | bytes 327712 | tf_op jit(solution)/shard_map/ppermute | solution.py:862
  179.3 1.0 copy-done.6
  180.2 1.0 copy-done.8
  181.2 1.1 copy-done.15
  182.3 1.9 finish.2.rest_3_
  184.2 1.3 add.69
  186.2 24.0 %collective-permute-done.39.rest_2_ = bf16[320,768]{1,0:T(8,128)(2,1)S(1)} collective-permute-done((bf16[320,768]{1,0:T(8,128)(2,1)}, bf16[320,768]{1,0:T(8,128)(2,1)S(1)}, u32[]{:S(2)}, u32[]{:S(2)}) %collective-permute-start.39) | collective-permute-done | bytes 491552 | tf_op jit(solution)/shard_map/ppermute | solution.py:862
  210.2 1.7 finish.3
  (115 shorter events, 7.9 us)
Async XLA Ops:
  5.7 18.3 %collective-permute-start = (bf16[80,1280]{1,0:T(8,128)(2,1)}, bf16[80,1280]{1,0:T(8,128)(2,1)S(1)}, u32[]{:S(2)}, u32[]{:S(2)}) collective-permute-start(bf16[80,1280]{1,0:T(8,128)(2,1)} %get-tuple-element.50.rest_0_), channel_id=1, source_target_pairs={{0,8},{8,16},{16,24},{24,28},{28,20},{20,12},{12,4},{4,0},{1,9},{9... | collective-permute-start | bytes 614408 | tf_op jit(solution)/shard_map/ppermute | solution.py:810
  8.8 15.7 %collective-permute-start.1 = (bf16[80,1280]{1,0:T(8,128)(2,1)}, bf16[80,1280]{1,0:T(8,128)(2,1)S(1)}, u32[]{:S(2)}, u32[]{:S(2)}) collective-permute-start(bf16[80,1280]{1,0:T(8,128)(2,1)} %get-tuple-element.50.rest_0_), channel_id=1, source_target_pairs={{8,0},{16,8},{24,16},{28,24},{20,28},{12,20},{4,12},{0,4},{9,1},{1... | collective-permute-start | bytes 614408 | tf_op jit(solution)/shard_map/ppermute | solution.py:810
  8.8 12.1 %collective-permute-start.2 = (bf16[64,1280]{1,0:T(8,128)(2,1)}, bf16[64,1280]{1,0:T(8,128)(2,1)S(1)}, u32[]{:S(2)}, u32[]{:S(2)}) collective-permute-start(bf16[64,1280]{1,0:T(8,128)(2,1)} %get-tuple-element.51.rest_8_), channel_id=1, source_target_pairs={{0,8},{8,16},{16,24},{24,28},{28,20},{20,12},{12,4},{4,0},{1,9},{9... | collective-permute-start | bytes 491528 | tf_op jit(solution)/shard_map/ppermute | solution.py:810
  10.8 11.6 %collective-permute-start.3 = (bf16[64,1280]{1,0:T(8,128)(2,1)}, bf16[64,1280]{1,0:T(8,128)(2,1)S(1)}, u32[]{:S(2)}, u32[]{:S(2)}) collective-permute-start(bf16[64,1280]{1,0:T(8,128)(2,1)} %get-tuple-element.51.rest_8_), channel_id=1, source_target_pairs={{8,0},{16,8},{24,16},{28,24},{20,28},{12,20},{4,12},{0,4},{9,1},{1... | collective-permute-start | bytes 491528 | tf_op jit(solution)/shard_map/ppermute | solution.py:810
  10.8 31.7 %collective-permute-start.4 = (bf16[512,640]{1,0:T(8,128)(2,1)}, bf16[512,640]{1,0:T(8,128)(2,1)S(1)}, u32[]{:S(2)}, u32[]{:S(2)}) collective-permute-start(bf16[512,640]{1,0:T(8,128)(2,1)} %shard.1), channel_id=1, source_target_pairs={{0,2},{1,3},{2,0},{3,1},{4,6},{5,7},{6,4},{7,5},{8,10},{9,11},{10,... | collective-permute-start | bytes 1966088 | tf_op jit(solution)/shard_map/ppermute | solution.py:850
  12.8 1.1 copy-start
  14.3 6.5 %copy-start.23 = (s32[8]{0:T(128)S(1)}, s32[8]{0:T(128)}, u32[]{:S(2)}) copy-start(s32[8]{0:T(128)} %constant.72.clone) | copy-start | bytes 100
  14.3 10.2 %copy-start.22 = (s32[4]{0:T(128)S(1)}, s32[4]{0:T(128)}, u32[]{:S(2)}) copy-start(s32[4]{0:T(128)} %constant.73.clone) | copy-start | bytes 52
  14.4 22.8 %copy-start.21 = (f32[1280]{0:T(1024)S(1)}, f32[1280]{0:T(1024)}, u32[]{:S(2)}) copy-start(f32[1280]{0:T(1024)} %param.19) | copy-start | bytes 15364
  14.4 22.9 %copy-start.1 = (bf16[512,640]{1,0:T(8,128)(2,1)S(1)}, bf16[512,640]{1,0:T(8,128)(2,1)}, u32[]{:S(2)}) copy-start(bf16[512,640]{1,0:T(8,128)(2,1)} %shard.1) | copy-start | bytes 1966084
  14.4 28.2 %copy-start.11 = (bf16[512,128]{1,0:T(8,128)(2,1)S(1)}, bf16[512,128]{1,0:T(8,128)(2,1)}, u32[]{:S(2)}) copy-start(bf16[512,128]{1,0:T(8,128)(2,1)} %read.11) | copy-start | bytes 393220
  14.4 28.2 %copy-start.12 = (bf16[512,128]{1,0:T(8,128)(2,1)S(1)}, bf16[512,128]{1,0:T(8,128)(2,1)}, u32[]{:S(2)}) copy-start(bf16[512,128]{1,0:T(8,128)(2,1)} %refs_5_.1) | copy-start | bytes 393220
  14.4 28.2 %copy-start.13 = (f32[512,128]{1,0:T(8,128)S(1)}, f32[512,128]{1,0:T(8,128)}, u32[]{:S(2)}) copy-start(f32[512,128]{1,0:T(8,128)} %get-tuple-element.46.seg_t.refs_6_) | copy-start | bytes 786436
  14.4 28.2 %copy-start.17 = (bf16[512,1280]{1,0:T(8,128)(2,1)S(1)}, bf16[512,1280]{1,0:T(8,128)(2,1)}, u32[]{:S(2)}) copy-start(bf16[512,1280]{1,0:T(8,128)(2,1)} %get-tuple-element.48.x.refs_2_) | copy-start | bytes 3932164
  14.4 28.2 %copy-start.19 = (f32[128,512]{1,0:T(8,128)S(1)}, f32[128,512]{1,0:T(8,128)}, u32[]{:S(2)}) copy-start(f32[128,512]{1,0:T(8,128)} %get-tuple-element.47.seg) | copy-start | bytes 786436
  14.4 28.2 %copy-start.20 = (f32[8,1280]{1,0:T(8,128)S(1)}, f32[8,1280]{1,0:T(8,128)}, u32[]{:S(2)}) copy-start(f32[8,1280]{1,0:T(8,128)} %get-tuple-element.49.skip.refs_9_) | copy-start | bytes 122884
  20.9 16.4 %collective-permute-start.24 = (bf16[320,512]{1,0:T(8,128)(2,1)S(1)}, bf16[320,512]{1,0:T(8,128)(2,1)S(1)}, u32[]{:S(2)}, u32[]{:S(2)}) collective-permute-start(bf16[320,512]{1,0:T(8,128)(2,1)S(1)} %pick.1), channel_id=1, source_target_pairs={{0,4},{4,0},{8,12},{12,8},{16,20},{20,16},{24,28},{28,24},{1,5},{5... | collective-permute-start | bytes 983048 | tf_op jit(solution)/shard_map/ppermute | solution.py:896
  22.5 12.6 %collective-permute-start.9 = (bf16[64,1280]{1,0:T(8,128)(2,1)S(1)}, bf16[64,1280]{1,0:T(8,128)(2,1)S(1)}, u32[]{:S(2)}, u32[]{:S(2)}) collective-permute-start(bf16[64,1280]{1,0:T(8,128)(2,1)S(1)} %collective-permute-done.2.rest_3_.rest_9_), channel_id=1, source_target_pairs={{0,8},{8,16},{16,24},{24,28},{28,20},{20,12},{12,4},{4,0},{1,9},{9... | collective-permute-start | bytes 491528 | tf_op jit(solution)/shard_map/ppermute | solution.py:810
  24.0 11.0 %collective-permute-start.10 = (bf16[64,1280]{1,0:T(8,128)(2,1)S(1)}, bf16[64,1280]{1,0:T(8,128)(2,1)S(1)}, u32[]{:S(2)}, u32[]{:S(2)}) collective-permute-start(bf16[64,1280]{1,0:T(8,128)(2,1)S(1)} %collective-permute-done.3.rest_4_.rest_10_), channel_id=1, source_target_pairs={{8,0},{16,8},{24,16},{28,24},{20,28},{12,20},{4,12},{0,4},{9,1},{1... | collective-permute-start | bytes 491528 | tf_op jit(solution)/shard_map/ppermute | solution.py:810
  24.5 14.2 %collective-permute-start.7 = (bf16[80,1280]{1,0:T(8,128)(2,1)S(1)}, bf16[80,1280]{1,0:T(8,128)(2,1)S(1)}, u32[]{:S(2)}, u32[]{:S(2)}) collective-permute-start(bf16[80,1280]{1,0:T(8,128)(2,1)S(1)} %collective-permute-done.rest_1_), channel_id=1, source_target_pairs={{0,8},{8,16},{16,24},{24,28},{28,20},{20,12},{12,4},{4,0},{1,9},{9... | collective-permute-start | bytes 614408 | tf_op jit(solution)/shard_map/ppermute | solution.py:810
  35.0 6.1 %collective-permute-start.8 = (bf16[80,1280]{1,0:T(8,128)(2,1)S(1)}, bf16[80,1280]{1,0:T(8,128)(2,1)S(1)}, u32[]{:S(2)}, u32[]{:S(2)}) collective-permute-start(bf16[80,1280]{1,0:T(8,128)(2,1)S(1)} %collective-permute-done.1.rest_2_), channel_id=1, source_target_pairs={{8,0},{16,8},{24,16},{28,24},{20,28},{12,20},{4,12},{0,4},{9,1},{1... | collective-permute-start | bytes 614408 | tf_op jit(solution)/shard_map/ppermute | solution.py:810
  35.1 6.2 %collective-permute-start.14 = (bf16[64,1280]{1,0:T(8,128)(2,1)S(1)}, bf16[64,1280]{1,0:T(8,128)(2,1)S(1)}, u32[]{:S(2)}, u32[]{:S(2)}) collective-permute-start(bf16[64,1280]{1,0:T(8,128)(2,1)S(1)} %collective-permute-done.9.refs_9_.rest_11_), channel_id=1, source_target_pairs={{0,8},{8,16},{16,24},{24,28},{28,20},{20,12},{12,4},{4,0},{1,9},{9... | collective-permute-start | bytes 491528 | tf_op jit(solution)/shard_map/ppermute | solution.py:810
  37.2 14.0 %slice-start = ((s8[6553600]{0:T(1024)(128)(4,1)}), s8[4194304]{0:T(1024)(128)(4,1)S(1)}, s32[]{:S(2)}) async-start(s8[6553600]{0:T(1024)(128)(4,1)} %bitcast.12), calls=%async_computation | async-start | bytes 8388608
  37.2 13.9 %slice-start.1 = ((s8[6553600]{0:T(1024)(128)(4,1)}), s8[2359296]{0:T(1024)(128)(4,1)S(1)}, s32[]{:S(2)}) async-start(s8[6553600]{0:T(1024)(128)(4,1)} %bitcast.12), calls=%async_computation.1 | async-start | bytes 4718592
  37.3 11.8 %collective-permute-start.5 = (bf16[512,640]{1,0:T(8,128)(2,1)S(1)}, bf16[512,640]{1,0:T(8,128)(2,1)S(1)}, u32[]{:S(2)}, u32[]{:S(2)}) collective-permute-start(bf16[512,640]{1,0:T(8,128)(2,1)S(1)} %copy-done.1), channel_id=1, source_target_pairs={{0,1},{1,0},{2,3},{3,2},{4,5},{5,4},{6,7},{7,6},{8,9},{9,8},{10,11... | collective-permute-start | bytes 1966088 | tf_op jit(solution)/shard_map/ppermute | solution.py:850
  38.7 9.1 %collective-permute-start.15 = (bf16[64,1280]{1,0:T(8,128)(2,1)S(1)}, bf16[64,1280]{1,0:T(8,128)(2,1)S(1)}, u32[]{:S(2)}, u32[]{:S(2)}) collective-permute-start(bf16[64,1280]{1,0:T(8,128)(2,1)S(1)} %collective-permute-done.10.refs_10_.rest_12_), channel_id=1, source_target_pairs={{8,0},{16,8},{24,16},{28,24},{20,28},{12,20},{4,12},{0,4},{9,1},{1... | collective-permute-start | bytes 491528 | tf_op jit(solution)/shard_map/ppermute | solution.py:810
  41.2 9.2 %collective-permute-start.25 = (bf16[320,512]{1,0:T(8,128)(2,1)S(1)}, bf16[320,512]{1,0:T(8,128)(2,1)S(1)}, u32[]{:S(2)}, u32[]{:S(2)}) collective-permute-start(bf16[320,512]{1,0:T(8,128)(2,1)S(1)} %collective-permute-done.24.rest_0_), channel_id=1, source_target_pairs={{0,2},{1,3},{2,0},{3,1},{4,6},{5,7},{6,4},{7,5},{8,10},{9,11},{10,... | collective-permute-start | bytes 983048 | tf_op jit(solution)/shard_map/ppermute | solution.py:850
  41.3 7.1 %collective-permute-start.11 = (bf16[80,1280]{1,0:T(8,128)(2,1)S(1)}, bf16[80,1280]{1,0:T(8,128)(2,1)S(1)}, u32[]{:S(2)}, u32[]{:S(2)}) collective-permute-start(bf16[80,1280]{1,0:T(8,128)(2,1)S(1)} %collective-permute-done.7.refs_7_.rest_3_), channel_id=1, source_target_pairs={{0,8},{8,16},{16,24},{24,28},{28,20},{20,12},{12,4},{4,0},{1,9},{9... | collective-permute-start | bytes 614408 | tf_op jit(solution)/shard_map/ppermute | solution.py:810
  42.6 8.6 %collective-permute-start.6 = (bf16[512,640]{1,0:T(8,128)(2,1)S(1)}, bf16[512,640]{1,0:T(8,128)(2,1)S(1)}, u32[]{:S(2)}, u32[]{:S(2)}) collective-permute-start(bf16[512,640]{1,0:T(8,128)(2,1)S(1)} %collective-permute-done.4.refs_3_), channel_id=1, source_target_pairs={{0,1},{1,0},{2,3},{3,2},{4,5},{5,4},{6,7},{7,6},{8,9},{9,8},{10,11... | collective-permute-start | bytes 1966088 | tf_op jit(solution)/shard_map/ppermute | solution.py:850
  47.7 11.2 %copy-start.4 = (bf16[512,1280]{1,0:T(8,128)(2,1)S(1)}, bf16[512,1280]{1,0:T(8,128)(2,1)}, u32[]{:S(2)}) copy-start(bf16[512,1280]{1,0:T(8,128)(2,1)} %gate.3) | copy-start | bytes 3932164
  47.7 11.2 %copy-start.9 = (bf16[80,1280]{1,0:T(8,128)(2,1)S(1)}, bf16[80,1280]{1,0:T(8,128)(2,1)}, u32[]{:S(2)}) copy-start(bf16[80,1280]{1,0:T(8,128)(2,1)} %get-tuple-element.50.rest_0_) | copy-start | bytes 614404
  47.8 11.2 %copy-start.10 = (bf16[64,1280]{1,0:T(8,128)(2,1)S(1)}, bf16[64,1280]{1,0:T(8,128)(2,1)}, u32[]{:S(2)}) copy-start(bf16[64,1280]{1,0:T(8,128)(2,1)} %get-tuple-element.51.rest_8_) | copy-start | bytes 491524
  47.8 11.2 %copy-start.16 = (bf16[256,1280]{1,0:T(8,128)(2,1)S(1)}, bf16[256,1280]{1,0:T(8,128)(2,1)}, u32[]{:S(2)}) copy-start(bf16[256,1280]{1,0:T(8,128)(2,1)} %get-tuple-element.53.spread2.refs_8_) | copy-start | bytes 1966084
  47.8 18.9 %collective-permute-start.26 = (bf16[320,512]{1,0:T(8,128)(2,1)S(1)}, bf16[320,512]{1,0:T(8,128)(2,1)S(1)}, u32[]{:S(2)}, u32[]{:S(2)}) collective-permute-start(bf16[320,512]{1,0:T(8,128)(2,1)S(1)} %collective-permute-done.24.rest_0_), channel_id=1, source_target_pairs={{0,1},{1,0},{2,3},{3,2},{4,5},{5,4},{6,7},{7,6},{8,9},{9,8},{10,11... | collective-permute-start | bytes 983048 | tf_op jit(solution)/shard_map/ppermute | solution.py:850
  48.4 9.8 %collective-permute-start.12 = (bf16[80,1280]{1,0:T(8,128)(2,1)S(1)}, bf16[80,1280]{1,0:T(8,128)(2,1)S(1)}, u32[]{:S(2)}, u32[]{:S(2)}) collective-permute-start(bf16[80,1280]{1,0:T(8,128)(2,1)S(1)} %collective-permute-done.8.refs_8_.rest_4_), channel_id=1, source_target_pairs={{8,0},{16,8},{24,16},{28,24},{20,28},{12,20},{4,12},{0,4},{9,1},{1... | collective-permute-start | bytes 614408 | tf_op jit(solution)/shard_map/ppermute | solution.py:810
  49.1 9.8 %collective-permute-start.16 = (bf16[64,1280]{1,0:T(8,128)(2,1)S(1)}, bf16[64,1280]{1,0:T(8,128)(2,1)S(1)}, u32[]{:S(2)}, u32[]{:S(2)}) collective-permute-start(bf16[64,1280]{1,0:T(8,128)(2,1)S(1)} %collective-permute-done.15.rest_14_), channel_id=1, source_target_pairs={{8,0},{16,8},{24,16},{28,24},{20,28},{12,20},{4,12},{0,4},{9,1},{1... | collective-permute-start | bytes 491528 | tf_op jit(solution)/shard_map/ppermute | solution.py:810
  50.4 8.5 %collective-permute-start.13 = (bf16[80,1280]{1,0:T(8,128)(2,1)S(1)}, bf16[80,1280]{1,0:T(8,128)(2,1)S(1)}, u32[]{:S(2)}, u32[]{:S(2)}) collective-permute-start(bf16[80,1280]{1,0:T(8,128)(2,1)S(1)} %collective-permute-done.11.rest_5_), channel_id=1, source_target_pairs={{0,8},{8,16},{16,24},{24,28},{28,20},{20,12},{12,4},{4,0},{1,9},{9... | collective-permute-start | bytes 614408 | tf_op jit(solution)/shard_map/ppermute | solution.py:810
  51.1 15.6 %collective-permute-start.27 = (bf16[320,512]{1,0:T(8,128)(2,1)S(1)}, bf16[320,512]{1,0:T(8,128)(2,1)S(1)}, u32[]{:S(2)}, u32[]{:S(2)}) collective-permute-start(bf16[320,512]{1,0:T(8,128)(2,1)S(1)} %collective-permute-done.25.rest_1_), channel_id=1, source_target_pairs={{0,1},{1,0},{2,3},{3,2},{4,5},{5,4},{6,7},{7,6},{8,9},{9,8},{10,11... | collective-permute-start | bytes 983048 | tf_op jit(solution)/shard_map/ppermute | solution.py:850
  64.1 1.2 collective-permute-start.17
  65.4 3.7 %collective-permute-start.18 = (f32[8,512]{1,0:T(8,128)S(1)}, f32[8,512]{1,0:T(8,128)S(1)}, u32[]{:S(2)}, u32[]{:S(2)}) collective-permute-start(f32[8,512]{1,0:T(8,128)S(1)} %add.63), channel_id=1, source_target_pairs={{0,2},{1,3},{2,0},{3,1},{4,6},{5,7},{6,4},{7,5},{8,10},{9,11},{10,... | collective-permute-start | bytes 49160 | tf_op jit(solution)/shard_map/ppermute | solution.py:840
  67.3 2.1 %copy-start.18 = (bf16[128,512]{1,0:T(8,128)(2,1)S(1)}, bf16[128,512]{1,0:T(8,128)(2,1)}, u32[]{:S(2)}) copy-start(bf16[128,512]{1,0:T(8,128)(2,1)} %get-tuple-element.56.read_t) | copy-start | bytes 393220
  75.1 29.9 %collective-permute-start.19 = (bf16[64,1280]{1,0:T(8,128)(2,1)S(1)}, bf16[64,1280]{1,0:T(8,128)(2,1)S(1)}, u32[]{:S(2)}, u32[]{:S(2)}) collective-permute-start(bf16[64,1280]{1,0:T(8,128)(2,1)S(1)} %get-tuple-element.66), channel_id=1, source_target_pairs={{0,4},{4,0},{8,12},{12,8},{16,20},{20,16},{24,28},{28,24},{1,5},{5... | collective-permute-start | bytes 491528 | tf_op jit(solution)/shard_map/ppermute | solution.py:615
  75.9 17.6 %collective-permute-start.23 = (bf16[512,512]{1,0:T(8,128)(2,1)S(1)}, bf16[512,512]{1,0:T(8,128)(2,1)S(1)}, u32[]{:S(2)}, u32[]{:S(2)}) collective-permute-start(bf16[512,512]{1,0:T(8,128)(2,1)S(1)} %multiply_convert_fusion.1.mine), channel_id=1, source_target_pairs={{0,4},{4,0},{8,12},{12,8},{16,20},{20,16},{24,28},{28,24},{1,5},{5... | collective-permute-start | bytes 1572872 | tf_op jit(solution)/shard_map/ppermute | solution.py:928
  77.1 56.8 %collective-permute-start.35 = (bf16[768,512]{1,0:T(8,128)(2,1)S(1)}, bf16[768,512]{1,0:T(8,128)(2,1)S(1)}, u32[]{:S(2)}, u32[]{:S(2)}) collective-permute-start(bf16[768,512]{1,0:T(8,128)(2,1)S(1)} %multiply_convert_fusion.mine), channel_id=1, source_target_pairs={{0,4},{4,0},{8,12},{12,8},{16,20},{20,16},{24,28},{28,24},{1,5},{5... | collective-permute-start | bytes 2359304 | tf_op jit(solution)/shard_map/ppermute | solution.py:928
  96.2 13.7 %collective-permute-start.28 = (bf16[320,512]{1,0:T(8,128)(2,1)S(1)}, bf16[320,512]{1,0:T(8,128)(2,1)S(1)}, u32[]{:S(2)}, u32[]{:S(2)}) collective-permute-start(bf16[320,512]{1,0:T(8,128)(2,1)S(1)} %get-tuple-element.70), channel_id=1, source_target_pairs={{0,8},{4,12},{24,16},{28,20},{1,9},{5,13},{25,17},{29,21},{2,10},{... | collective-permute-start | bytes 983048 | tf_op jit(solution)/shard_map/ppermute | solution.py:862
  105.7 8.1 %collective-permute-start.20 = (bf16[64,1280]{1,0:T(8,128)(2,1)S(1)}, bf16[64,1280]{1,0:T(8,128)(2,1)S(1)}, u32[]{:S(2)}, u32[]{:S(2)}) collective-permute-start(bf16[64,1280]{1,0:T(8,128)(2,1)S(1)} %shard_map.179), channel_id=1, source_target_pairs={{8,0},{12,4},{16,8},{20,12},{24,16},{28,20},{9,1},{13,5},{17,9},{2... | collective-permute-start | bytes 491528 | tf_op jit(solution)/shard_map/ppermute | solution.py:621
  107.0 13.7 %collective-permute-start.21 = (bf16[64,1280]{1,0:T(8,128)(2,1)S(1)}, bf16[64,1280]{1,0:T(8,128)(2,1)S(1)}, u32[]{:S(2)}, u32[]{:S(2)}) collective-permute-start(bf16[64,1280]{1,0:T(8,128)(2,1)S(1)} %shard_map.179), channel_id=1, source_target_pairs={{16,0},{20,4},{24,8},{28,12},{17,1},{21,5},{25,9},{29,13},{18,2},{... | collective-permute-start | bytes 491528 | tf_op jit(solution)/shard_map/ppermute | solution.py:621
  108.3 12.4 %collective-permute-start.22 = (bf16[64,1280]{1,0:T(8,128)(2,1)S(1)}, bf16[64,1280]{1,0:T(8,128)(2,1)S(1)}, u32[]{:S(2)}, u32[]{:S(2)}) collective-permute-start(bf16[64,1280]{1,0:T(8,128)(2,1)S(1)} %shard_map.179), channel_id=1, source_target_pairs={{24,0},{28,4},{25,1},{29,5},{26,2},{30,6},{27,3},{31,7}} | collective-permute-start | bytes 491528 | tf_op jit(solution)/shard_map/ppermute | solution.py:621
  121.4 5.4 %collective-permute-start.29 = (bf16[64,1280]{1,0:T(8,128)(2,1)S(1)}, bf16[64,1280]{1,0:T(8,128)(2,1)S(1)}, u32[]{:S(2)}, u32[]{:S(2)}) collective-permute-start(bf16[64,1280]{1,0:T(8,128)(2,1)S(1)} %get-tuple-element.72), channel_id=1, source_target_pairs={{0,4},{4,0},{8,12},{12,8},{16,20},{20,16},{24,28},{28,24},{1,5},{5... | collective-permute-start | bytes 491528 | tf_op jit(solution)/shard_map/ppermute | solution.py:632
  133.9 19.9 %collective-permute-start.30 = (f32[2,512,128]{2,1,0:T(8,128)S(1)}, f32[2,512,128]{2,1,0:T(8,128)S(1)}, u32[]{:S(2)}, u32[]{:S(2)}) collective-permute-start(f32[2,512,128]{2,1,0:T(8,128)S(1)} %get-tuple-element.75), channel_id=1, source_target_pairs={{0,1},{1,0},{2,3},{3,2},{4,5},{5,4},{6,7},{7,6},{8,9},{9,8},{10,11... | collective-permute-start | bytes 1572872 | tf_op jit(solution)/shard_map/ppermute | solution.py:840
  137.2 23.4 %collective-permute-start.38 = (bf16[320,768]{1,0:T(8,128)(2,1)}, bf16[320,768]{1,0:T(8,128)(2,1)S(1)}, u32[]{:S(2)}, u32[]{:S(2)}) collective-permute-start(bf16[320,768]{1,0:T(8,128)(2,1)} %get-tuple-element.79), channel_id=1, source_target_pairs={{0,8},{4,12},{24,16},{28,20},{1,9},{5,13},{25,17},{29,21},{2,10},{... | collective-permute-start | bytes 1474568 | tf_op jit(solution)/shard_map/ppermute | solution.py:862
  138.5 12.7 %collective-permute-start.32 = (f32[8,1280]{1,0:T(8,128)S(1)}, f32[8,1280]{1,0:T(8,128)S(1)}, u32[]{:S(2)}, u32[]{:S(2)}) collective-permute-start(f32[8,1280]{1,0:T(8,128)S(1)} %get-tuple-element.77), channel_id=1, source_target_pairs={{0,8},{4,12},{8,0},{12,4},{16,24},{20,28},{24,16},{28,20},{1,9},{5... | collective-permute-start | bytes 122888 | tf_op jit(solution)/shard_map/ppermute | solution.py:840
  138.6 27.0 %collective-permute-start.40 = (bf16[320,512]{1,0:T(8,128)(2,1)S(1)}, bf16[320,512]{1,0:T(8,128)(2,1)S(1)}, u32[]{:S(2)}, u32[]{:S(2)}) collective-permute-start(bf16[320,512]{1,0:T(8,128)(2,1)S(1)} %get-tuple-element.70), channel_id=1, source_target_pairs={{8,16},{12,20},{16,8},{20,12},{9,17},{13,21},{17,9},{21,13},{10,18... | collective-permute-start | bytes 983048 | tf_op jit(solution)/shard_map/ppermute | solution.py:862
  139.3 30.2 %collective-permute-start.41 = (bf16[320,512]{1,0:T(8,128)(2,1)S(1)}, bf16[320,512]{1,0:T(8,128)(2,1)S(1)}, u32[]{:S(2)}, u32[]{:S(2)}) collective-permute-start(bf16[320,512]{1,0:T(8,128)(2,1)S(1)} %get-tuple-element.83), channel_id=1, source_target_pairs={{0,8},{4,12},{8,0},{12,4},{16,24},{20,28},{24,16},{28,20},{1,9},{5... | collective-permute-start | bytes 983048 | tf_op jit(solution)/shard_map/ppermute | solution.py:862
  151.2 7.7 %collective-permute-start.33 = (f32[8,1280]{1,0:T(8,128)S(1)}, f32[8,1280]{1,0:T(8,128)S(1)}, u32[]{:S(2)}, u32[]{:S(2)}) collective-permute-start(f32[8,1280]{1,0:T(8,128)S(1)} %add.70), channel_id=1, source_target_pairs={{0,16},{4,20},{8,24},{12,28},{16,0},{20,4},{24,8},{28,12},{1,17},{... | collective-permute-start | bytes 122888 | tf_op jit(solution)/shard_map/ppermute | solution.py:840
  154.8 29.4 %collective-permute-start.31 = (f32[2,512,128]{2,1,0:T(8,128)}, f32[2,512,128]{2,1,0:T(8,128)}, u32[]{:S(2)}, u32[]{:S(2)}) collective-permute-start(f32[2,512,128]{2,1,0:T(8,128)} %add.68), channel_id=1, source_target_pairs={{0,2},{1,3},{2,0},{3,1},{4,6},{5,7},{6,4},{7,5},{8,10},{9,11},{10,... | collective-permute-start | bytes 1572872 | tf_op jit(solution)/shard_map/ppermute | solution.py:840
  158.9 6.1 %collective-permute-start.34 = (f32[8,1280]{1,0:T(8,128)S(1)}, f32[8,1280]{1,0:T(8,128)S(1)}, u32[]{:S(2)}, u32[]{:S(2)}) collective-permute-start(f32[8,1280]{1,0:T(8,128)S(1)} %add.71), channel_id=1, source_target_pairs={{0,4},{4,0},{8,12},{12,8},{16,20},{20,16},{24,28},{28,24},{1,5},{5... | collective-permute-start | bytes 122888 | tf_op jit(solution)/shard_map/ppermute | solution.py:840
  160.7 18.6 %collective-permute-start.42 = (bf16[320,512]{1,0:T(8,128)(2,1)S(1)}, bf16[320,512]{1,0:T(8,128)(2,1)}, u32[]{:S(2)}, u32[]{:S(2)}) collective-permute-start(bf16[320,512]{1,0:T(8,128)(2,1)S(1)} %add_convert_fusion.1.refs_8_), channel_id=1, source_target_pairs={{0,16},{4,20},{8,24},{12,28},{16,0},{20,4},{24,8},{28,12},{1,17},{... | collective-permute-start | bytes 983048 | tf_op jit(solution)/shard_map/ppermute | solution.py:862
  165.0 20.5 %collective-permute-start.36 = (bf16[320,768]{1,0:T(8,128)(2,1)}, bf16[320,768]{1,0:T(8,128)(2,1)S(1)}, u32[]{:S(2)}, u32[]{:S(2)}) collective-permute-start(bf16[320,768]{1,0:T(8,128)(2,1)} %get-tuple-element.79), channel_id=1, source_target_pairs={{8,16},{12,20},{16,8},{20,12},{9,17},{13,21},{17,9},{21,13},{10,18... | collective-permute-start | bytes 1474568 | tf_op jit(solution)/shard_map/ppermute | solution.py:862
  166.4 19.8 %collective-permute-start.37 = (bf16[320,768]{1,0:T(8,128)(2,1)S(1)}, bf16[320,768]{1,0:T(8,128)(2,1)S(1)}, u32[]{:S(2)}, u32[]{:S(2)}) collective-permute-start(bf16[320,768]{1,0:T(8,128)(2,1)S(1)} %get-tuple-element.80), channel_id=1, source_target_pairs={{0,8},{4,12},{8,0},{12,4},{16,24},{20,28},{24,16},{28,20},{1,9},{5... | collective-permute-start | bytes 1474568 | tf_op jit(solution)/shard_map/ppermute | solution.py:862
  170.2 40.0 %collective-permute-start.39 = (bf16[320,768]{1,0:T(8,128)(2,1)}, bf16[320,768]{1,0:T(8,128)(2,1)S(1)}, u32[]{:S(2)}, u32[]{:S(2)}) collective-permute-start(bf16[320,768]{1,0:T(8,128)(2,1)} %add_convert_fusion), channel_id=1, source_target_pairs={{0,16},{4,20},{8,24},{12,28},{16,0},{20,4},{24,8},{28,12},{1,17},{... | collective-permute-start | bytes 1474568 | tf_op jit(solution)/shard_map/ppermute | solution.py:862
  181.2 1.1 copy-start.15
  185.5 26.4 %copy-start.2 = (f32[512,128]{1,0:T(8,128)}, f32[512,128]{1,0:T(8,128)S(1)}, u32[]{:S(2)}) copy-start(f32[512,128]{1,0:T(8,128)S(1)} %get-tuple-element.86.rest_5_) | copy-start | bytes 786436
  185.5 26.4 %copy-start.3 = (f32[512,128]{1,0:T(8,128)}, f32[512,128]{1,0:T(8,128)S(1)}, u32[]{:S(2)}) copy-start(f32[512,128]{1,0:T(8,128)S(1)} %get-tuple-element.87.rest_4_) | copy-start | bytes 786436
  (5 other events, 4.2 us)
